TPU v7x, 32 devices: a whole 2x2x4 slice. The times are simulated.
32 devices in a mesh: dp: 8 (over z, y), tensor: 4 (over x, core).
Axes of the slice: x: 2, y: 2, z: 4, core: 2. Of those that a mesh axis runs over, the one named last changes fastest.
Arguments:
- tokens: bfloat16 [2048, 2048], P('dp'), may hold values from -6 to 6
- qkv_weight: bfloat16 [2048, 3, 2048], P('dp', None, 'tensor'), may hold values from -0.13258252 to 0.13258252
- out_weight: bfloat16 [2048, 2048], P('dp', 'tensor'), may hold values from -0.125 to 0.125
- gu_weight: bfloat16 [2048, 2, 8192], P('dp', None, 'tensor'), may hold values from -0.125 to 0.125
- down_weight: bfloat16 [2048, 8192], P('dp', 'tensor'), may hold values from -0.0625 to 0.0625
- attn_gain: bfloat16 [2048], P('dp'), may hold values from 0.25 to 1.75
- ffn_gain: bfloat16 [2048], P('dp'), may hold values from 0.25 to 1.75
- q_gain: bfloat16 [2048], P(('tensor', 'dp')), may hold values from 0.5 to 5
- k_gain: bfloat16 [2048], P(('tensor', 'dp')), may hold values from 0.5 to 5
- out_grad: float32 [2048, 2048], P('dp'), may hold values from -6 to 6
Outputs:
- block_out: float32 [2048, 2048], P('dp')
- grad_tokens: float32 [2048, 2048], P('dp')
- grad_qkv_weight: float32 [2048, 3, 2048], P('dp', None, 'tensor')
- grad_out_weight: float32 [2048, 2048], P('dp', 'tensor')
- grad_gu_weight: float32 [2048, 2, 8192], P('dp', None, 'tensor')
- grad_down_weight: float32 [2048, 8192], P('dp', 'tensor')
- grad_attn_gain: float32 [2048], P('dp')
- grad_ffn_gain: float32 [2048], P('dp')
- grad_q_gain: float32 [2048], P(('tensor', 'dp'))
- grad_k_gain: float32 [2048], P(('tensor', 'dp'))
All inputs are finite; a program needn't handle non-finite values.
Results may differ from a plain program's by a relative error of at most 0.015.
The roundings to bfloat16 on the way count: a program that leaves them out, or rounds other values in their place, can miss the bound.
Values may be sent and summed in bfloat16 or wider, within the bound.
A program may use at most 256 MiB of HBM per device.

v0:
```python
import jax
import jax.numpy as jnp
from jax import lax
from jax.sharding import PartitionSpec as P

D = 2048
HD = 128
SEQ_LEN = 256
HQ = 2048


epsilon = 1e-06
rope_base = 500000.0


def rope_tables(length, width):
    half_width = width // 2
    inv_freq = rope_base ** (-(jnp.arange(half_width, dtype=jnp.float32) * 2.0) / width)
    angles = jnp.arange(length, dtype=jnp.float32)[:, None] * inv_freq[None, :]
    cos_table = jnp.concatenate([jnp.cos(angles), jnp.cos(angles)], axis=1)
    sine_table = jnp.concatenate([jnp.sin(angles), jnp.sin(angles)], axis=1)
    return (cos_table[None, :, None, :], sine_table[None, :, None, :])


def rotate(operand):
    half_width = operand.shape[-1] // 2
    return jnp.concatenate([-operand[..., half_width:], operand[..., :half_width]], axis=-1)


def rotate_back(operand):
    half_width = operand.shape[-1] // 2
    return jnp.concatenate([operand[..., half_width:], -operand[..., :half_width]], axis=-1)


def norm_back(upstream, source, inverse, gain):
    scaled = upstream * gain
    return inverse * scaled - source * inverse**3 * jnp.mean(scaled * source, axis=1, keepdims=True)


def on_device(
    tokens,
    qkv_weight,
    out_weight,
    gu_weight,
    down_weight,
    attn_gain,
    ffn_gain,
    q_gain,
    k_gain,
    out_grad,
):
    f32 = jnp.float32
    bf16 = jnp.bfloat16
    gathered = (
        lax.all_gather(qkv_weight, "dp", axis=0, tiled=True),
        lax.all_gather(out_weight, "dp", axis=0, tiled=True),
        lax.all_gather(gu_weight, "dp", axis=0, tiled=True),
        lax.all_gather(down_weight, "dp", axis=0, tiled=True),
        lax.all_gather(attn_gain, "dp", axis=0, tiled=True),
        lax.all_gather(ffn_gain, "dp", axis=0, tiled=True),
        lax.all_gather(q_gain, "dp", axis=0, tiled=True),
        lax.all_gather(k_gain, "dp", axis=0, tiled=True),
    )
    w_qkv, w_out, w_gu, w_down, g_attn, g_ffn, g_query, g_key = gathered
    tok_rows = tokens.shape[0]
    local_q = w_out.shape[1]
    local_ff = w_down.shape[1]
    local_seqs = tok_rows // SEQ_LEN
    local_heads = local_q // HD
    head_shape = (local_seqs, SEQ_LEN, local_heads, HD)
    score_scale = HD ** (-0.5)
    gain_query = g_query.astype(f32)
    gain_key = g_key.astype(f32)
    gain_attn = g_attn.astype(f32)
    gain_ffn = g_ffn.astype(f32)
    qkv_proj = jnp.dot(tokens, w_qkv.reshape(D, 3 * local_q), preferred_element_type=f32)
    queries = qkv_proj[:, :local_q]
    key_rows = qkv_proj[:, local_q : 2 * local_q]
    value_rows = qkv_proj[:, 2 * local_q :].astype(bf16)
    squares = lax.psum(
        (jnp.sum(queries * queries, axis=1), jnp.sum(key_rows * key_rows, axis=1)), "tensor"
    )
    q_inv = lax.rsqrt(squares[0][:, None] / HQ + epsilon)
    k_inv = lax.rsqrt(squares[1][:, None] / HQ + epsilon)
    q_normed = queries * q_inv * gain_query
    k_normed = key_rows * k_inv * gain_key
    cos_table, sine_table = rope_tables(SEQ_LEN, HD)
    q_heads = q_normed.reshape(head_shape)
    k_heads = k_normed.reshape(head_shape)
    q_rot = (q_heads * cos_table + rotate(q_heads) * sine_table).astype(bf16)
    k_rot = (k_heads * cos_table + rotate(k_heads) * sine_table).astype(bf16)
    v_heads = value_rows.reshape(head_shape)
    causal = (jnp.arange(SEQ_LEN)[:, None] >= jnp.arange(SEQ_LEN)[None, :])[None, None]

    def score_of(q_side, k_side):
        raw = (
            jnp.einsum("sqhd,skhd->shqk", q_side, k_side, preferred_element_type=f32) * score_scale
        )
        return jnp.where(causal, raw, -1e30)

    scores = score_of(q_rot, k_rot)
    row_max = jnp.max(scores, axis=-1, keepdims=True)
    shifted = jnp.exp(scores - row_max)
    row_total = jnp.sum(shifted, axis=-1, keepdims=True)
    log_total = row_max + jnp.log(row_total)
    prob_rows = (shifted / row_total).astype(bf16)
    attended = (
        jnp.einsum("shqk,skhd->sqhd", prob_rows, v_heads, preferred_element_type=f32)
        .astype(bf16)
        .reshape(tok_rows, local_q)
    )
    attn_part = jnp.einsum("tf,df->td", attended, w_out, preferred_element_type=f32)
    attn_proj = lax.psum(attn_part, "tensor")
    attn_inv = lax.rsqrt(jnp.mean(attn_proj * attn_proj, axis=1, keepdims=True) + epsilon)
    residual = tokens.astype(f32) + attn_proj * attn_inv * gain_attn
    residual_rows_b = residual.astype(bf16)
    gate_up = jnp.dot(residual_rows_b, w_gu.reshape(D, 2 * local_ff), preferred_element_type=f32)
    gate_proj = gate_up[:, :local_ff]
    up_proj = gate_up[:, local_ff:]
    gate_sigmoid = jax.nn.sigmoid(gate_proj)
    active = gate_proj * gate_sigmoid
    hidden = (active * up_proj).astype(bf16)
    mlp_part = jnp.einsum("tf,df->td", hidden, w_down, preferred_element_type=f32)
    mlp_proj = lax.psum(mlp_part, "tensor")
    mlp_inv = lax.rsqrt(jnp.mean(mlp_proj * mlp_proj, axis=1, keepdims=True) + epsilon)
    block_rows = residual + mlp_proj * mlp_inv * gain_ffn
    again = (
        lax.all_gather(qkv_weight, "dp", axis=0, tiled=True),
        lax.all_gather(out_weight, "dp", axis=0, tiled=True),
        lax.all_gather(gu_weight, "dp", axis=0, tiled=True),
        lax.all_gather(down_weight, "dp", axis=0, tiled=True),
        lax.all_gather(attn_gain, "dp", axis=0, tiled=True),
        lax.all_gather(ffn_gain, "dp", axis=0, tiled=True),
        lax.all_gather(q_gain, "dp", axis=0, tiled=True),
        lax.all_gather(k_gain, "dp", axis=0, tiled=True),
    )
    back_qkv, back_out, back_gu, back_down = (again[0], again[1], again[2], again[3])
    grad_ffn_gain = jnp.sum(out_grad * mlp_proj * mlp_inv, axis=0)
    grad_mlp_rows = norm_back(out_grad, mlp_proj, mlp_inv, gain_ffn).astype(bf16)
    grad_hidden = jnp.dot(grad_mlp_rows, back_down, preferred_element_type=f32)
    grad_down = jnp.einsum("td,tf->df", grad_mlp_rows, hidden, preferred_element_type=f32)
    grad_gate = grad_hidden * up_proj * (gate_sigmoid * (1.0 + gate_proj * (1.0 - gate_sigmoid)))
    grad_up = grad_hidden * active
    grad_gu = jnp.concatenate([grad_gate, grad_up], axis=1).astype(bf16)
    grad_gu_w = jnp.einsum(
        "td,tf->df", residual_rows_b, grad_gu, preferred_element_type=f32
    ).reshape(D, 2, local_ff)
    back_part = jnp.einsum(
        "tf,df->td", grad_gu, back_gu.reshape(D, 2 * local_ff), preferred_element_type=f32
    )
    back_sum = lax.psum(back_part, "tensor")
    grad_residual = out_grad + back_sum
    grad_attn_gain = jnp.sum(grad_residual * attn_proj * attn_inv, axis=0)
    grad_proj_part = norm_back(grad_residual, attn_proj, attn_inv, gain_attn).astype(bf16)
    grad_attended = jnp.dot(grad_proj_part, back_out, preferred_element_type=f32).astype(bf16)
    grad_out_w = jnp.einsum("td,tf->df", grad_proj_part, attended, preferred_element_type=f32)
    grad_heads = grad_attended.reshape(head_shape)
    prob_again = jnp.exp(score_of(q_rot, k_rot) - log_total)
    prob_again_b = prob_again.astype(bf16)
    grad_v = jnp.einsum("shqk,sqhd->skhd", prob_again_b, grad_heads, preferred_element_type=f32)
    grad_p = jnp.einsum("sqhd,skhd->shqk", grad_heads, v_heads, preferred_element_type=f32)
    delta = jnp.sum(prob_again * grad_p, axis=-1, keepdims=True)
    grad_scores = (prob_again * (grad_p - delta) * score_scale).astype(bf16)
    grad_q_rot = jnp.einsum("shqk,skhd->sqhd", grad_scores, k_rot, preferred_element_type=f32)
    grad_k_rot = jnp.einsum("shqk,sqhd->skhd", grad_scores, q_rot, preferred_element_type=f32)
    grad_q_normed = (grad_q_rot * cos_table + rotate_back(grad_q_rot * sine_table)).reshape(
        tok_rows, local_q
    )
    grad_k_normed = (grad_k_rot * cos_table + rotate_back(grad_k_rot * sine_table)).reshape(
        tok_rows, local_q
    )
    grad_q_gain = jnp.sum(grad_q_normed * queries * q_inv, axis=0)
    grad_k_gain = jnp.sum(grad_k_normed * key_rows * k_inv, axis=0)
    scaled_q = grad_q_normed * gain_query
    scaled_k = grad_k_normed * gain_key
    inner = lax.psum(
        (jnp.sum(scaled_q * queries, axis=1), jnp.sum(scaled_k * key_rows, axis=1)), "tensor"
    )
    grad_q = q_inv * scaled_q - queries * q_inv**3 * (inner[0][:, None] / HQ)
    grad_k = k_inv * scaled_k - key_rows * k_inv**3 * (inner[1][:, None] / HQ)
    grad_qkv = jnp.concatenate([grad_q, grad_k, grad_v.reshape(tok_rows, local_q)], axis=1).astype(
        bf16
    )
    grad_qkv_w = jnp.einsum("td,tf->df", tokens, grad_qkv, preferred_element_type=f32).reshape(
        D, 3, local_q
    )
    input_part = jnp.einsum(
        "tf,df->td", grad_qkv, back_qkv.reshape(D, 3 * local_q), preferred_element_type=f32
    )
    input_sum = lax.psum(input_part, "tensor")
    grad_rows = grad_residual + input_sum
    all_sums = (
        lax.psum_scatter(grad_qkv_w, "dp", scatter_dimension=0, tiled=True),
        lax.psum_scatter(grad_out_w, "dp", scatter_dimension=0, tiled=True),
        lax.psum_scatter(grad_gu_w, "dp", scatter_dimension=0, tiled=True),
        lax.psum_scatter(grad_down, "dp", scatter_dimension=0, tiled=True),
        lax.psum_scatter(grad_attn_gain, "dp", scatter_dimension=0, tiled=True),
        lax.psum_scatter(grad_ffn_gain, "dp", scatter_dimension=0, tiled=True),
        lax.psum_scatter(grad_q_gain, "dp", scatter_dimension=0, tiled=True),
        lax.psum_scatter(grad_k_gain, "dp", scatter_dimension=0, tiled=True),
    )
    summed_qkv, summed_out, summed_gu, summed_down = (
        all_sums[0],
        all_sums[1],
        all_sums[2],
        all_sums[3],
    )
    summed_attn_gain, summed_ffn_gain = (all_sums[4], all_sums[5])
    summed_q_gain, summed_k_gain = (all_sums[6], all_sums[7])
    return (
        block_rows,
        grad_rows,
        summed_qkv,
        summed_out,
        summed_gu,
        summed_down,
        summed_attn_gain,
        summed_ffn_gain,
        summed_q_gain,
        summed_k_gain,
    )


def solution(mesh):
    return jax.shard_map(
        on_device,
        mesh=mesh,
        in_specs=(
            P("dp", None),
            P("dp", None, "tensor"),
            P("dp", "tensor"),
            P("dp", None, "tensor"),
            P("dp", "tensor"),
            P("dp"),
            P("dp"),
            P(("tensor", "dp")),
            P(("tensor", "dp")),
            P("dp", None),
        ),
        out_specs=(
            P("dp", None),
            P("dp", None),
            P("dp", None, "tensor"),
            P("dp", "tensor"),
            P("dp", None, "tensor"),
            P("dp", "tensor"),
            P("dp"),
            P("dp"),
            P(("tensor", "dp")),
            P(("tensor", "dp")),
        ),
        check_vma=False,
    )
```

profile of v0, /device:TPU:8, one launch (start us, length us, event | category | flops | bytes accessed | tf_op | source)
XLA Modules:
  0.0 2364.5 jit_solution(10394203160521481441)
XLA Ops:
  12.2 19.3 all-reduce.10
  33.2 76.6 %all-gather.7.cloned.1.call-done = bf16[2048,3,512]{0,2,1:T(8,128)(2,1)} async-done(((bf16[256,3,512]{0,2,1:T(8,128)(2,1)}), bf16[2048,3,512]{0,2,1:T(8,128)(2,1)}) %all-gather.7.cloned.1.call-update) | async-done | bytes 6291472 | tf_op jit(solution)/shard_map/all_gather | solution.py:55
  124.3 36.8 %all-gather.9.cloned.1.call-done = bf16[2048,512]{1,0:T(8,128)(2,1)} async-done(((bf16[256,512]{1,0:T(8,128)(2,1)}), bf16[2048,512]{1,0:T(8,128)(2,1)}) %all-gather.9.cloned.1.call-update) | async-done | bytes 2097168 | tf_op jit(solution)/shard_map/all_gather | solution.py:56
  166.1 15.9 all-gather
  182.0 32.9 %all-reduce.17.cloned.1.call-done = f32[256,2048]{1,0:T(8,128)} async-done(((f32[256,2048]{1,0:T(8,128)}), f32[256,2048]{1,0:T(8,128)}) %all-reduce.17.cloned.1.call-update) | async-done | bytes 2097168 | tf_op jit(solution)/shard_map/psum | solution.py:113
  220.6 221.8 %all-gather.11.cloned.1.call-done = bf16[2048,2,2048]{2,1,0:T(2,128)(2,1)} async-done(((bf16[256,2,2048]{2,1,0:T(2,128)(2,1)}), bf16[2048,2,2048]{2,1,0:T(2,128)(2,1)}) %all-gather.11.cloned.1.call-update) | async-done | bytes 16777232 | tf_op jit(solution)/shard_map/all_gather | solution.py:57
  442.4 12.6 copy.97
  464.4 102.6 %all-gather.13.cloned.1.call-done = bf16[2048,2048]{1,0:T(8,128)(2,1)} async-done(((bf16[256,2048]{1,0:T(8,128)(2,1)}), bf16[2048,2048]{1,0:T(8,128)(2,1)}) %all-gather.13.cloned.1.call-update) | async-done | bytes 8388624 | tf_op jit(solution)/shard_map/all_gather | solution.py:58
  567.0 7.4 fusion.58
  575.1 16.9 all-gather.1
  592.0 34.0 %all-reduce.19.cloned.1.call-done = f32[256,2048]{1,0:T(8,128)} async-done(((f32[256,2048]{1,0:T(8,128)}), f32[256,2048]{1,0:T(8,128)}) %all-reduce.19.cloned.1.call-update) | async-done | bytes 2097168 | tf_op jit(solution)/shard_map/psum | solution.py:124
  633.4 8.2 multiply_convert_fusion.1
  641.6 12.3 fusion.7
  655.4 50.0 %all-reduce.21.cloned.1.call-done = f32[256,2048]{1,0:T(8,128)} async-done(((f32[256,2048]{1,0:T(8,128)}), f32[256,2048]{1,0:T(8,128)}) %all-reduce.21.cloned.1.call-update) | async-done | bytes 2097168 | tf_op jit(solution)/shard_map/psum | solution.py:151
  738.6 14.9 fusion.6
  753.5 42.8 %reshape.272 = f32[2048,2,2048]{2,1,0:T(2,128)} reshape(f32[2048,4096]{1,0:T(8,128)} %fusion.6) | data formatting | bytes 67108864 | tf_op jit(solution)/shard_map/reshape | solution.py:147
  801.5 6.3 fusion.29
  807.8 12.6 copy.81
  822.0 8.2 fusion.60
  831.7 36.3 %all-reduce.7 = (f32[2048]{0:T(1024)S(1)}, f32[2048]{0:T(1024)S(1)}, f32[512]{0:T(512)S(1)}, f32[512]{0:T(512)S(1)}) all-reduce(f32[2048]{0:T(1024)S(1)} %copy-done.32, f32[2048]{0:T(1024)S(1)} %copy-done.31, f32[512]{0:T(512)S(1)} %get-tuple-element.19, f32[512]{0:T(512)S(1)} %get-tuple-element.14), channel_id=6, replica_groups=mesh['dp'=8,'tensor'=4] {'dp'}, use_global_device_ids=true, to_apply=%region_24.25.clone | all-reduce | flops 5120 | bytes 40960
  873.7 896.0 %all-reduce.25.cloned.1.call-done = f32[2048,2,2048]{2,1,0:T(2,128)} async-done(((f32[2048,2,2048]{2,1,0:T(2,128)}), f32[2048,2,2048]{2,1,0:T(2,128)}) %all-reduce.25.cloned.1.call-update) | async-done | bytes 33554448
  1775.8 87.7 %reduce-scatter.6.cloned.1.call-done = f32[256,512]{1,0:T(8,128)} async-done(((f32[2048,512]{1,0:T(8,128)}), f32[256,512]{1,0:T(8,128)}) %reduce-scatter.6.cloned.1.call-update) | async-done | bytes 524304 | tf_op jit(solution)/shard_map/reduce_scatter | solution.py:194
  1863.4 209.7 %reduce-scatter.4.cloned.1.call-done = f32[256,3,512]{2,0,1:T(8,128)} async-done(((f32[2048,3,512]{2,0,1:T(8,128)}), f32[256,3,512]{2,0,1:T(8,128)}) %reduce-scatter.4.cloned.1.call-update) | async-done | bytes 1572880 | tf_op jit(solution)/shard_map/reduce_scatter | solution.py:193
  2073.1 284.3 %reduce-scatter.8.cloned.1.call-done = f32[256,2048]{1,0:T(8,128)} async-done(((f32[2048,2048]{1,0:T(8,128)}), f32[256,2048]{1,0:T(8,128)}) %reduce-scatter.8.cloned.1.call-update) | async-done | bytes 2097168 | tf_op jit(solution)/shard_map/reduce_scatter | solution.py:196
  (202 shorter events, 101.4 us)
Async XLA Ops:
  7.2 102.6 %copy-start.9 = (bf16[256,2048]{1,0:T(8,128)(2,1)S(1)}, bf16[256,2048]{1,0:T(8,128)(2,1)}, u32[]{:S(2)}) copy-start(bf16[256,2048]{1,0:T(8,128)(2,1)} %param.10) | copy-start | bytes 3145732
  7.2 102.6 %all-gather.7.cloned.1.call-start = ((), (), s32[]{:S(2)}) async-start(), calls=%async_computation.3 | async-start | bytes 7077888 | tf_op jit(solution)/shard_map/all_gather | solution.py:55
  9.7 151.5 %all-gather.9.cloned.1.call-start = ((), (), s32[]{:S(2)}) async-start(), calls=%async_computation.4 | async-start | bytes 2359296 | tf_op jit(solution)/shard_map/all_gather | solution.py:56
  10.4 204.4 %all-reduce.17.cloned.1.call-start = ((), (), s32[]{:S(2)}) async-start(), calls=%async_computation.5 | async-start | bytes 4194304 | tf_op jit(solution)/shard_map/psum | solution.py:113
  31.6 89.4 %copy-start.33 = (f32[512]{0:T(512)}, f32[512]{0:T(512)S(1)}, u32[]{:S(2)}) copy-start(f32[512]{0:T(512)S(1)} %convert_element_type.69) | copy-start | bytes 6148
  31.6 89.4 %copy-start.35 = (f32[512]{0:T(512)}, f32[512]{0:T(512)S(1)}, u32[]{:S(2)}) copy-start(f32[512]{0:T(512)S(1)} %convert_element_type.71) | copy-start | bytes 6148
  114.4 9.3 copy-start.7
  124.3 40.5 %copy-start.25 = (bf16[4,128,256]{2,1,0:T(8,128)(2,1)}, bf16[4,128,256]{2,1,0:T(8,128)(2,1)S(1)}, u32[]{:S(2)}) copy-start(bf16[4,128,256]{2,1,0:T(8,128)(2,1)S(1)} %convolution_convert_fusion.2) | copy-start | bytes 786436
  164.8 277.5 %all-gather.11.cloned.1.call-start = ((), (), s32[]{:S(2)}) async-start(), calls=%async_computation.6 | async-start | bytes 18874368 | tf_op jit(solution)/shard_map/all_gather | solution.py:57
  165.4 401.6 %all-gather.13.cloned.1.call-start = ((), (), s32[]{:S(2)}) async-start(), calls=%async_computation.7 | async-start | bytes 9437184 | tf_op jit(solution)/shard_map/all_gather | solution.py:58
  166.0 460.0 %all-reduce.19.cloned.1.call-start = ((), (), s32[]{:S(2)}) async-start(), calls=%async_computation.8 | async-start | bytes 4194304 | tf_op jit(solution)/shard_map/psum | solution.py:124
  442.4 12.6 copy-start.14
  455.0 5.7 copy-start.6
  574.4 131.0 %all-reduce.21.cloned.1.call-start = ((), (), s32[]{:S(2)}) async-start(), calls=%async_computation.9 | async-start | bytes 4194304 | tf_op jit(solution)/shard_map/psum | solution.py:151
  633.4 8.2 copy-start.19
  653.8 216.6 %all-reduce.23.cloned.1.call-start = ((), (), s32[]{:S(2)}) async-start(), calls=%async_computation.10 | async-start | bytes 4194304 | tf_op jit(solution)/shard_map/psum | solution.py:190
  724.3 6.5 copy-start.47
  724.3 6.5 copy-start.48
  724.8 6.3 copy-start.23
  737.1 1032.5 %all-reduce.25.cloned.1.call-start = ((), (), s32[]{:S(2)}) async-start(), calls=%async_computation.14 | async-start | bytes 67108864
  796.3 1067.1 %reduce-scatter.6.cloned.1.call-start = ((), (), s32[]{:S(2)}) async-start(), calls=%async_computation.12 | async-start | bytes 4718592 | tf_op jit(solution)/shard_map/reduce_scatter | solution.py:194
  800.3 1272.8 %reduce-scatter.4.cloned.1.call-start = ((), (), s32[]{:S(2)}) async-start(), calls=%async_computation.11 | async-start | bytes 14155776 | tf_op jit(solution)/shard_map/reduce_scatter | solution.py:193
  820.5 1536.9 %reduce-scatter.8.cloned.1.call-start = ((), (), s32[]{:S(2)}) async-start(), calls=%async_computation.13 | async-start | bytes 18874368 | tf_op jit(solution)/shard_map/reduce_scatter | solution.py:196
  830.3 40.2 %copy-start.4 = (f32[256,2048]{1,0:T(8,128)S(1)}, f32[256,2048]{1,0:T(8,128)}, u32[]{:S(2)}) copy-start(f32[256,2048]{1,0:T(8,128)} %copy-done.3) | copy-start | bytes 6291460
  (42 other events, 80.6 us)
Sparse Core Ops, SparseCore 0:
  10.6 99.1 all-gather.6
  111.9 49.1 all-gather.8
  164.9 49.8 all-reduce.16
  216.8 225.5 all-gather.10
  444.3 122.6 all-gather.12
  574.6 51.4 all-reduce.18
  654.0 51.4 all-reduce.20
  737.2 52.0 all-reduce.22
  796.4 973.2 all-reduce.24
  1773.7 89.6 reduce-scatter.5
  1867.6 205.5 reduce-scatter.3
  2077.4 279.9 reduce-scatter.7
where the time goes:
time: 2370 us; the launch traced here: 2360 us
  waiting for transfers between devices  2030 us (86%)
  blocking collectives  99.9 us (4%)
  local copies, waits for them, and re-layouts  95.3 us (4%)
  matrix products  87.4 us (4%)
  other arithmetic  29.6 us (1%)
    unnamed x13, waiting for transfers between devices  898 us
    reduce_scatter x1, waiting for transfers between devices, on_device(): lax.psum_scatter(grad_down, 'dp', scatter_dimension=0, tiled=True)  284 us
    all_gather x1, waiting for transfers between devices, on_device(): lax.all_gather(gu_weight, 'dp', axis=0, tiled=True)  222 us
    reduce_scatter x1, waiting for transfers between devices, on_device(): lax.psum_scatter(grad_qkv_w, 'dp', scatter_dimension=0, tiled=True)  210 us
    all_gather x1, waiting for transfers between devices, on_device(): lax.all_gather(down_weight, 'dp', axis=0, tiled=True)  103 us
    reduce_scatter x1, waiting for transfers between devices, on_device(): lax.psum_scatter(grad_out_w, 'dp', scatter_dimension=0, tiled=True)  87.7 us
    all_gather x1, waiting for transfers between devices, on_device(): lax.all_gather(qkv_weight, 'dp', axis=0, tiled=True)  76.6 us
    unnamed x2, blocking collectives  55.6 us
  transfers between devices with their start and end apart: 12, of which 11 were waited for; matrix products, arithmetic and copies ran while one was open for 6% of the time, Pallas kernels for 0%

commit v1 on v0

v1 whole, which is shorter than its diff:
```python
import functools

import jax
import jax.numpy as jnp
from jax import lax
from jax.experimental import pallas as pl
from jax.experimental.pallas import tpu as pltpu
from jax.sharding import Mesh, PartitionSpec as P

HEADS = 16
HD = 128
SEQ_LEN = 256
HQ = 2048

epsilon = 1e-06
rope_base = 500000.0

f32 = jnp.float32
bf16 = jnp.bfloat16
MESH = pl.DeviceIdType.MESH
EXACT = lax.Precision.HIGHEST
VMEM_LIMIT = 60 * 1024 * 1024
TILE = 64


def flip(index, bit):
    return index + bit - 2 * bit * ((index // bit) % 2)


def across(index, k):
    bit = 1
    while bit <= k:
        if k & bit:
            index = flip(index, bit)
        bit *= 2
    return index


def swap(operand, axis, k=1):
    n = lax.axis_size(axis)
    return lax.ppermute(operand, axis, [(i, i ^ k) for i in range(n)])


def pick(operand, index, axis):
    return lax.dynamic_index_in_dim(operand, index, axis, keepdims=False)


def span(index, size):
    return pl.ds(pl.multiple_of(index * size, size), size)


def lead(na):
    return list(range(1, na)) + [0]


class Links:
    def __init__(self, send_sem, recv_sem):
        self.send_sem, self.recv_sem, self.count, self.copies = send_sem, recv_sem, 0, []

    def send(self, source, target, device):
        copy = pltpu.make_async_remote_copy(
            src_ref=source,
            dst_ref=target,
            send_sem=self.send_sem.at[self.count],
            recv_sem=self.recv_sem.at[self.count],
            device_id=device,
            device_id_type=MESH,
        )
        copy.start()
        self.count += 1
        self.copies.append(copy)
        return copy

    def finish(self):
        for copy in self.copies:
            copy.wait_send()


def greet(peers):
    barrier = pltpu.get_barrier_semaphore()
    for peer in peers:
        pl.semaphore_signal(barrier, inc=1, device_id=peer, device_id_type=MESH)
    pl.semaphore_wait(barrier, len(peers))


def tiles(rows, body):
    def step(i, carry):
        body(pl.ds(pl.multiple_of(i * TILE, TILE), TILE))
        return carry

    lax.fori_loop(0, rows // TILE, step, 0)


def fold(block):
    total = block[:, :128]
    for i in range(1, block.shape[1] // 128):
        total = total + block[:, i * 128 : (i + 1) * 128]
    return total


def wide(column, width):
    return jnp.concatenate([column] * (width // 128), axis=1)


def row_mask(row):
    return (lax.broadcasted_iota(jnp.int32, (8, 128), 0) == row).astype(f32)


def to_row(block, row):
    return lax.dot_general(
        row_mask(row), block, (((1,), (1,)), ((), ())), precision=EXACT, preferred_element_type=f32
    )


def to_column(stats, row):
    return lax.dot_general(
        stats, row_mask(row), (((0,), (0,)), ((), ())), precision=EXACT, preferred_element_type=f32
    )


def spread_copies(links, out, na, a, p, q, forward):
    quarter = out.shape[-1] // 4
    half = 2 * quarter
    mine = span(2 * q + p, quarter)
    pair = span(q, half)
    blocks = range(na) if forward else range(1)
    first = {
        k: links.send(out.at[0, :, mine], out.at[k, :, mine], {"a": across(a, k)}) for k in blocks if k
    }
    second, third = {}, {}
    for k in blocks:
        if k:
            first[k].wait_recv()
        second[k] = links.send(out.at[k, :, mine], out.at[k, :, mine], {"p": 1 - p})
    for k in blocks:
        second[k].wait_recv()
        third[k] = links.send(out.at[k, :, pair], out.at[k, :, pair], {"q": 1 - q})
    for k in blocks:
        third[k].wait_recv()


def reduce_kernel(na, mode, *refs):
    n_in = {"attn": 3, "mlp": 4, "back": 5, "tok": 2}[mode]
    n_out = {"attn": 4, "mlp": 3, "back": 3, "tok": 1}[mode]
    ins, outs, scratch = refs[:n_in], refs[n_in : n_in + n_out], refs[n_in + n_out :]
    from_q, half_sum, from_p, to_a, from_a, total, parts, cols, stat, send_sem, recv_sem = scratch
    part_ref, out = ins[0], outs[0]
    a, p, q = lax.axis_index("a"), lax.axis_index("p"), lax.axis_index("q")
    rows, width = part_ref.shape[1], part_ref.shape[2]
    quarter, half = width // 4, width // 2
    greet([{"q": 1 - q}, {"p": 1 - p}] + [{"a": across(a, k)} for k in range(1, na)])
    links = Links(send_sem, recv_sem)

    give, keep = span(1 - q, half), span(q, half)
    step_q = {
        k: links.send(part_ref.at[k, :, give], from_q.at[k], {"q": 1 - q}) for k in lead(na)
    }
    step_p, step_a = {}, {}
    for k in lead(na):
        step_q[k].wait_recv()

        def add_half(at, k=k):
            own = part_ref[k, at, keep].astype(f32)
            half_sum[k, at] = (own + from_q[k, at].astype(f32)).astype(bf16)

        tiles(rows, add_half)
        step_p[k] = links.send(half_sum.at[k, :, span(1 - p, quarter)], from_p.at[k], {"p": 1 - p})
    for k in lead(na):
        step_p[k].wait_recv()
        if k:

            def add_quarter(at, k=k):
                own = half_sum[k, at, span(p, quarter)].astype(f32)
                to_a[k - 1, at] = (own + from_p[k, at].astype(f32)).astype(bf16)

            tiles(rows, add_quarter)
            step_a[k] = links.send(to_a.at[k - 1], from_a.at[k - 1], {"a": across(a, k)})
    for k in range(1, na):
        step_a[k].wait_recv()

    def add_all(at):
        own = half_sum[0, at, span(p, quarter)].astype(f32) + from_p[0, at].astype(f32)
        for k in range(1, na):
            own = own + from_a[k - 1, at].astype(f32)
        return own

    mine = span(2 * q + p, quarter)

    def exchange(count):
        stats = to_row(parts[0], 0)
        if count == 2:
            stats = stats + to_row(parts[1], 1)
        stat[0] = stats
        links.send(stat.at[0], stat.at[1], {"p": 1 - p}).wait_recv()
        stat[2] = stat[0] + stat[1]
        links.send(stat.at[2], stat.at[3], {"q": 1 - q}).wait_recv()
        stats = (stat[2] + stat[3]) / width
        for i in range(count):
            cols[i] = to_column(stats, i)

    if mode == "attn":
        _, tok_ref, gain_ref = ins
        _, proj_ref, inv_ref, res_ref = outs

        def first(at):
            own = add_all(at)
            proj_ref[at] = own
            parts[0, at] = fold(own * own)

        tiles(rows, first)
        exchange(1)

        def second(at):
            own = proj_ref[at]
            inv = lax.rsqrt(cols[0, at] + epsilon)
            inv_ref[at] = inv
            residual = tok_ref[at].astype(f32) + own * wide(inv, quarter) * gain_ref[0:1]
            res_ref[at] = residual
            out[0, at, mine] = residual.astype(bf16)

        tiles(rows, second)
    elif mode == "mlp":
        _, res_ref, grad_ref, gain_ref = ins
        _, block_ref, sum_ref = outs

        def first(at):
            own = add_all(at)
            total[at] = own
            parts[0, at] = fold(own * own)
            parts[1, at] = fold(grad_ref[at] * gain_ref[0:1] * own)

        tiles(rows, first)
        exchange(2)
        sum_ref[...] = jnp.zeros_like(sum_ref)

        def second(at):
            own = total[at]
            inv = wide(lax.rsqrt(cols[0, at] + epsilon), quarter)
            upstream = grad_ref[at]
            scaled = upstream * gain_ref[0:1]
            normed = own * inv
            block_ref[0, at, mine] = (res_ref[at] + normed * gain_ref[0:1]).astype(bf16)
            gains = upstream * normed
            sum_ref[...] += jnp.sum(gains.reshape(TILE // 8, 8, quarter), axis=0)
            grad = inv * scaled - own * inv * inv * inv * wide(cols[1, at], quarter)
            out[0, at, mine] = grad.astype(bf16)

        tiles(rows, second)
    elif mode == "back":
        _, grad_ref, proj_ref, inv_ref, gain_ref = ins
        _, res_ref, sum_ref = outs

        def first(at):
            grad = grad_ref[at] + add_all(at)
            res_ref[at] = grad
            parts[0, at] = fold(grad * gain_ref[0:1] * proj_ref[at])

        tiles(rows, first)
        exchange(1)
        sum_ref[...] = jnp.zeros_like(sum_ref)

        def second(at):
            own = proj_ref[at]
            inv = wide(inv_ref[at], quarter)
            upstream = res_ref[at]
            gains = upstream * own * inv
            sum_ref[...] += jnp.sum(gains.reshape(TILE // 8, 8, quarter), axis=0)
            grad = inv * (upstream * gain_ref[0:1])
            grad = grad - own * inv * inv * inv * wide(cols[0, at], quarter)
            out[0, at, mine] = grad.astype(bf16)

        tiles(rows, second)
    else:
        _, grad_ref = ins

        def first(at):
            out[0, at, mine] = (grad_ref[at] + add_all(at)).astype(bf16)

        tiles(rows, first)

    if mode == "mlp":
        spread_copies(links, out, na, a, p, q, True)
        spread_copies(links, block_ref, na, a, p, q, False)
    else:
        spread_copies(links, out, na, a, p, q, mode != "tok")
    links.finish()


def reduce_call(mode, part, *operands):
    na, rows, width = part.shape
    quarter = width // 4
    shape = jax.ShapeDtypeStruct
    full = shape((na, rows, width), bf16)
    one = shape((1, rows, width), bf16)
    share = shape((rows, quarter), f32)
    sums = shape((8, quarter), f32)
    outs = {
        "attn": (full, share, shape((rows, 128), f32), share),
        "mlp": (full, one, sums),
        "back": (full, share, sums),
        "tok": (one,),
    }[mode]
    copies = 3 * na + 1 + {"attn": 3 * na + 1, "mlp": 3 * na + 3, "back": 3 * na + 1, "tok": 2}[mode]
    return pl.pallas_call(
        functools.partial(reduce_kernel, na, mode),
        out_shape=outs,
        in_specs=[pl.BlockSpec(memory_space=pltpu.VMEM)] * (1 + len(operands)),
        out_specs=tuple([pl.BlockSpec(memory_space=pltpu.VMEM)] * len(outs)),
        scratch_shapes=[
            pltpu.VMEM((na, rows, width // 2), bf16),
            pltpu.VMEM((na, rows, width // 2), bf16),
            pltpu.VMEM((na, rows, quarter), bf16),
            pltpu.VMEM((na - 1, rows, quarter), bf16),
            pltpu.VMEM((na - 1, rows, quarter), bf16),
            pltpu.VMEM((rows, quarter), f32),
            pltpu.VMEM((2, rows, 128), f32),
            pltpu.VMEM((2, rows, 128), f32),
            pltpu.VMEM((4, 8, rows), f32),
            pltpu.SemaphoreType.DMA((copies,)),
            pltpu.SemaphoreType.DMA((copies,)),
        ],
        compiler_params=pltpu.CompilerParams(
            collective_id={"attn": 1, "mlp": 2, "back": 3, "tok": 4}[mode],
            has_side_effects=True,
            vmem_limit_bytes=VMEM_LIMIT,
        ),
        cost_estimate=pl.CostEstimate(flops=10**8, bytes_accessed=10**8, transcendentals=0),
        name="reduce_" + mode,
    )(part, *operands)


def start_kernel(na, nb, tok_ref, qkv_ref, wout_ref, x_ref, w_ref, local_sem, send_sem, recv_sem):
    a, b, p, q = (lax.axis_index(axis) for axis in ("a", "b", "p", "q"))
    rows = wout_ref.shape[0]
    quarter = tok_ref.shape[1]
    greet(
        [{"q": 1 - q}, {"p": 1 - p}]
        + [{"a": across(a, k)} for k in range(1, na)]
        + [{"b": across(b, j)} for j in range(1, nb)]
    )
    links = Links(send_sem, recv_sem)
    mine = span(2 * q + p, quarter)
    pair = span(q, 2 * quarter)
    place = span(a * nb + b, rows)
    locals_ = [pltpu.make_async_copy(tok_ref, x_ref.at[0, :, mine], local_sem.at[0])]
    arrive = {}
    for k in range(na):
        block = span(across(a, k), HD)
        sources = [qkv_ref.at[c, :, block] for c in range(3)] + [wout_ref.at[:, block]]
        for c, source in enumerate(sources):
            target = w_ref.at[place, c * HD : (c + 1) * HD]
            if k:
                arrive[k, c] = links.send(source, target, {"a": across(a, k)})
            else:
                locals_.append(pltpu.make_async_copy(source, target, local_sem.at[1 + c]))
    first = {
        k: links.send(tok_ref, x_ref.at[k, :, mine], {"a": across(a, k)}) for k in range(1, na)
    }
    for copy in locals_:
        copy.start()
    for copy in locals_:
        copy.wait()
    ends, second, third = [], {}, {}
    for k in range(na):
        if k:
            for c in range(4):
                arrive[k, c].wait_recv()
        at = w_ref.at[span(across(a, k) * nb + b, rows), :]
        for j in range(1, nb):
            ends.append(links.send(at, at, {"b": across(b, j)}))
        if k:
            first[k].wait_recv()
        second[k] = links.send(x_ref.at[k, :, mine], x_ref.at[k, :, mine], {"p": 1 - p})
    for k in range(na):
        second[k].wait_recv()
        third[k] = links.send(x_ref.at[k, :, pair], x_ref.at[k, :, pair], {"q": 1 - q})
    for copy in list(third.values()) + ends:
        copy.wait_recv()
    links.finish()


def start_call(na, nb, tok_mine, qkv, w_out):
    rows, quarter = tok_mine.shape
    width = 4 * quarter
    copies = (na - 1) * 5 + na * (nb - 1) + 2 * na
    return pl.pallas_call(
        functools.partial(start_kernel, na, nb),
        out_shape=(
            jax.ShapeDtypeStruct((na, rows, width), bf16),
            jax.ShapeDtypeStruct((width, 4 * HD), bf16),
        ),
        in_specs=[pl.BlockSpec(memory_space=pltpu.VMEM)] * 3,
        out_specs=(pl.BlockSpec(memory_space=pltpu.VMEM), pl.BlockSpec(memory_space=pltpu.VMEM)),
        scratch_shapes=[
            pltpu.SemaphoreType.DMA((5,)),
            pltpu.SemaphoreType.DMA((copies,)),
            pltpu.SemaphoreType.DMA((copies,)),
        ],
        compiler_params=pltpu.CompilerParams(
            collective_id=5, has_side_effects=True, vmem_limit_bytes=VMEM_LIMIT
        ),
        name="start",
    )(tok_mine, qkv, w_out)


def stats_kernel(na, stats_ref, out_ref, held, from_a, send_sem, recv_sem):
    a, p, q = lax.axis_index("a"), lax.axis_index("p"), lax.axis_index("q")
    greet([{"q": 1 - q}, {"p": 1 - p}] + [{"a": across(a, k)} for k in range(1, na)])
    links = Links(send_sem, recv_sem)
    links.send(stats_ref, held.at[0], {"p": 1 - p}).wait_recv()
    held[1] = stats_ref[...] + held[0]
    links.send(held.at[1], held.at[2], {"q": 1 - q}).wait_recv()
    held[3] = held[1] + held[2]
    copies = [links.send(held.at[3], from_a.at[k - 1], {"a": across(a, k)}) for k in range(1, na)]
    for copy in copies:
        copy.wait_recv()
    for k in range(na):
        for i in range(2):
            at = 2 * k + i
            total = held[3, at : at + 1]
            for j in range(1, na):
                other = 2 * (k ^ j) + i
                total = total + from_a[j - 1, other : other + 1]
            out_ref[at : at + 1] = total
    links.finish()


def stats_call(na, stats, ident):
    return pl.pallas_call(
        functools.partial(stats_kernel, na),
        out_shape=jax.ShapeDtypeStruct(stats.shape, f32),
        in_specs=[pl.BlockSpec(memory_space=pltpu.VMEM)],
        out_specs=pl.BlockSpec(memory_space=pltpu.VMEM),
        scratch_shapes=[
            pltpu.VMEM((4,) + stats.shape, f32),
            pltpu.VMEM((na - 1,) + stats.shape, f32),
            pltpu.SemaphoreType.DMA((na + 1,)),
            pltpu.SemaphoreType.DMA((na + 1,)),
        ],
        compiler_params=pltpu.CompilerParams(collective_id=ident, has_side_effects=True),
        name="stats" + str(ident),
    )(stats)


def local_call(kernel, name, na, operands, outs, scratch=(), flops=10**9):
    def spec(shape, kind):
        if kind == "row":
            return pl.BlockSpec((1,) + tuple(shape[1:]), lambda k: (k,) + (0,) * (len(shape) - 1))
        if kind == "all":
            return pl.BlockSpec(tuple(shape), lambda k: (0,) * len(shape))
        return pl.BlockSpec(memory_space=pl.ANY)

    return pl.pallas_call(
        kernel,
        grid=(na,),
        out_shape=tuple(jax.ShapeDtypeStruct(shape, dtype) for shape, dtype, _ in outs),
        in_specs=[spec(array.shape, kind) for array, kind in operands],
        out_specs=tuple(spec(shape, kind) for shape, _, kind in outs),
        scratch_shapes=list(scratch),
        compiler_params=pltpu.CompilerParams(
            dimension_semantics=("arbitrary",), vmem_limit_bytes=VMEM_LIMIT
        ),
        cost_estimate=pl.CostEstimate(flops=flops, bytes_accessed=2 * 10**7, transcendentals=0),
        name=name,
    )(*[array for array, _ in operands])


def dot(left, right):
    return jnp.dot(left, right, preferred_element_type=f32)


def dot_t(left, right):
    return lax.dot_general(left, right, (((1,), (1,)), ((), ())), preferred_element_type=f32)


def t_dot(left, right):
    return lax.dot_general(left, right, (((0,), (0,)), ((), ())), preferred_element_type=f32)


def add_stats(stats_ref, first, second):
    k = pl.program_id(0)

    @pl.when(k == 0)
    def _():
        stats_ref[...] = jnp.zeros_like(stats_ref)

    stats_ref[...] += to_row(first, 2 * k) + to_row(second, 2 * k + 1)


def qkv_kernel(x_ref, w_ref, qkv_ref, stats_ref):
    out = dot(x_ref[0], w_ref[:, : 3 * HD])
    qkv_ref[0] = out
    queries, key_rows = out[:, :HD], out[:, HD : 2 * HD]
    add_stats(stats_ref, queries * queries, key_rows * key_rows)


def rotate(operand):
    half = HD // 2
    return jnp.concatenate([-operand[:, half:], operand[:, :half]], axis=1)


def rotate_back(operand):
    half = HD // 2
    return jnp.concatenate([operand[:, half:], -operand[:, :half]], axis=1)


def attention(qkv_ref, stats_ref, gain_ref, cos_ref, sin_ref):
    k = pl.program_id(0)
    stats = stats_ref[...] / HQ
    q_inv = lax.rsqrt(to_column(stats, 2 * k) + epsilon)
    k_inv = lax.rsqrt(to_column(stats, 2 * k + 1) + epsilon)
    queries, key_rows = qkv_ref[0, :, :HD], qkv_ref[0, :, HD : 2 * HD]
    values = qkv_ref[0, :, 2 * HD :].astype(bf16)
    cos_table, sine_table = cos_ref[...], sin_ref[...]
    q_normed = queries * q_inv * gain_ref[0:1]
    k_normed = key_rows * k_inv * gain_ref[1:2]
    q_rot = (q_normed * cos_table + rotate(q_normed) * sine_table).astype(bf16)
    k_rot = (k_normed * cos_table + rotate(k_normed) * sine_table).astype(bf16)
    scores = dot_t(q_rot, k_rot) * HD ** (-0.5)
    ahead = lax.broadcasted_iota(jnp.int32, scores.shape, 1) > lax.broadcasted_iota(
        jnp.int32, scores.shape, 0
    )
    scores = jnp.where(ahead, -1e30, scores)
    shifted = jnp.exp(scores - jnp.max(scores, axis=1, keepdims=True))
    probs = shifted / jnp.sum(shifted, axis=1, keepdims=True)
    return queries, key_rows, values, q_inv, k_inv, q_rot, k_rot, probs


def attend_kernel(qkv_ref, stats_ref, gain_ref, cos_ref, sin_ref, w_ref, att_ref, part_ref):
    values, probs = (attention(qkv_ref, stats_ref, gain_ref, cos_ref, sin_ref)[i] for i in (2, 7))
    attended = dot(probs.astype(bf16), values).astype(bf16)
    att_ref[0] = attended
    part_ref[0] = dot_t(attended, w_ref[:, 3 * HD :]).astype(bf16)


def attend_back_kernel(
    proj_ref, qkv_ref, stats_ref, gain_ref, cos_ref, sin_ref, w_ref, grad_ref, inner_ref, sums_ref
):
    k = pl.program_id(0)
    queries, key_rows, values, q_inv, k_inv, q_rot, k_rot, probs = attention(
        qkv_ref, stats_ref, gain_ref, cos_ref, sin_ref
    )
    cos_table, sine_table = cos_ref[...], sin_ref[...]
    grad_att = dot(proj_ref[0], w_ref[:, 3 * HD :]).astype(bf16)
    grad_v = t_dot(probs.astype(bf16), grad_att)
    grad_p = dot_t(grad_att, values)
    delta = jnp.sum(probs * grad_p, axis=1, keepdims=True)
    grad_scores = (probs * (grad_p - delta) * HD ** (-0.5)).astype(bf16)
    grad_q = dot(grad_scores, k_rot)
    grad_k = t_dot(grad_scores, q_rot)
    grad_q = grad_q * cos_table + rotate_back(grad_q * sine_table)
    grad_k = grad_k * cos_table + rotate_back(grad_k * sine_table)

    @pl.when(k == 0)
    def _():
        sums_ref[...] = jnp.zeros_like(sums_ref)

    sums_ref[0:1] += jnp.sum(grad_q * queries * q_inv, axis=0, keepdims=True)
    sums_ref[1:2] += jnp.sum(grad_k * key_rows * k_inv, axis=0, keepdims=True)
    scaled_q = grad_q * gain_ref[0:1]
    scaled_k = grad_k * gain_ref[1:2]
    grad_ref[0, :, :HD] = scaled_q
    grad_ref[0, :, HD : 2 * HD] = scaled_k
    grad_ref[0, :, 2 * HD :] = grad_v
    add_stats(inner_ref, scaled_q * queries, scaled_k * key_rows)


def qkv_back_kernel(scaled_ref, qkv_ref, stats_ref, inner_ref, w_ref, grad_ref, part_ref):
    k = pl.program_id(0)
    for i in range(2):
        at = slice(i * HD, (i + 1) * HD)
        inv = lax.rsqrt(to_column(stats_ref[...] / HQ, 2 * k + i) + epsilon)
        mean = to_column(inner_ref[...] / HQ, 2 * k + i)
        grad = inv * scaled_ref[0, :, at] - qkv_ref[0, :, at] * inv * inv * inv * mean
        grad_ref[0, :, at] = grad.astype(bf16)
    grad_ref[0, :, 2 * HD :] = scaled_ref[0, :, 2 * HD :].astype(bf16)
    part_ref[0] = dot_t(grad_ref[0], w_ref[:, : 3 * HD]).astype(bf16)


def load_weights(na, nb, pieces, w_ref, sem):
    a, b = lax.axis_index("a"), lax.axis_index("b")

    @pl.when(pl.program_id(0) == 0)
    def _():
        rows, units = pieces[0].shape[1:]
        copies = []
        for k in range(na):
            for j in range(nb):
                place = span(across(a, k) * nb + across(b, j), rows)
                for c in range(3):
                    copies.append(
                        pltpu.make_async_copy(
                            pieces[k * nb + j].at[c],
                            w_ref.at[place, c * units : (c + 1) * units],
                            sem.at[len(copies)],
                        )
                    )
        for copy in copies:
            copy.start()
        for copy in copies:
            copy.wait()


def mlp_kernel(na, nb, *refs):
    pieces, (x_ref, gu_ref, hidden_ref, part_ref, w_ref, sem) = refs[: na * nb], refs[na * nb :]
    load_weights(na, nb, pieces, w_ref, sem)
    units = hidden_ref.shape[2]
    gate_up = dot(x_ref[0], w_ref[:, : 2 * units])
    gu_ref[0] = gate_up
    gate, up = gate_up[:, :units], gate_up[:, units:]
    hidden = (gate * jax.nn.sigmoid(gate) * up).astype(bf16)
    hidden_ref[0] = hidden
    part_ref[0] = dot_t(hidden, w_ref[:, 2 * units :]).astype(bf16)


def mlp_back_kernel(na, nb, *refs):
    pieces, (grad_ref, gu_ref, out_ref, part_ref, w_ref, sem) = refs[: na * nb], refs[na * nb :]
    load_weights(na, nb, pieces, w_ref, sem)
    units = gu_ref.shape[2] // 2
    grad_hidden = dot(grad_ref[0], w_ref[:, 2 * units :])
    gate, up = gu_ref[0, :, :units], gu_ref[0, :, units:]
    sigmoid = jax.nn.sigmoid(gate)
    active = gate * sigmoid
    out_ref[0, :, :units] = (
        grad_hidden * up * (sigmoid * (1.0 + gate * (1.0 - sigmoid)))
    ).astype(bf16)
    out_ref[0, :, units:] = (grad_hidden * active).astype(bf16)
    part_ref[0] = dot_t(out_ref[0], w_ref[:, : 2 * units]).astype(bf16)


def widen_kernel(na, count, *refs):
    pieces, out = refs[:na], refs[na]
    a = lax.axis_index("a")
    columns = out.shape[2] // na
    for k in range(na):
        for c in range(count):
            out[c, :, span(across(a, k), columns)] = pieces[k][
                :, c * columns : (c + 1) * columns
            ].astype(f32)


def widen(pieces, count, name):
    na = len(pieces)
    rows, width = pieces[0].shape
    return pl.pallas_call(
        functools.partial(widen_kernel, na, count),
        out_shape=jax.ShapeDtypeStruct((count, rows, na * width // count), f32),
        in_specs=[pl.BlockSpec(memory_space=pltpu.VMEM)] * na,
        out_specs=pl.BlockSpec(memory_space=pltpu.VMEM),
        compiler_params=pltpu.CompilerParams(vmem_limit_bytes=VMEM_LIMIT),
        name=name,
    )(*pieces)


def rope_tables(length, width):
    half_width = width // 2
    inv_freq = rope_base ** (-(jnp.arange(half_width, dtype=f32) * 2.0) / width)
    angles = jnp.arange(length, dtype=f32)[:, None] * inv_freq[None, :]
    cos_table = jnp.concatenate([jnp.cos(angles), jnp.cos(angles)], axis=1)
    sine_table = jnp.concatenate([jnp.sin(angles), jnp.sin(angles)], axis=1)
    return cos_table, sine_table


def on_device(
    tokens,
    qkv_weight,
    out_weight,
    gu_weight,
    down_weight,
    attn_gain,
    ffn_gain,
    q_gain,
    k_gain,
    out_grad,
):
    na, nb = lax.axis_size("a"), lax.axis_size("b")
    a, b = lax.axis_index("a"), lax.axis_index("b")
    share = lax.axis_index("q") * 2 + lax.axis_index("p")
    rows, width = tokens.shape
    quarter = width // 4
    w_rows = out_weight.shape[0]
    units = down_weight.shape[1] // na

    def quarter_of(operand):
        return lax.dynamic_slice_in_dim(operand, share * quarter, quarter, 1)

    def whole_gain(gain):
        own = jnp.zeros((HQ,), f32)
        return lax.dynamic_update_slice_in_dim(own, gain.astype(f32), (a * nb + b) * gain.shape[0], 0)

    tok_mine, grad_mine = quarter_of(tokens), quarter_of(out_grad)
    x_all, w_attn = start_call(
        na, nb, tok_mine, qkv_weight.transpose(1, 0, 2), out_weight
    )

    shards = jnp.concatenate([gu_weight.transpose(1, 0, 2), down_weight[None]], axis=0)
    shards = shards.reshape(3, w_rows, na, units)
    pieces = []
    for k in range(na):
        piece = pick(shards, a ^ k, 2)
        if k:
            piece = swap(piece, "a", k)
        pieces += [piece] + [swap(piece, "b", j) for j in range(1, nb)]

    gains = lax.psum(jnp.stack([whole_gain(attn_gain), whole_gain(ffn_gain)]), ("a", "b"))
    gains = lax.dynamic_slice_in_dim(gains, share * quarter, quarter, 1)
    gain_attn = jnp.broadcast_to(gains[0:1], (8, quarter))
    gain_ffn = jnp.broadcast_to(gains[1:2], (8, quarter))
    n_h = q_gain.shape[0]
    head_gain = jnp.zeros((nb, 2, n_h), f32)
    own = jnp.stack([q_gain, k_gain]).astype(f32)
    head_gain = lax.psum(lax.dynamic_update_index_in_dim(head_gain, own, b, 0), "b")
    head_gain = head_gain.transpose(1, 0, 2).reshape(2, HD)
    head_gain = jnp.concatenate([head_gain, jnp.zeros((6, HD), f32)])
    cos_table, sine_table = rope_tables(SEQ_LEN, HD)

    qkv, stats = local_call(
        qkv_kernel,
        "qkv",
        na,
        [(x_all, "row"), (w_attn, "all")],
        [((na, rows, 3 * HD), f32, "row"), ((8, rows), f32, "all")],
    )
    stats = stats_call(na, stats, 6)
    tables = [(stats, "all"), (head_gain, "all"), (cos_table, "all"), (sine_table, "all")]
    full = (na, rows, width)
    attended, part = local_call(
        attend_kernel,
        "attend",
        na,
        [(qkv, "row")] + tables + [(w_attn, "all")],
        [((na, rows, HD), bf16, "row"), (full, bf16, "row")],
    )
    res_all, proj_mine, inv_mine, res_mine = reduce_call("attn", part, tok_mine, gain_attn)

    mlp_scratch = [
        pltpu.VMEM((width, 3 * units), bf16),
        pltpu.SemaphoreType.DMA((3 * na * nb,)),
    ]
    far = [(piece, "far") for piece in pieces]
    gate_up, hidden, part = local_call(
        functools.partial(mlp_kernel, na, nb),
        "mlp",
        na,
        far + [(res_all, "row")],
        [((na, rows, 2 * units), f32, "row"), ((na, rows, units), bf16, "row"), (full, bf16, "row")],
        mlp_scratch,
    )
    grad_mlp, block_rows, ffn_sums = reduce_call("mlp", part, res_mine, grad_mine, gain_ffn)
    grad_gu, part = local_call(
        functools.partial(mlp_back_kernel, na, nb),
        "mlp_back",
        na,
        far + [(grad_mlp, "row"), (gate_up, "row")],
        [((na, rows, 2 * units), bf16, "row"), (full, bf16, "row")],
        mlp_scratch,
    )

    def weight_grad(left, right):
        out = jnp.einsum("krd,kru->du", left, right, preferred_element_type=f32)
        return out.astype(bf16).reshape(na, nb, w_rows, right.shape[2])

    def reduce_b(grad):
        total = pick(grad, b, 1).astype(f32)
        for j in range(1, nb):
            total = total + swap(pick(grad, b ^ j, 1), "b", j).astype(f32)
        return total.astype(bf16)

    def to_owner(grad):
        return [pick(grad, a, 0)] + [swap(pick(grad, a ^ k, 0), "a", k) for k in range(1, na)]

    down_sum = to_owner(reduce_b(weight_grad(grad_mlp, hidden)))
    gu_sum = to_owner(reduce_b(weight_grad(res_all, grad_gu)))
    grad_proj, grad_res, attn_sums = reduce_call(
        "back", part, grad_mine, proj_mine, inv_mine, gain_attn
    )
    scaled, inner, head_sums = local_call(
        attend_back_kernel,
        "attend_back",
        na,
        [(grad_proj, "row"), (qkv, "row")] + tables + [(w_attn, "all")],
        [((na, rows, 3 * HD), f32, "row"), ((8, rows), f32, "all"), ((8, HD), f32, "all")],
    )
    out_sum = to_owner(reduce_b(weight_grad(grad_proj, attended)))
    inner = stats_call(na, inner, 7)
    grad_qkv, part = local_call(
        qkv_back_kernel,
        "qkv_back",
        na,
        [(scaled, "row"), (qkv, "row"), (stats, "all"), (inner, "all"), (w_attn, "all")],
        [((na, rows, 3 * HD), bf16, "row"), (full, bf16, "row")],
    )
    qkv_sum = to_owner(reduce_b(weight_grad(x_all, grad_qkv)))
    (grad_rows,) = reduce_call("tok", part, grad_res)

    sums = jnp.stack([jnp.sum(attn_sums, axis=0), jnp.sum(ffn_sums, axis=0)])
    place = jnp.zeros((2, width), f32)
    width_sums = lax.dynamic_update_slice_in_dim(place, sums, share * quarter, 1)
    width_sums = lax.psum(width_sums, ("a", "b", "p", "q"))
    n_d = attn_gain.shape[0]
    width_sums = lax.dynamic_slice_in_dim(width_sums, (a * nb + b) * n_d, n_d, 1)
    head_sums = lax.psum(head_sums[:2], "b")
    head_sums = lax.dynamic_slice_in_dim(head_sums, b * n_h, n_h, 1)
    return (
        block_rows[0].astype(f32),
        grad_rows[0].astype(f32),
        widen(qkv_sum, 3, "widen_qkv").transpose(1, 0, 2),
        widen(out_sum, 1, "widen_out")[0],
        widen(gu_sum, 2, "widen_gu").transpose(1, 0, 2),
        widen(down_sum, 1, "widen_down")[0],
        width_sums[0],
        width_sums[1],
        head_sums[0],
        head_sums[1],
    )


def solution(mesh):
    dp, tp = mesh.shape["dp"], mesh.shape["tensor"]
    na = HEADS // tp
    fine = Mesh(mesh.devices.reshape(na, dp // na, tp // 2, 2), ("a", "b", "p", "q"))
    dp_axes, tp_axes = ("a", "b"), ("p", "q")
    both = tp_axes + dp_axes
    return jax.shard_map(
        on_device,
        mesh=fine,
        in_specs=(
            P(dp_axes, None),
            P(dp_axes, None, tp_axes),
            P(dp_axes, tp_axes),
            P(dp_axes, None, tp_axes),
            P(dp_axes, tp_axes),
            P(dp_axes),
            P(dp_axes),
            P(both),
            P(both),
            P(dp_axes, None),
        ),
        out_specs=(
            P(dp_axes, None),
            P(dp_axes, None),
            P(dp_axes, None, tp_axes),
            P(dp_axes, tp_axes),
            P(dp_axes, None, tp_axes),
            P(dp_axes, tp_axes),
            P(dp_axes),
            P(dp_axes),
            P(both),
            P(both),
        ),
        check_vma=False,
    )
```

time: 2370 us -> 765 us (0.32)
  waiting for transfers between devices: 2030 us -> 17.7 us
  Pallas kernels: 0 us -> 532 us
  matrix products: 87.4 us -> 20.3 us
  local copies, waits for them, and re-layouts: 95.3 us -> 38.3 us
  starting transfers between devices: 0.95 us -> 29.4 us
    unnamed x13 -> x0, waiting for transfers between devices: 898 us -> none
    reduce_scatter x3 -> x0, waiting for transfers between devices: 582 us -> none  [the longest x1 284 us: on_device(): lax.psum_scatter(grad_down, 'dp', scatter_dimension=0, tiled=True)]
    pallas_call x0 -> x17, Pallas kernels: none -> 532 us  [the longest x4 317 us: reduce_call(): pl.pallas_call(functools.partial(reduce_kernel, na, mode), out_shape=outs...]
    all_gather x4 -> x0, waiting for transfers between devices: 438 us -> none  [the longest x1 222 us: on_device(): lax.all_gather(gu_weight, 'dp', axis=0, tiled=True)]
    psum x4 -> x0, waiting for transfers between devices: 117 us -> none  [the longest x1 50 us: on_device(): back_sum = lax.psum(back_part, 'tensor')]
    psum x2 -> x4, blocking collectives: 11.5 us -> 111 us  [the longest x1 66.7 us: on_device(): width_sums = lax.psum(width_sums, ('a', 'b', 'p', 'q'))]
    dot_general x18 -> x4, matrix products: 87.4 us -> 20.3 us  [weight_grad(): out = jnp.einsum('krd,kru->du', left, right, preferred_element_type=f32)]
    reshape x7 -> x1, local copies, waits for them, and re-layouts: 57 us -> 0.08 us  [on_device(): head_gain = head_gain.transpose(1, 0, 2).reshape(2, HD)]
  transfers between devices with their start and end apart: 12 -> 23, of which waited for: 11 -> 3; matrix products, arithmetic and copies ran while one was open for 6% -> 5% of each run, Pallas kernels for 0% -> 55%
where the time goes in v1:
time: 765 us; the launch traced here: 762 us
  Pallas kernels  532 us (70%)
  blocking collectives  111 us (15%)
  local copies, waits for them, and re-layouts  38.3 us (5%)
  starting transfers between devices  29.4 us (4%)
  matrix products  20.3 us (3%)
  waiting for transfers between devices  17.7 us (2%)
  other arithmetic  12.5 us (2%)
    pallas_call x4, Pallas kernels, reduce_call(): pl.pallas_call(functools.partial(reduce_kernel, na, mode), out_shape=outs...  317 us
    pallas_call x1, Pallas kernels, start_call(): pl.pallas_call(functools.partial(start_kernel, na, nb), out_shape=(jax.Sh...  121 us
    psum x1, blocking collectives, on_device(): width_sums = lax.psum(width_sums, ('a', 'b', 'p', 'q'))  66.7 us
    pallas_call x6, Pallas kernels, local_call(): pl.pallas_call(kernel, grid=(na,), out_shape=tuple((jax.ShapeDtypeStruct(...  63.9 us
    psum x1, blocking collectives, on_device(): lax.psum(jnp.stack([whole_gain(attn_gain), whole_gain(ffn_gain)]), ('a',...  34.6 us
    ppermute x23, starting transfers between devices, swap(): return lax.ppermute(operand, axis, [(i, i ^ k) for i in range(n)])  29.4 us
    dot_general x4, matrix products, weight_grad(): out = jnp.einsum('krd,kru->du', left, right, preferred_element_type=f32)  20.3 us
    pallas_call x2, Pallas kernels, stats_call(): pl.pallas_call(functools.partial(stats_kernel, na), out_shape=jax.ShapeDt...  19.5 us
  transfers between devices with their start and end apart: 23, of which 3 were waited for; matrix products, arithmetic and copies ran while one was open for 5% of the time, Pallas kernels for 55%

profile of v1, /device:TPU:8, one launch (start us, length us, event | category | flops | bytes accessed | tf_op | source)
XLA Modules:
  0.0 762.4 jit_solution(15991082151496757296)
XLA Ops:
  0.7 4.5 concatenate.24
  21.8 121.0 %start.1 = (bf16[4,256,2048]{2,1,0:T(8,128)(2,1)}, bf16[2048,512]{1,0:T(8,128)(2,1)}) custom-call(bf16[256,512]{1,0:T(8,128)(2,1)} %constant_dynamic-slice_fusion.4.tok_ref.refs_1_, bf16[3,256,512]{2,1,0:T(8,128)(2,1)} %bitcast.130, bf16[256,512]{1,0:T(8,128)(2,1)} %wout_ref.1), custom_call_target="tpu_custom_call" | custom-call | tf_op jit(solution)/shard_map/start/pallas_call | solution.py:386
  142.8 8.2 %qkv.1 = (f32[4,256,384]{2,1,0:T(8,128)}, f32[8,256]{1,0:T(8,128)}) custom-call(bf16[4,256,2048]{2,1,0:T(8,128)(2,1)} %get-tuple-element.36.x_ref, bf16[2048,512]{1,0:T(8,128)(2,1)} %get-tuple-element.37.w_ref), custom_call_target="tpu_custom_call" | custom-call | flops 1000000000 | bytes 20000000 | tf_op jit(solution)/shard_map/qkv/pallas_call | solution.py:453
  151.0 9.2 %stats6.1.stats_ref = f32[8,256]{1,0:T(8,128)} custom-call(f32[8,256]{1,0:T(8,128)} %get-tuple-element.39.stats_ref), custom_call_target="tpu_custom_call" | custom-call | tf_op jit(solution)/shard_map/stats6/pallas_call | solution.py:429
  160.4 4.9 psum.28
  166.0 34.6 %psum.29 = f32[2,2048]{1,0:T(2,128)S(1)} all-reduce(f32[2,2048]{1,0:T(2,128)S(1)} %pad_maximum_fusion.2), channel_id=1, replica_groups=mesh['a'=4,'b'=2,'p'=2,'q'=2] {'a','b'}, use_global_device_ids=true, to_apply=%region_1.2 | all-reduce | flops 4096 | bytes 32768 | tf_op jit(solution)/shard_map/psum | solution.py:705
  204.1 8.7 %attend.1 = (bf16[4,256,128]{2,1,0:T(8,128)(2,1)}, bf16[4,256,2048]{2,1,0:T(8,128)(2,1)}) custom-call(f32[4,256,384]{2,1,0:T(8,128)} %get-tuple-element.38.qkv_ref, f32[8,256]{1,0:T(8,128)} %stats6.1.stats_ref, f32[8,128]{1,0:T(8,128)} %concatenate.27.gain_ref, f32[256,128]{1,0:T(8,128)} %get-tuple-element.100.cos_ref, ...), custom_call_target="tpu_custom_call" | custom-call | flops 1000000000 | bytes 20000000 | tf_op jit(solution)/shard_map/attend/pallas_call | solution.py:453
  213.5 82.1 %reduce_attn.1 = (bf16[4,256,2048]{2,1,0:T(8,128)(2,1)}, f32[256,512]{1,0:T(8,128)}, f32[256,128]{1,0:T(8,128)}, f32[256,512]{1,0:T(8,128)}) custom-call(bf16[4,256,2048]{2,1,0:T(8,128)(2,1)} %get-tuple-element.40.refs_0_, bf16[256,512]{1,0:T(8,128)(2,1)} %constant_dynamic-slice_fusion.4.tok_ref.refs_1_, f32[8,512]{1,0:T(8,128)} %broadcast_in_dim.28.refs_2_.refs_4_), custom_call_target="tpu_custom_call" | custom-call | flops 100000000 | bytes 100000000 | tf_op jit(solution)/shard_map/reduce_attn/pallas_call | solution.py:304
  296.5 12.9 %mlp.1 = (f32[4,256,1024]{2,1,0:T(8,128)}, bf16[4,256,512]{2,1,0:T(8,128)(2,1)}, bf16[4,256,2048]{2,1,0:T(8,128)(2,1)}) custom-call(bf16[3,256,512]{2,1,0:T(8,128)(2,1)} %copy-done.2, bf16[3,256,512]{2,1,0:T(8,128)(2,1)} %collective-permute-done.refs_1_, bf16[3,256,512]{2,1,0:T(8,128)(2,1)} %collective-permute-done.1.refs_2_, ...), custom_call_target="tpu_custom_call" | custom-call | flops 1000000000 | bytes 20000000 | tf_op jit(solution)/shard_map/mlp/pallas_call | solution.py:453
  310.0 96.2 %reduce_mlp.1 = (bf16[4,256,2048]{2,1,0:T(8,128)(2,1)}, bf16[1,256,2048]{2,1,0:T(8,128)(2,1)}, f32[8,512]{1,0:T(8,128)}) custom-call(bf16[4,256,2048]{2,1,0:T(8,128)(2,1)} %get-tuple-element.42.refs_0_, f32[256,512]{1,0:T(8,128)} %get-tuple-element.43.refs_1_, f32[256,512]{1,0:T(8,128)} %constant_dynamic-slice_fusion.3.refs_2_.refs_1_, ...), custom_call_target="tpu_custom_call" | custom-call | flops 100000000 | bytes 100000000 | tf_op jit(solution)/shard_map/reduce_mlp/pallas_call | solution.py:304
  406.2 4.6 bitcast_convert_fusion.1
  412.9 13.7 %mlp_back.1 = (bf16[4,256,1024]{2,1,0:T(8,128)(2,1)}, bf16[4,256,2048]{2,1,0:T(8,128)(2,1)}) custom-call(bf16[3,256,512]{2,1,0:T(8,128)(2,1)} %copy-done.2, bf16[3,256,512]{2,1,0:T(8,128)(2,1)} %collective-permute-done.refs_1_, bf16[3,256,512]{2,1,0:T(8,128)(2,1)} %collective-permute-done.1.refs_2_, bf16[3,256,512]{2,1,0:T(8,128)(2,1)} %collective-permute-done.2.refs_3_, ...), custom_call_target="tpu_custom_call" | custom-call | flops 1000000000 | bytes 20000000 | tf_op jit(solution)/shard_map/mlp_back/pallas_call | solution.py:453
  426.6 7.4 bitcast_convert_fusion
  437.3 84.1 %reduce_back.1 = (bf16[4,256,2048]{2,1,0:T(8,128)(2,1)}, f32[256,512]{1,0:T(8,128)}, f32[8,512]{1,0:T(8,128)}) custom-call(bf16[4,256,2048]{2,1,0:T(8,128)(2,1)} %get-tuple-element.47.refs_0_, f32[256,512]{1,0:T(8,128)} %constant_dynamic-slice_fusion.3.refs_2_.refs_1_, f32[256,512]{1,0:T(8,128)} %get-tuple-element.48.refs_2_, ...), custom_call_target="tpu_custom_call" | custom-call | flops 100000000 | bytes 100000000 | tf_op jit(solution)/shard_map/reduce_back/pallas_call | solution.py:304
  521.4 12.1 %attend_back.1 = (f32[4,256,384]{2,1,0:T(8,128)}, f32[8,256]{1,0:T(8,128)}, f32[8,128]{1,0:T(8,128)}) custom-call(bf16[4,256,2048]{2,1,0:T(8,128)(2,1)} %get-tuple-element.50.proj_ref, f32[4,256,384]{2,1,0:T(8,128)} %get-tuple-element.38.qkv_ref, f32[8,256]{1,0:T(8,128)} %stats6.1.stats_ref, f32[8,128]{1,0:T(8,128)} %concatenate.27.gain_ref, ...), custom_call_target="tpu_custom_call" | custom-call | flops 1000000000 | bytes 20000000 | tf_op jit(solution)/shard_map/attend_back/pallas_call | solution.py:453
  539.0 10.2 %stats7.1.inner_ref = f32[8,256]{1,0:T(8,128)} custom-call(f32[8,256]{1,0:T(8,128)} %get-tuple-element.52.stats_ref), custom_call_target="tpu_custom_call" | custom-call | tf_op jit(solution)/shard_map/stats7/pallas_call | solution.py:429
  549.2 8.4 %qkv_back.1 = (bf16[4,256,384]{2,1,0:T(8,128)(2,1)}, bf16[4,256,2048]{2,1,0:T(8,128)(2,1)}) custom-call(f32[4,256,384]{2,1,0:T(8,128)} %get-tuple-element.51.scaled_ref, f32[4,256,384]{2,1,0:T(8,128)} %get-tuple-element.38.qkv_ref, f32[8,256]{1,0:T(8,128)} %stats6.1.stats_ref, f32[8,256]{1,0:T(8,128)} %stats7.1.inner_ref, ...), custom_call_target="tpu_custom_call" | custom-call | flops 1000000000 | bytes 20000000 | tf_op jit(solution)/shard_map/qkv_back/pallas_call | solution.py:453
  557.6 4.8 bitcast_convert_fusion.2
  563.9 54.2 %reduce_tok.1 = bf16[1,256,2048]{2,1,0:T(8,128)(2,1)} custom-call(bf16[4,256,2048]{2,1,0:T(8,128)(2,1)} %get-tuple-element.53.refs_0_, f32[256,512]{1,0:T(8,128)} %get-tuple-element.54.refs_1_), custom_call_target="tpu_custom_call" | custom-call | flops 100000000 | bytes 100000000 | tf_op jit(solution)/shard_map/reduce_tok/pallas_call | solution.py:304
  623.3 4.9 psum.31
  653.0 66.7 %psum.30 = f32[2,2048]{1,0:T(2,128)S(1)} all-reduce(f32[2,2048]{1,0:T(2,128)S(1)} %constant_dynamic-update-slice_fusion), channel_id=1, replica_groups=mesh['a'=4,'b'=2,'p'=2,'q'=2] {'a','b','p','q'}, use_global_device_ids=true, to_apply=%region_4.5 | all-reduce | flops 4096 | bytes 32768 | tf_op jit(solution)/shard_map/psum | solution.py:799
  729.6 10.1 %collective-permute-done.21.refs_2_ = bf16[256,512]{1,0:T(8,128)(2,1)S(1)} collective-permute-done((bf16[256,512]{1,0:T(8,128)(2,1)}, bf16[256,512]{1,0:T(8,128)(2,1)S(1)}, u32[]{:S(2)}, u32[]{:S(2)}) %collective-permute-start.21) | collective-permute-done | bytes 262176 | tf_op jit(solution)/shard_map/ppermute | solution.py:41
  739.7 6.8 collective-permute-done.22.refs_3_
  754.8 7.6 copy.31
  (151 shorter events, 83.3 us)
Async XLA Ops:
  0.6 295.0 %copy-start = (f32[256,2048]{1,0:T(8,128)S(1)}, f32[256,2048]{1,0:T(8,128)}, u32[]{:S(2)}) copy-start(f32[256,2048]{1,0:T(8,128)} %param.19) | copy-start | bytes 6291460
  15.1 185.6 %collective-permute-start.1 = (bf16[3,256,512]{2,1,0:T(8,128)(2,1)}, bf16[3,256,512]{2,1,0:T(8,128)(2,1)}, u32[]{:S(2)}, u32[]{:S(2)}) collective-permute-start(bf16[3,256,512]{2,1,0:T(8,128)(2,1)} %get-tuple-element.74), channel_id=1, source_target_pairs={{0,8},{8,0},{16,24},{24,16},{1,9},{9,1},{17,25},{25,17},{2,10},{10... | collective-permute-start | bytes 2359304 | tf_op jit(solution)/shard_map/ppermute | solution.py:41
  15.1 185.6 %collective-permute-start.3 = (bf16[3,256,512]{2,1,0:T(8,128)(2,1)}, bf16[3,256,512]{2,1,0:T(8,128)(2,1)}, u32[]{:S(2)}, u32[]{:S(2)}) collective-permute-start(bf16[3,256,512]{2,1,0:T(8,128)(2,1)} %get-tuple-element.73), channel_id=1, source_target_pairs={{0,16},{8,24},{16,0},{24,8},{1,17},{9,25},{17,1},{25,9},{2,18},{10... | collective-permute-start | bytes 2359304 | tf_op jit(solution)/shard_map/ppermute | solution.py:41
  18.1 184.6 %collective-permute-start.5 = (bf16[3,256,512]{2,1,0:T(8,128)(2,1)}, bf16[3,256,512]{2,1,0:T(8,128)(2,1)}, u32[]{:S(2)}, u32[]{:S(2)}) collective-permute-start(bf16[3,256,512]{2,1,0:T(8,128)(2,1)} %get-tuple-element.72), channel_id=1, source_target_pairs={{0,24},{8,16},{16,8},{24,0},{1,25},{9,17},{17,9},{25,1},{2,26},{10... | collective-permute-start | bytes 2359304 | tf_op jit(solution)/shard_map/ppermute | solution.py:41
  18.6 277.9 %collective-permute-start = (bf16[3,256,512]{2,1,0:T(8,128)(2,1)S(1)}, bf16[3,256,512]{2,1,0:T(8,128)(2,1)}, u32[]{:S(2)}, u32[]{:S(2)}) collective-permute-start(bf16[3,256,512]{2,1,0:T(8,128)(2,1)S(1)} %get-tuple-element.75.refs_0_), channel_id=1, source_target_pairs={{0,4},{4,0},{1,5},{5,1},{2,6},{6,2},{3,7},{7,3},{8,12},{12,8},{9,1... | collective-permute-start | bytes 2359304 | tf_op jit(solution)/shard_map/ppermute | solution.py:41
  200.6 95.8 %collective-permute-start.2 = (bf16[3,256,512]{2,1,0:T(8,128)(2,1)}, bf16[3,256,512]{2,1,0:T(8,128)(2,1)}, u32[]{:S(2)}, u32[]{:S(2)}) collective-permute-start(bf16[3,256,512]{2,1,0:T(8,128)(2,1)} %collective-permute-done.1.refs_2_), channel_id=1, source_target_pairs={{0,4},{4,0},{1,5},{5,1},{2,6},{6,2},{3,7},{7,3},{8,12},{12,8},{9,1... | collective-permute-start | bytes 2359304 | tf_op jit(solution)/shard_map/ppermute | solution.py:41
  200.6 95.8 %collective-permute-start.4 = (bf16[3,256,512]{2,1,0:T(8,128)(2,1)}, bf16[3,256,512]{2,1,0:T(8,128)(2,1)}, u32[]{:S(2)}, u32[]{:S(2)}) collective-permute-start(bf16[3,256,512]{2,1,0:T(8,128)(2,1)} %collective-permute-done.3.refs_4_), channel_id=1, source_target_pairs={{0,4},{4,0},{1,5},{5,1},{2,6},{6,2},{3,7},{7,3},{8,12},{12,8},{9,1... | collective-permute-start | bytes 2359304 | tf_op jit(solution)/shard_map/ppermute | solution.py:41
  202.7 93.8 %collective-permute-start.6 = (bf16[3,256,512]{2,1,0:T(8,128)(2,1)}, bf16[3,256,512]{2,1,0:T(8,128)(2,1)}, u32[]{:S(2)}, u32[]{:S(2)}) collective-permute-start(bf16[3,256,512]{2,1,0:T(8,128)(2,1)} %collective-permute-done.5.refs_6_), channel_id=1, source_target_pairs={{0,4},{4,0},{1,5},{5,1},{2,6},{6,2},{3,7},{7,3},{8,12},{12,8},{9,1... | collective-permute-start | bytes 2359304 | tf_op jit(solution)/shard_map/ppermute | solution.py:41
  410.9 225.0 %collective-permute-start.19 = (bf16[4,256,512]{2,1,0:T(8,128)(2,1)S(1)}, bf16[4,256,512]{2,1,0:T(8,128)(2,1)}, u32[]{:S(2)}, u32[]{:S(2)}) collective-permute-start(bf16[4,256,512]{2,1,0:T(8,128)(2,1)S(1)} %dynamic-slice_bitcast_fusion.1), channel_id=1, source_target_pairs={{0,4},{4,0},{1,5},{5,1},{2,6},{6,2},{3,7},{7,3},{8,12},{12,8},{9,1... | collective-permute-start | bytes 3145736 | tf_op jit(solution)/shard_map/ppermute | solution.py:41
  436.7 202.9 %collective-permute-start.15 = (bf16[4,256,1024]{2,1,0:T(8,128)(2,1)}, bf16[4,256,1024]{2,1,0:T(8,128)(2,1)}, u32[]{:S(2)}, u32[]{:S(2)}) collective-permute-start(bf16[4,256,1024]{2,1,0:T(8,128)(2,1)} %dynamic-slice_bitcast_fusion), channel_id=1, source_target_pairs={{0,4},{4,0},{1,5},{5,1},{2,6},{6,2},{3,7},{7,3},{8,12},{12,8},{9,1... | collective-permute-start | bytes 6291464 | tf_op jit(solution)/shard_map/ppermute | solution.py:41
  537.1 91.2 %collective-permute-start.11 = (bf16[4,256,128]{2,1,0:T(8,128)(2,1)S(1)}, bf16[4,256,128]{2,1,0:T(8,128)(2,1)}, u32[]{:S(2)}, u32[]{:S(2)}) collective-permute-start(bf16[4,256,128]{2,1,0:T(8,128)(2,1)S(1)} %dynamic-slice_bitcast_fusion.15), channel_id=1, source_target_pairs={{0,4},{4,0},{1,5},{5,1},{2,6},{6,2},{3,7},{7,3},{8,12},{12,8},{9,1... | collective-permute-start | bytes 786440 | tf_op jit(solution)/shard_map/ppermute | solution.py:41
  563.5 69.3 %collective-permute-start.7 = (bf16[4,256,384]{2,1,0:T(8,128)(2,1)}, bf16[4,256,384]{2,1,0:T(8,128)(2,1)}, u32[]{:S(2)}, u32[]{:S(2)}) collective-permute-start(bf16[4,256,384]{2,1,0:T(8,128)(2,1)} %dynamic-slice_bitcast_fusion.2), channel_id=1, source_target_pairs={{0,4},{4,0},{1,5},{5,1},{2,6},{6,2},{3,7},{7,3},{8,12},{12,8},{9,1... | collective-permute-start | bytes 2359304 | tf_op jit(solution)/shard_map/ppermute | solution.py:41
  630.0 14.0 %collective-permute-start.12 = (bf16[256,128]{1,0:T(8,128)(2,1)S(1)}, bf16[256,128]{1,0:T(8,128)(2,1)S(1)}, u32[]{:S(2)}, u32[]{:S(2)}) collective-permute-start(bf16[256,128]{1,0:T(8,128)(2,1)S(1)} %get-tuple-element.90), channel_id=1, source_target_pairs={{0,8},{8,0},{16,24},{24,16},{1,9},{9,1},{17,25},{25,17},{2,10},{10... | collective-permute-start | bytes 196616 | tf_op jit(solution)/shard_map/ppermute | solution.py:41
  630.0 15.5 %collective-permute-start.13 = (bf16[256,128]{1,0:T(8,128)(2,1)S(1)}, bf16[256,128]{1,0:T(8,128)(2,1)S(1)}, u32[]{:S(2)}, u32[]{:S(2)}) collective-permute-start(bf16[256,128]{1,0:T(8,128)(2,1)S(1)} %get-tuple-element.89), channel_id=1, source_target_pairs={{0,16},{8,24},{16,0},{24,8},{1,17},{9,25},{17,1},{25,9},{2,18},{10... | collective-permute-start | bytes 196616 | tf_op jit(solution)/shard_map/ppermute | solution.py:41
  632.8 14.7 %collective-permute-start.14 = (bf16[256,128]{1,0:T(8,128)(2,1)S(1)}, bf16[256,128]{1,0:T(8,128)(2,1)S(1)}, u32[]{:S(2)}, u32[]{:S(2)}) collective-permute-start(bf16[256,128]{1,0:T(8,128)(2,1)S(1)} %get-tuple-element.88), channel_id=1, source_target_pairs={{0,24},{8,16},{16,8},{24,0},{1,25},{9,17},{17,9},{25,1},{2,26},{10... | collective-permute-start | bytes 196616 | tf_op jit(solution)/shard_map/ppermute | solution.py:41
  635.8 12.2 %collective-permute-start.10 = (bf16[256,384]{1,0:T(8,128)(2,1)S(1)}, bf16[256,384]{1,0:T(8,128)(2,1)S(1)}, u32[]{:S(2)}, u32[]{:S(2)}) collective-permute-start(bf16[256,384]{1,0:T(8,128)(2,1)S(1)} %get-tuple-element.84), channel_id=1, source_target_pairs={{0,24},{8,16},{16,8},{24,0},{1,25},{9,17},{17,9},{25,1},{2,26},{10... | collective-permute-start | bytes 589832 | tf_op jit(solution)/shard_map/ppermute | solution.py:41
  639.6 11.4 %collective-permute-start.8 = (bf16[256,384]{1,0:T(8,128)(2,1)S(1)}, bf16[256,384]{1,0:T(8,128)(2,1)S(1)}, u32[]{:S(2)}, u32[]{:S(2)}) collective-permute-start(bf16[256,384]{1,0:T(8,128)(2,1)S(1)} %get-tuple-element.86), channel_id=1, source_target_pairs={{0,8},{8,0},{16,24},{24,16},{1,9},{9,1},{17,25},{25,17},{2,10},{10... | collective-permute-start | bytes 589832 | tf_op jit(solution)/shard_map/ppermute | solution.py:41
  644.0 80.0 %collective-permute-start.20 = (bf16[256,512]{1,0:T(8,128)(2,1)}, bf16[256,512]{1,0:T(8,128)(2,1)}, u32[]{:S(2)}, u32[]{:S(2)}) collective-permute-start(bf16[256,512]{1,0:T(8,128)(2,1)} %get-tuple-element.82), channel_id=1, source_target_pairs={{0,8},{8,0},{16,24},{24,16},{1,9},{9,1},{17,25},{25,17},{2,10},{10... | collective-permute-start | bytes 786440 | tf_op jit(solution)/shard_map/ppermute | solution.py:41
  645.4 75.0 %collective-permute-start.9 = (bf16[256,384]{1,0:T(8,128)(2,1)}, bf16[256,384]{1,0:T(8,128)(2,1)S(1)}, u32[]{:S(2)}, u32[]{:S(2)}) collective-permute-start(bf16[256,384]{1,0:T(8,128)(2,1)} %get-tuple-element.85), channel_id=1, source_target_pairs={{0,16},{8,24},{16,0},{24,8},{1,17},{9,25},{17,1},{25,9},{2,18},{10... | collective-permute-start | bytes 589832 | tf_op jit(solution)/shard_map/ppermute | solution.py:41
  647.4 102.5 %collective-permute-start.16 = (bf16[256,1024]{1,0:T(8,128)(2,1)}, bf16[256,1024]{1,0:T(8,128)(2,1)S(1)}, u32[]{:S(2)}, u32[]{:S(2)}) collective-permute-start(bf16[256,1024]{1,0:T(8,128)(2,1)} %get-tuple-element.78), channel_id=1, source_target_pairs={{0,8},{8,0},{16,24},{24,16},{1,9},{9,1},{17,25},{25,17},{2,10},{10... | collective-permute-start | bytes 1572872 | tf_op jit(solution)/shard_map/ppermute | solution.py:41
  648.0 101.9 %collective-permute-start.17 = (bf16[256,1024]{1,0:T(8,128)(2,1)S(1)}, bf16[256,1024]{1,0:T(8,128)(2,1)S(1)}, u32[]{:S(2)}, u32[]{:S(2)}) collective-permute-start(bf16[256,1024]{1,0:T(8,128)(2,1)S(1)} %get-tuple-element.77), channel_id=1, source_target_pairs={{0,16},{8,24},{16,0},{24,8},{1,17},{9,25},{17,1},{25,9},{2,18},{10... | collective-permute-start | bytes 1572872 | tf_op jit(solution)/shard_map/ppermute | solution.py:41
  651.0 98.9 %collective-permute-start.18 = (bf16[256,1024]{1,0:T(8,128)(2,1)S(1)}, bf16[256,1024]{1,0:T(8,128)(2,1)S(1)}, u32[]{:S(2)}, u32[]{:S(2)}) collective-permute-start(bf16[256,1024]{1,0:T(8,128)(2,1)S(1)} %get-tuple-element.76), channel_id=1, source_target_pairs={{0,24},{8,16},{16,8},{24,0},{1,25},{9,17},{17,9},{25,1},{2,26},{10... | collective-permute-start | bytes 1572872 | tf_op jit(solution)/shard_map/ppermute | solution.py:41
  721.1 18.6 %collective-permute-start.21 = (bf16[256,512]{1,0:T(8,128)(2,1)}, bf16[256,512]{1,0:T(8,128)(2,1)S(1)}, u32[]{:S(2)}, u32[]{:S(2)}) collective-permute-start(bf16[256,512]{1,0:T(8,128)(2,1)} %get-tuple-element.81), channel_id=1, source_target_pairs={{0,16},{8,24},{16,0},{24,8},{1,17},{9,25},{17,1},{25,9},{2,18},{10... | collective-permute-start | bytes 786440 | tf_op jit(solution)/shard_map/ppermute | solution.py:41
  724.0 22.6 %collective-permute-start.22 = (bf16[256,512]{1,0:T(8,128)(2,1)S(1)}, bf16[256,512]{1,0:T(8,128)(2,1)S(1)}, u32[]{:S(2)}, u32[]{:S(2)}) collective-permute-start(bf16[256,512]{1,0:T(8,128)(2,1)S(1)} %get-tuple-element.80), channel_id=1, source_target_pairs={{0,24},{8,16},{16,8},{24,0},{1,25},{9,17},{17,9},{25,1},{2,26},{10... | collective-permute-start | bytes 786440 | tf_op jit(solution)/shard_map/ppermute | solution.py:41
  (27 other events, 521.2 us)

commit v2 on v1

--- a/solution.py
+++ b/solution.py
@@ -7,6 +7,7 @@
 from jax.experimental.pallas import tpu as pltpu
 from jax.sharding import Mesh, PartitionSpec as P
 
+
 HEADS = 16
 HD = 128
 SEQ_LEN = 256
@@ -21,6 +22,7 @@
 EXACT = lax.Precision.HIGHEST
 VMEM_LIMIT = 60 * 1024 * 1024
 TILE = 64
+HALVES = 2
 
 
 def flip(index, bit):
@@ -47,10 +49,6 @@
 
 def span(index, size):
     return pl.ds(pl.multiple_of(index * size, size), size)
-
-
-def lead(na):
-    return list(range(1, na)) + [0]
 
 
 class Links:
@@ -83,14 +81,6 @@
     pl.semaphore_wait(barrier, len(peers))
 
 
-def tiles(rows, body):
-    def step(i, carry):
-        body(pl.ds(pl.multiple_of(i * TILE, TILE), TILE))
-        return carry
-
-    lax.fori_loop(0, rows // TILE, step, 0)
-
-
 def fold(block):
     total = block[:, :128]
     for i in range(1, block.shape[1] // 128):
@@ -118,65 +108,87 @@
     )
 
 
-def spread_copies(links, out, na, a, p, q, forward):
-    quarter = out.shape[-1] // 4
-    half = 2 * quarter
-    mine = span(2 * q + p, quarter)
-    pair = span(q, half)
-    blocks = range(na) if forward else range(1)
-    first = {
-        k: links.send(out.at[0, :, mine], out.at[k, :, mine], {"a": across(a, k)}) for k in blocks if k
-    }
-    second, third = {}, {}
-    for k in blocks:
-        if k:
-            first[k].wait_recv()
-        second[k] = links.send(out.at[k, :, mine], out.at[k, :, mine], {"p": 1 - p})
-    for k in blocks:
-        second[k].wait_recv()
-        third[k] = links.send(out.at[k, :, pair], out.at[k, :, pair], {"q": 1 - q})
-    for k in blocks:
-        third[k].wait_recv()
-
-
-def reduce_kernel(na, mode, *refs):
-    n_in = {"attn": 3, "mlp": 4, "back": 5, "tok": 2}[mode]
-    n_out = {"attn": 4, "mlp": 3, "back": 3, "tok": 1}[mode]
+def reduce_kernel(na, nb, mode, *refs):
+    n_in = {"attn": 3, "mlp": 4, "back": 5, "tok": 5}[mode]
+    n_out = {"attn": 4, "mlp": 3, "back": 3, "tok": 2}[mode]
     ins, outs, scratch = refs[:n_in], refs[n_in : n_in + n_out], refs[n_in + n_out :]
-    from_q, half_sum, from_p, to_a, from_a, total, parts, cols, stat, send_sem, recv_sem = scratch
+    from_q, half_sum, from_p, to_a, from_a, total, parts, cols, stat, *scratch = scratch
+    send_sem, recv_sem = scratch[-2:]
     part_ref, out = ins[0], outs[0]
-    a, p, q = lax.axis_index("a"), lax.axis_index("p"), lax.axis_index("q")
+    a, b = lax.axis_index("a"), lax.axis_index("b")
+    p, q = lax.axis_index("p"), lax.axis_index("q")
     rows, width = part_ref.shape[1], part_ref.shape[2]
     quarter, half = width // 4, width // 2
-    greet([{"q": 1 - q}, {"p": 1 - p}] + [{"a": across(a, k)} for k in range(1, na)])
+    count = rows // HALVES
+    mine, pair = span(2 * q + p, quarter), span(q, half)
+    peers = [{"q": 1 - q}, {"p": 1 - p}] + [{"a": across(a, k)} for k in range(1, na)]
+    if mode == "tok":
+        own_sums, a_sums, b_sums = scratch[:3]
+        sums_ref = outs[1]
+        own_sums[...] = jnp.zeros_like(own_sums)
+        own_sums[0:1, mine] = jnp.sum(ins[2][...], axis=0, keepdims=True)
+        own_sums[1:2, mine] = jnp.sum(ins[3][...], axis=0, keepdims=True)
+        peers += [{"b": across(b, j)} for j in range(1, nb)]
+    greet(peers)
     links = Links(send_sem, recv_sem)
-
+    halves = [slice(h * count, (h + 1) * count) for h in range(HALVES)]
+    lead = list(range(2, na)) + [1, 0]
     give, keep = span(1 - q, half), span(q, half)
-    step_q = {
-        k: links.send(part_ref.at[k, :, give], from_q.at[k], {"q": 1 - q}) for k in lead(na)
-    }
-    step_p, step_a = {}, {}
-    for k in lead(na):
-        step_q[k].wait_recv()
-
-        def add_half(at, k=k):
-            own = part_ref[k, at, keep].astype(f32)
-            half_sum[k, at] = (own + from_q[k, at].astype(f32)).astype(bf16)
-
-        tiles(rows, add_half)
-        step_p[k] = links.send(half_sum.at[k, :, span(1 - p, quarter)], from_p.at[k], {"p": 1 - p})
-    for k in lead(na):
-        step_p[k].wait_recv()
-        if k:
+
+    def each(h, body):
+        def step(i, carry):
+            body(pl.ds(pl.multiple_of(h * count + i * TILE, TILE), TILE))
+            return carry
+
+        lax.fori_loop(0, count // TILE, step, 0)
+
+    if mode == "tok":
+        sums_p = links.send(own_sums.at[:, mine], own_sums.at[:, mine], {"p": 1 - p})
+
+    step_q, step_p, step_a = {}, {}, {}
+    for h, at_h in enumerate(halves):
+        for k in lead:
+            step_q[h, k] = links.send(
+                part_ref.at[k, at_h, give], from_q.at[k, at_h], {"q": 1 - q}
+            )
+    for h, at_h in enumerate(halves):
+        for k in lead:
+            step_q[h, k].wait_recv()
+
+            def add_half(at, k=k):
+                own = part_ref[k, at, keep].astype(f32)
+                half_sum[k, at] = (own + from_q[k, at].astype(f32)).astype(bf16)
+
+            each(h, add_half)
+            step_p[h, k] = links.send(
+                half_sum.at[k, at_h, span(1 - p, quarter)], from_p.at[k, at_h], {"p": 1 - p}
+            )
+    if mode == "tok":
+        sums_p.wait_recv()
+        sums_q = links.send(own_sums.at[:, pair], own_sums.at[:, pair], {"q": 1 - q})
+
+    def send_a(h):
+        at_h = halves[h]
+        for k in lead[:-1]:
+            step_p[h, k].wait_recv()
 
             def add_quarter(at, k=k):
                 own = half_sum[k, at, span(p, quarter)].astype(f32)
                 to_a[k - 1, at] = (own + from_p[k, at].astype(f32)).astype(bf16)
 
-            tiles(rows, add_quarter)
-            step_a[k] = links.send(to_a.at[k - 1], from_a.at[k - 1], {"a": across(a, k)})
-    for k in range(1, na):
-        step_a[k].wait_recv()
+            each(h, add_quarter)
+            step_a[h, k] = links.send(
+                to_a.at[k - 1, at_h], from_a.at[k - 1, at_h], {"a": across(a, k)}
+            )
+
+    for h in range(HALVES):
+        send_a(h)
+    if mode == "tok":
+        sums_q.wait_recv()
+        sums_a = [
+            links.send(own_sums.at[:, span(across(a, k), quarter)], a_sums.at[k - 1], {"a": across(a, k)})
+            for k in range(1, na)
+        ]
 
     def add_all(at):
         own = half_sum[0, at, span(p, quarter)].astype(f32) + from_p[0, at].astype(f32)
@@ -184,31 +196,28 @@
             own = own + from_a[k - 1, at].astype(f32)
         return own
 
-    mine = span(2 * q + p, quarter)
-
-    def exchange(count):
-        stats = to_row(parts[0], 0)
-        if count == 2:
-            stats = stats + to_row(parts[1], 1)
-        stat[0] = stats
-        links.send(stat.at[0], stat.at[1], {"p": 1 - p}).wait_recv()
-        stat[2] = stat[0] + stat[1]
-        links.send(stat.at[2], stat.at[3], {"q": 1 - q}).wait_recv()
-        stats = (stat[2] + stat[3]) / width
-        for i in range(count):
-            cols[i] = to_column(stats, i)
+    def exchange(h, number):
+        at_h = halves[h]
+        stats = to_row(parts[0, at_h], 0)
+        if number == 2:
+            stats = stats + to_row(parts[1, at_h], 1)
+        stat[h, 0] = stats
+        links.send(stat.at[h, 0], stat.at[h, 1], {"p": 1 - p}).wait_recv()
+        stat[h, 2] = stat[h, 0] + stat[h, 1]
+        links.send(stat.at[h, 2], stat.at[h, 3], {"q": 1 - q}).wait_recv()
+        stats = (stat[h, 2] + stat[h, 3]) / width
+        for i in range(number):
+            cols[i, at_h] = to_column(stats, i)
 
     if mode == "attn":
         _, tok_ref, gain_ref = ins
         _, proj_ref, inv_ref, res_ref = outs
+        number = 1
 
         def first(at):
             own = add_all(at)
             proj_ref[at] = own
             parts[0, at] = fold(own * own)
-
-        tiles(rows, first)
-        exchange(1)
 
         def second(at):
             own = proj_ref[at]
@@ -218,45 +227,41 @@
             res_ref[at] = residual
             out[0, at, mine] = residual.astype(bf16)
 
-        tiles(rows, second)
     elif mode == "mlp":
         _, res_ref, grad_ref, gain_ref = ins
         _, block_ref, sum_ref = outs
+        number = 2
 
         def first(at):
             own = add_all(at)
             total[at] = own
             parts[0, at] = fold(own * own)
-            parts[1, at] = fold(grad_ref[at] * gain_ref[0:1] * own)
-
-        tiles(rows, first)
-        exchange(2)
+            parts[1, at] = fold(grad_ref[at] * gain_ref[1:2] * own)
+
         sum_ref[...] = jnp.zeros_like(sum_ref)
 
         def second(at):
             own = total[at]
             inv = wide(lax.rsqrt(cols[0, at] + epsilon), quarter)
             upstream = grad_ref[at]
-            scaled = upstream * gain_ref[0:1]
+            scaled = upstream * gain_ref[1:2]
             normed = own * inv
-            block_ref[0, at, mine] = (res_ref[at] + normed * gain_ref[0:1]).astype(bf16)
+            block_ref[0, at, mine] = (res_ref[at] + normed * gain_ref[1:2]).astype(bf16)
             gains = upstream * normed
             sum_ref[...] += jnp.sum(gains.reshape(TILE // 8, 8, quarter), axis=0)
             grad = inv * scaled - own * inv * inv * inv * wide(cols[1, at], quarter)
             out[0, at, mine] = grad.astype(bf16)
 
-        tiles(rows, second)
     elif mode == "back":
         _, grad_ref, proj_ref, inv_ref, gain_ref = ins
         _, res_ref, sum_ref = outs
+        number = 1
 
         def first(at):
             grad = grad_ref[at] + add_all(at)
             res_ref[at] = grad
             parts[0, at] = fold(grad * gain_ref[0:1] * proj_ref[at])
 
-        tiles(rows, first)
-        exchange(1)
         sum_ref[...] = jnp.zeros_like(sum_ref)
 
         def second(at):
@@ -269,24 +274,70 @@
             grad = grad - own * inv * inv * inv * wide(cols[0, at], quarter)
             out[0, at, mine] = grad.astype(bf16)
 
-        tiles(rows, second)
     else:
-        _, grad_ref = ins
+        grad_ref = ins[1]
+        number = 0
 
         def first(at):
             out[0, at, mine] = (grad_ref[at] + add_all(at)).astype(bf16)
 
-        tiles(rows, first)
-
+    blocks = range(1) if mode == "tok" else range(na)
+    spread_a, spread_p, spread_q = {}, {}, {}
+    for h, at_h in enumerate(halves):
+        step_p[h, 0].wait_recv()
+        for k in range(1, na):
+            step_a[h, k].wait_recv()
+        each(h, first)
+        if number:
+            exchange(h, number)
+            each(h, second)
+        here = out.at[0, at_h, mine]
+        for k in blocks:
+            if k:
+                spread_a[h, k] = links.send(here, out.at[k, at_h, mine], {"a": across(a, k)})
+        spread_p[h, 0] = links.send(here, here, {"p": 1 - p})
+    if mode == "tok":
+        for copy in sums_a:
+            copy.wait_recv()
+        held = own_sums[:, span(a, quarter)]
+        for k in range(1, na):
+            held = held + a_sums[k - 1]
+        b_sums[0, :, :quarter] = held
+        b_sums[0, :, quarter:] = ins[4][...]
+        sums_b = [
+            links.send(b_sums.at[0], b_sums.at[j], {"b": across(b, j)}) for j in range(1, nb)
+        ]
+    for h, at_h in enumerate(halves):
+        for k in blocks:
+            if k:
+                spread_a[h, k].wait_recv()
+                here = out.at[k, at_h, mine]
+                spread_p[h, k] = links.send(here, here, {"p": 1 - p})
     if mode == "mlp":
-        spread_copies(links, out, na, a, p, q, True)
-        spread_copies(links, block_ref, na, a, p, q, False)
-    else:
-        spread_copies(links, out, na, a, p, q, mode != "tok")
+        here = block_ref.at[0, :, mine]
+        block_p = links.send(here, here, {"p": 1 - p})
+    for h, at_h in enumerate(halves):
+        for k in blocks:
+            spread_p[h, k].wait_recv()
+            here = out.at[k, at_h, pair]
+            spread_q[h, k] = links.send(here, here, {"q": 1 - q})
+    if mode == "mlp":
+        block_p.wait_recv()
+        here = block_ref.at[0, :, pair]
+        links.send(here, here, {"q": 1 - q}).wait_recv()
+    if mode == "tok":
+        for copy in sums_b:
+            copy.wait_recv()
+        held = b_sums[0]
+        for j in range(1, nb):
+            held = held + b_sums[j]
+        sums_ref[...] = held
+    for copy in spread_q.values():
+        copy.wait_recv()
     links.finish()
 
 
-def reduce_call(mode, part, *operands):
+def reduce_call(mode, nb, part, *operands):
     na, rows, width = part.shape
     quarter = width // 4
     shape = jax.ShapeDtypeStruct
@@ -298,14 +349,25 @@
         "attn": (full, share, shape((rows, 128), f32), share),
         "mlp": (full, one, sums),
         "back": (full, share, sums),
-        "tok": (one,),
+        "tok": (one, shape((8, quarter + HD), f32)),
     }[mode]
-    copies = 3 * na + 1 + {"attn": 3 * na + 1, "mlp": 3 * na + 3, "back": 3 * na + 1, "tok": 2}[mode]
+    copies = HALVES * (3 * na - 1)
+    if mode == "tok":
+        copies += HALVES * 2 + 1 + na + nb
+        extra = [
+            pltpu.VMEM((8, width), f32),
+            pltpu.VMEM((na - 1, 8, quarter), f32),
+            pltpu.VMEM((nb, 8, quarter + HD), f32),
+        ]
+    else:
+        copies += HALVES * (2 + 3 * na - 1) + (2 if mode == "mlp" else 0)
+        extra = []
+    vmem = pl.BlockSpec(memory_space=pltpu.VMEM)
     return pl.pallas_call(
-        functools.partial(reduce_kernel, na, mode),
+        functools.partial(reduce_kernel, na, nb, mode),
         out_shape=outs,
-        in_specs=[pl.BlockSpec(memory_space=pltpu.VMEM)] * (1 + len(operands)),
-        out_specs=tuple([pl.BlockSpec(memory_space=pltpu.VMEM)] * len(outs)),
+        in_specs=[vmem] * (1 + len(operands)),
+        out_specs=(vmem,) * len(outs),
         scratch_shapes=[
             pltpu.VMEM((na, rows, width // 2), bf16),
             pltpu.VMEM((na, rows, width // 2), bf16),
@@ -315,36 +377,44 @@
             pltpu.VMEM((rows, quarter), f32),
             pltpu.VMEM((2, rows, 128), f32),
             pltpu.VMEM((2, rows, 128), f32),
-            pltpu.VMEM((4, 8, rows), f32),
-            pltpu.SemaphoreType.DMA((copies,)),
-            pltpu.SemaphoreType.DMA((copies,)),
-        ],
+            pltpu.VMEM((HALVES, 4, 8, rows // HALVES), f32),
+        ]
+        + extra
+        + [pltpu.SemaphoreType.DMA((copies,)), pltpu.SemaphoreType.DMA((copies,))],
         compiler_params=pltpu.CompilerParams(
             collective_id={"attn": 1, "mlp": 2, "back": 3, "tok": 4}[mode],
             has_side_effects=True,
             vmem_limit_bytes=VMEM_LIMIT,
         ),
         cost_estimate=pl.CostEstimate(flops=10**8, bytes_accessed=10**8, transcendentals=0),
-        name="reduce_" + mode,
     )(part, *operands)
 
 
-def start_kernel(na, nb, tok_ref, qkv_ref, wout_ref, x_ref, w_ref, local_sem, send_sem, recv_sem):
+def start_kernel(na, nb, *refs):
+    tok_ref, qkv_ref, wout_ref, gu_ref, down_ref = refs[:5]
+    gain_refs, (x_ref, w_ref, gains_ref) = refs[5:9], refs[9:12]
+    piece_refs, (own_gains, local_sem, send_sem, recv_sem) = refs[12 : 12 + na], refs[12 + na :]
     a, b, p, q = (lax.axis_index(axis) for axis in ("a", "b", "p", "q"))
     rows = wout_ref.shape[0]
     quarter = tok_ref.shape[1]
+    own_gains[...] = jnp.zeros_like(own_gains)
+    for i, ref in enumerate(gain_refs):
+        own_gains[i : i + 1, : ref.shape[1]] = ref[...].astype(f32)
+    gains_ref[a, b] = own_gains[...]
     greet(
         [{"q": 1 - q}, {"p": 1 - p}]
         + [{"a": across(a, k)} for k in range(1, na)]
         + [{"b": across(b, j)} for j in range(1, nb)]
     )
     links = Links(send_sem, recv_sem)
-    mine = span(2 * q + p, quarter)
-    pair = span(q, 2 * quarter)
+    gains_a = [
+        links.send(own_gains, gains_ref.at[a, b], {"a": across(a, k)}) for k in range(1, na)
+    ]
+    mine, pair = span(2 * q + p, quarter), span(q, 2 * quarter)
     place = span(a * nb + b, rows)
     locals_ = [pltpu.make_async_copy(tok_ref, x_ref.at[0, :, mine], local_sem.at[0])]
-    arrive = {}
-    for k in range(na):
+    arrive, first = {}, {}
+    for k in list(range(1, na)) + [0]:
         block = span(across(a, k), HD)
         sources = [qkv_ref.at[c, :, block] for c in range(3)] + [wout_ref.at[:, block]]
         for c, source in enumerate(sources):
@@ -353,45 +423,72 @@
                 arrive[k, c] = links.send(source, target, {"a": across(a, k)})
             else:
                 locals_.append(pltpu.make_async_copy(source, target, local_sem.at[1 + c]))
-    first = {
-        k: links.send(tok_ref, x_ref.at[k, :, mine], {"a": across(a, k)}) for k in range(1, na)
-    }
+        if k:
+            first[k] = links.send(tok_ref, x_ref.at[k, :, mine], {"a": across(a, k)})
     for copy in locals_:
         copy.start()
     for copy in locals_:
         copy.wait()
-    ends, second, third = [], {}, {}
-    for k in range(na):
-        if k:
-            for c in range(4):
-                arrive[k, c].wait_recv()
+    ends, second = [], {}
+
+    def forward(k):
         at = w_ref.at[span(across(a, k) * nb + b, rows), :]
         for j in range(1, nb):
             ends.append(links.send(at, at, {"b": across(b, j)}))
-        if k:
-            first[k].wait_recv()
-        second[k] = links.send(x_ref.at[k, :, mine], x_ref.at[k, :, mine], {"p": 1 - p})
+        at = x_ref.at[k, :, mine]
+        second[k] = links.send(at, at, {"p": 1 - p})
+
+    forward(0)
+    units = down_ref.shape[1] // na
+    for k in range(na):
+        block = span(across(a, k), units)
+
+        def cut(i, carry, k=k, block=block):
+            at = pl.ds(pl.multiple_of(i * TILE, TILE), TILE)
+            piece_refs[k][0, at] = gu_ref[at, 0, block]
+            piece_refs[k][1, at] = gu_ref[at, 1, block]
+            piece_refs[k][2, at] = down_ref[at, block]
+            return carry
+
+        lax.fori_loop(0, rows // TILE, cut, 0)
+    for copy in gains_a:
+        copy.wait_recv()
+    at = gains_ref.at[:, b]
+    for j in range(1, nb):
+        ends.append(links.send(at, at, {"b": across(b, j)}))
+    for k in range(1, na):
+        for c in range(4):
+            arrive[k, c].wait_recv()
+        first[k].wait_recv()
+        forward(k)
     for k in range(na):
         second[k].wait_recv()
-        third[k] = links.send(x_ref.at[k, :, pair], x_ref.at[k, :, pair], {"q": 1 - q})
-    for copy in list(third.values()) + ends:
+        at = x_ref.at[k, :, pair]
+        ends.append(links.send(at, at, {"q": 1 - q}))
+    for copy in ends:
         copy.wait_recv()
     links.finish()
 
 
-def start_call(na, nb, tok_mine, qkv, w_out):
+def start_call(na, nb, tok_mine, qkv, w_out, gu, down, gains):
     rows, quarter = tok_mine.shape
     width = 4 * quarter
-    copies = (na - 1) * 5 + na * (nb - 1) + 2 * na
-    return pl.pallas_call(
+    w_rows, units = down.shape[0], down.shape[1] // na
+    lanes = max(128, gains[0].shape[1])
+    copies = (na - 1) * 6 + na * (nb - 1) + (nb - 1) + 2 * na
+    vmem = pl.BlockSpec(memory_space=pltpu.VMEM)
+    outs = [
+        jax.ShapeDtypeStruct((na, rows, width), bf16),
+        jax.ShapeDtypeStruct((width, 4 * HD), bf16),
+        jax.ShapeDtypeStruct((na, nb, 8, lanes), f32),
+    ] + [jax.ShapeDtypeStruct((3, w_rows, units), bf16)] * na
+    x_all, w_attn, gains_all, *pieces = pl.pallas_call(
         functools.partial(start_kernel, na, nb),
-        out_shape=(
-            jax.ShapeDtypeStruct((na, rows, width), bf16),
-            jax.ShapeDtypeStruct((width, 4 * HD), bf16),
-        ),
-        in_specs=[pl.BlockSpec(memory_space=pltpu.VMEM)] * 3,
-        out_specs=(pl.BlockSpec(memory_space=pltpu.VMEM), pl.BlockSpec(memory_space=pltpu.VMEM)),
+        out_shape=tuple(outs),
+        in_specs=[vmem] * 9,
+        out_specs=(vmem,) * len(outs),
         scratch_shapes=[
+            pltpu.VMEM((8, lanes), f32),
             pltpu.SemaphoreType.DMA((5,)),
             pltpu.SemaphoreType.DMA((copies,)),
             pltpu.SemaphoreType.DMA((copies,)),
@@ -400,7 +497,8 @@
             collective_id=5, has_side_effects=True, vmem_limit_bytes=VMEM_LIMIT
         ),
         name="start",
-    )(tok_mine, qkv, w_out)
+    )(tok_mine, qkv, w_out, gu, down, *gains)
+    return x_all, w_attn, gains_all, pieces
 
 
 def stats_kernel(na, stats_ref, out_ref, held, from_a, send_sem, recv_sem):
@@ -438,11 +536,10 @@
             pltpu.SemaphoreType.DMA((na + 1,)),
         ],
         compiler_params=pltpu.CompilerParams(collective_id=ident, has_side_effects=True),
-        name="stats" + str(ident),
     )(stats)
 
 
-def local_call(kernel, name, na, operands, outs, scratch=(), flops=10**9):
+def local_call(kernel, na, operands, outs, scratch=(), flops=10**9):
     def spec(shape, kind):
         if kind == "row":
             return pl.BlockSpec((1,) + tuple(shape[1:]), lambda k: (k,) + (0,) * (len(shape) - 1))
@@ -461,7 +558,6 @@
             dimension_semantics=("arbitrary",), vmem_limit_bytes=VMEM_LIMIT
         ),
         cost_estimate=pl.CostEstimate(flops=flops, bytes_accessed=2 * 10**7, transcendentals=0),
-        name=name,
     )(*[array for array, _ in operands])
 
 
@@ -639,7 +735,7 @@
             ].astype(f32)
 
 
-def widen(pieces, count, name):
+def widen(pieces, count):
     na = len(pieces)
     rows, width = pieces[0].shape
     return pl.pallas_call(
@@ -648,7 +744,6 @@
         in_specs=[pl.BlockSpec(memory_space=pltpu.VMEM)] * na,
         out_specs=pl.BlockSpec(memory_space=pltpu.VMEM),
         compiler_params=pltpu.CompilerParams(vmem_limit_bytes=VMEM_LIMIT),
-        name=name,
     )(*pieces)
 
 
@@ -661,7 +756,7 @@
     return cos_table, sine_table
 
 
-def on_device(
+def block(
     tokens,
     qkv_weight,
     out_weight,
@@ -684,39 +779,26 @@
     def quarter_of(operand):
         return lax.dynamic_slice_in_dim(operand, share * quarter, quarter, 1)
 
-    def whole_gain(gain):
-        own = jnp.zeros((HQ,), f32)
-        return lax.dynamic_update_slice_in_dim(own, gain.astype(f32), (a * nb + b) * gain.shape[0], 0)
-
     tok_mine, grad_mine = quarter_of(tokens), quarter_of(out_grad)
-    x_all, w_attn = start_call(
-        na, nb, tok_mine, qkv_weight.transpose(1, 0, 2), out_weight
-    )
-
-    shards = jnp.concatenate([gu_weight.transpose(1, 0, 2), down_weight[None]], axis=0)
-    shards = shards.reshape(3, w_rows, na, units)
-    pieces = []
-    for k in range(na):
-        piece = pick(shards, a ^ k, 2)
-        if k:
-            piece = swap(piece, "a", k)
-        pieces += [piece] + [swap(piece, "b", j) for j in range(1, nb)]
-
-    gains = lax.psum(jnp.stack([whole_gain(attn_gain), whole_gain(ffn_gain)]), ("a", "b"))
-    gains = lax.dynamic_slice_in_dim(gains, share * quarter, quarter, 1)
-    gain_attn = jnp.broadcast_to(gains[0:1], (8, quarter))
-    gain_ffn = jnp.broadcast_to(gains[1:2], (8, quarter))
-    n_h = q_gain.shape[0]
-    head_gain = jnp.zeros((nb, 2, n_h), f32)
-    own = jnp.stack([q_gain, k_gain]).astype(f32)
-    head_gain = lax.psum(lax.dynamic_update_index_in_dim(head_gain, own, b, 0), "b")
-    head_gain = head_gain.transpose(1, 0, 2).reshape(2, HD)
-    head_gain = jnp.concatenate([head_gain, jnp.zeros((6, HD), f32)])
+    x_all, w_attn, gains, cuts = start_call(
+        na,
+        nb,
+        tok_mine,
+        qkv_weight.transpose(1, 0, 2),
+        out_weight,
+        gu_weight,
+        down_weight,
+        [gain[None] for gain in (attn_gain, ffn_gain, q_gain, k_gain)],
+    )
+    n_d, n_h = attn_gain.shape[0], q_gain.shape[0]
+    width_gain = pick(gains, share, 0)[:, :2, :n_d].transpose(1, 0, 2).reshape(2, quarter)
+    head_gain = pick(gains, a, 0)[:, 2:4, :n_h].transpose(1, 0, 2).reshape(2, HD)
     cos_table, sine_table = rope_tables(SEQ_LEN, HD)
+
+    arrived = [cuts[k] if k == 0 else swap(cuts[k], "a", k) for k in range(na)]
 
     qkv, stats = local_call(
         qkv_kernel,
-        "qkv",
         na,
         [(x_all, "row"), (w_attn, "all")],
         [((na, rows, 3 * HD), f32, "row"), ((8, rows), f32, "all")],
@@ -726,12 +808,15 @@
     full = (na, rows, width)
     attended, part = local_call(
         attend_kernel,
-        "attend",
         na,
         [(qkv, "row")] + tables + [(w_attn, "all")],
         [((na, rows, HD), bf16, "row"), (full, bf16, "row")],
     )
-    res_all, proj_mine, inv_mine, res_mine = reduce_call("attn", part, tok_mine, gain_attn)
+    part, arrived = lax.optimization_barrier((part, arrived))
+    pieces = []
+    for piece in arrived:
+        pieces += [piece] + [swap(piece, "b", j) for j in range(1, nb)]
+    res_all, proj_mine, inv_mine, res_mine = reduce_call("attn", nb, part, tok_mine, width_gain)
 
     mlp_scratch = [
         pltpu.VMEM((width, 3 * units), bf16),
@@ -740,16 +825,14 @@
     far = [(piece, "far") for piece in pieces]
     gate_up, hidden, part = local_call(
         functools.partial(mlp_kernel, na, nb),
-        "mlp",
         na,
         far + [(res_all, "row")],
         [((na, rows, 2 * units), f32, "row"), ((na, rows, units), bf16, "row"), (full, bf16, "row")],
         mlp_scratch,
     )
-    grad_mlp, block_rows, ffn_sums = reduce_call("mlp", part, res_mine, grad_mine, gain_ffn)
+    grad_mlp, block_rows, ffn_sums = reduce_call("mlp", nb, part, res_mine, grad_mine, width_gain)
     grad_gu, part = local_call(
         functools.partial(mlp_back_kernel, na, nb),
-        "mlp_back",
         na,
         far + [(grad_mlp, "row"), (gate_up, "row")],
         [((na, rows, 2 * units), bf16, "row"), (full, bf16, "row")],
@@ -767,47 +850,44 @@
         return total.astype(bf16)
 
     def to_owner(grad):
-        return [pick(grad, a, 0)] + [swap(pick(grad, a ^ k, 0), "a", k) for k in range(1, na)]
-
-    down_sum = to_owner(reduce_b(weight_grad(grad_mlp, hidden)))
-    gu_sum = to_owner(reduce_b(weight_grad(res_all, grad_gu)))
+        parts = [pick(grad, a ^ k, 0) for k in range(na)]
+        return parts[:1] + [swap(parts[k], "a", k) for k in range(1, na)]
+
+    down_sum = reduce_b(weight_grad(grad_mlp, hidden))
+    gu_sum = reduce_b(weight_grad(res_all, grad_gu))
     grad_proj, grad_res, attn_sums = reduce_call(
-        "back", part, grad_mine, proj_mine, inv_mine, gain_attn
-    )
+        "back", nb, part, grad_mine, proj_mine, inv_mine, width_gain
+    )
+    grad_proj, down_sum, gu_sum = lax.optimization_barrier((grad_proj, down_sum, gu_sum))
+    down_sum = to_owner(down_sum)
     scaled, inner, head_sums = local_call(
         attend_back_kernel,
-        "attend_back",
         na,
         [(grad_proj, "row"), (qkv, "row")] + tables + [(w_attn, "all")],
         [((na, rows, 3 * HD), f32, "row"), ((8, rows), f32, "all"), ((8, HD), f32, "all")],
     )
-    out_sum = to_owner(reduce_b(weight_grad(grad_proj, attended)))
+    out_sum = reduce_b(weight_grad(grad_proj, attended))
     inner = stats_call(na, inner, 7)
+    inner, gu_sum = lax.optimization_barrier((inner, gu_sum))
+    gu_sum = to_owner(gu_sum)
     grad_qkv, part = local_call(
         qkv_back_kernel,
-        "qkv_back",
         na,
         [(scaled, "row"), (qkv, "row"), (stats, "all"), (inner, "all"), (w_attn, "all")],
         [((na, rows, 3 * HD), bf16, "row"), (full, bf16, "row")],
     )
     qkv_sum = to_owner(reduce_b(weight_grad(x_all, grad_qkv)))
-    (grad_rows,) = reduce_call("tok", part, grad_res)
-
-    sums = jnp.stack([jnp.sum(attn_sums, axis=0), jnp.sum(ffn_sums, axis=0)])
-    place = jnp.zeros((2, width), f32)
-    width_sums = lax.dynamic_update_slice_in_dim(place, sums, share * quarter, 1)
-    width_sums = lax.psum(width_sums, ("a", "b", "p", "q"))
-    n_d = attn_gain.shape[0]
-    width_sums = lax.dynamic_slice_in_dim(width_sums, (a * nb + b) * n_d, n_d, 1)
-    head_sums = lax.psum(head_sums[:2], "b")
-    head_sums = lax.dynamic_slice_in_dim(head_sums, b * n_h, n_h, 1)
+    out_sum = to_owner(out_sum)
+    grad_rows, sums = reduce_call("tok", nb, part, grad_res, attn_sums, ffn_sums, head_sums)
+    width_sums = lax.dynamic_slice_in_dim(sums[:2, :quarter], b * n_d, n_d, 1)
+    head_sums = lax.dynamic_slice_in_dim(sums[:2, quarter:], b * n_h, n_h, 1)
     return (
         block_rows[0].astype(f32),
         grad_rows[0].astype(f32),
-        widen(qkv_sum, 3, "widen_qkv").transpose(1, 0, 2),
-        widen(out_sum, 1, "widen_out")[0],
-        widen(gu_sum, 2, "widen_gu").transpose(1, 0, 2),
-        widen(down_sum, 1, "widen_down")[0],
+        widen(qkv_sum, 3).transpose(1, 0, 2),
+        widen(out_sum, 1)[0],
+        widen(gu_sum, 2).transpose(1, 0, 2),
+        widen(down_sum, 1)[0],
         width_sums[0],
         width_sums[1],
         head_sums[0],
@@ -822,7 +902,7 @@
     dp_axes, tp_axes = ("a", "b"), ("p", "q")
     both = tp_axes + dp_axes
     return jax.shard_map(
-        on_device,
+        block,
         mesh=fine,
         in_specs=(
             P(dp_axes, None),

time: 765 us -> 603 us (0.79)
  blocking collectives: 111 us -> 0 us
  Pallas kernels: 532 us -> 464 us
  waiting for transfers between devices: 17.7 us -> 42.9 us
  local copies, waits for them, and re-layouts: 38.3 us -> 29.2 us
    pallas_call x5, Pallas kernels: 438 us -> 316 us  [the longest x4 252 us: reduce_call(): pl.pallas_call(functools.partial(reduce_kernel, na, nb, mode), out_shape=...]
    psum x4 -> x0, blocking collectives: 111 us -> none  [the longest x1 66.7 us: on_device(): width_sums = lax.psum(width_sums, ('a', 'b', 'p', 'q'))]
    pallas_call x2, Pallas kernels: 19.5 us -> 73.1 us  [stats_call(): pl.pallas_call(functools.partial(stats_kernel, na), out_shape=jax.ShapeDt...]
    ppermute x23, waiting for transfers between devices: 17.7 us -> 42.9 us  [swap(): return lax.ppermute(operand, axis, [(i, i ^ k) for i in range(n)])]
    concatenate x4 -> x0, local copies, waits for them, and re-layouts: 8.13 us -> none  [the longest x3 7.53 us: on_device(): jnp.concatenate([gu_weight.transpose(1, 0, 2), down_weight[None]], axis=0)]
  transfers between devices with their start and end apart: 23 -> 23, of which waited for: 3 -> 2; matrix products, arithmetic and copies ran while one was open for 5% -> 7% of each run, Pallas kernels for 55% -> 49%
where the time goes in v2:
time: 603 us; the launch traced here: 598 us
  Pallas kernels  464 us (77%)
  waiting for transfers between devices  42.9 us (7%)
  starting transfers between devices  30.4 us (5%)
  local copies, waits for them, and re-layouts  29.2 us (5%)
  matrix products  18.2 us (3%)
  other arithmetic  12.6 us (2%)
    pallas_call x4, Pallas kernels, reduce_call(): pl.pallas_call(functools.partial(reduce_kernel, na, nb, mode), out_shape=...  252 us
    pallas_call x2, Pallas kernels, stats_call(): pl.pallas_call(functools.partial(stats_kernel, na), out_shape=jax.ShapeDt...  73.1 us
    pallas_call x1, Pallas kernels, start_call(): pl.pallas_call(functools.partial(start_kernel, na, nb), out_shape=tuple(o...  64.3 us
    pallas_call x6, Pallas kernels, local_call(): pl.pallas_call(kernel, grid=(na,), out_shape=tuple((jax.ShapeDtypeStruct(...  64 us
    ppermute x23, waiting for transfers between devices, swap(): return lax.ppermute(operand, axis, [(i, i ^ k) for i in range(n)])  42.9 us
    ppermute x23, starting transfers between devices, swap(): return lax.ppermute(operand, axis, [(i, i ^ k) for i in range(n)])  30.4 us
    dot_general x4, matrix products, weight_grad(): out = jnp.einsum('krd,kru->du', left, right, preferred_element_type=f32)  18.2 us
  transfers between devices with their start and end apart: 23, of which 2 were waited for; matrix products, arithmetic and copies ran while one was open for 7% of the time, Pallas kernels for 49%

profile of v2, /device:TPU:8, one launch (start us, length us, event | category | flops | bytes accessed | tf_op | source)
XLA Modules:
  0.0 598.1 jit_solution(18196649317056807593)
XLA Ops:
  4.9 64.3 %start.1 = (bf16[4,256,2048]{2,1,0:T(8,128)(2,1)}, bf16[2048,512]{1,0:T(8,128)(2,1)}, f32[4,2,8,256]{3,2,1,0:T(8,128)}, bf16[3,256,512]{2,1,0:T(8,128)(2,1)}, bf...) custom-call(bf16[256,512]{1,0:T(8,128)(2,1)} %constant_dynamic-slice_fusion.3.refs_0_.refs_1_,, ...), custom_call_target="tpu_custom_call" | custom-call | tf_op jit(solution)/shard_map/start/pallas_call | solution.py:485
  69.3 2.9 collective-permute-start.1
  74.2 8.1 %shard_map.177 = (f32[4,256,384]{2,1,0:T(8,128)}, f32[8,256]{1,0:T(8,128)}) custom-call(bf16[4,256,2048]{2,1,0:T(8,128)(2,1)} %get-tuple-element.53.x_ref, bf16[2048,512]{1,0:T(8,128)(2,1)} %get-tuple-element.54.w_ref), custom_call_target="tpu_custom_call" | custom-call | flops 1000000000 | bytes 20000000 | tf_op jit(solution)/shard_map/pallas_call | solution.py:550
  82.3 60.3 %shard_map.178.stats_ref = f32[8,256]{1,0:T(8,128)} custom-call(f32[8,256]{1,0:T(8,128)} %get-tuple-element.56.stats_ref), custom_call_target="tpu_custom_call" | custom-call | tf_op jit(solution)/shard_map/pallas_call | solution.py:527
  143.9 8.7 %shard_map.179 = (bf16[4,256,128]{2,1,0:T(8,128)(2,1)}, bf16[4,256,2048]{2,1,0:T(8,128)(2,1)}) custom-call(f32[4,256,384]{2,1,0:T(8,128)} %get-tuple-element.55.qkv_ref, f32[8,256]{1,0:T(8,128)} %shard_map.178.stats_ref, f32[2,128]{1,0:T(2,128)} %reshape.57.gain_ref, f32[256,128]{1,0:T(8,128)} %get-tuple-element.140.cos_ref, ...), custom_call_target="tpu_custom_call" | custom-call | flops 1000000000 | bytes 20000000 | tf_op jit(solution)/shard_map/pallas_call | solution.py:550
  158.2 68.5 %shard_map.180 = (bf16[4,256,2048]{2,1,0:T(8,128)(2,1)}, f32[256,512]{1,0:T(8,128)}, f32[256,128]{1,0:T(8,128)}, f32[256,512]{1,0:T(8,128)}) custom-call(bf16[4,256,2048]{2,1,0:T(8,128)(2,1)} %get-tuple-element.67.refs_0_, bf16[256,512]{1,0:T(8,128)(2,1)} %constant_dynamic-slice_fusion.3.refs_0_.refs_1_, f32[2,512]{1,0:T(2,128)} %bitcast.123), custom_call_target="tpu_custom_call" | custom-call | flops 100000000 | bytes 100000000 | tf_op jit(solution)/shard_map/pallas_call | solution.py:366
  226.8 13.0 %shard_map.181 = (f32[4,256,1024]{2,1,0:T(8,128)}, bf16[4,256,512]{2,1,0:T(8,128)(2,1)}, bf16[4,256,2048]{2,1,0:T(8,128)(2,1)}) custom-call(bf16[3,256,512]{2,1,0:T(8,128)(2,1)} %get-tuple-element.63.refs_0_, bf16[3,256,512]{2,1,0:T(8,128)(2,1)} %collective-permute-done.3.refs_1_, bf16[3,256,512]{2,1,0:T(8,128)(2,1)} %collective-permute-done.refs_2_, ...), custom_call_target="tpu_custom_call" | custom-call | flops 1000000000 | bytes 20000000 | tf_op jit(solution)/shard_map/pallas_call | solution.py:550
  239.8 75.1 %shard_map.182 = (bf16[4,256,2048]{2,1,0:T(8,128)(2,1)}, bf16[1,256,2048]{2,1,0:T(8,128)(2,1)}, f32[8,512]{1,0:T(8,128)}) custom-call(bf16[4,256,2048]{2,1,0:T(8,128)(2,1)} %get-tuple-element.69.refs_0_, f32[256,512]{1,0:T(8,128)} %get-tuple-element.70.refs_1_, f32[256,512]{1,0:T(8,128)} %constant_dynamic-slice_fusion.2.refs_2_.refs_1_, f32[2,512]{1,0:T(2,128)} %bitcast.124), custom_call_target="tpu_custom_call" | custom-call | flops 100000000 | bytes 100000000 | tf_op jit(solution)/shard_map/pallas_call | solution.py:366
  314.9 13.8 %shard_map.183 = (bf16[4,256,1024]{2,1,0:T(8,128)(2,1)}, bf16[4,256,2048]{2,1,0:T(8,128)(2,1)}) custom-call(bf16[3,256,512]{2,1,0:T(8,128)(2,1)} %get-tuple-element.63.refs_0_, bf16[3,256,512]{2,1,0:T(8,128)(2,1)} %collective-permute-done.3.refs_1_, bf16[3,256,512]{2,1,0:T(8,128)(2,1)} %collective-permute-done.refs_2_, ...), custom_call_target="tpu_custom_call" | custom-call | flops 1000000000 | bytes 20000000 | tf_op jit(solution)/shard_map/pallas_call | solution.py:550
  328.7 7.5 %bitcast_convert_fusion = bf16[2048,1024]{1,0:T(8,128)(2,1)S(1)} fusion(bf16[4,256,2048]{2,1,0:T(8,128)(2,1)} %get-tuple-element.68.refs_8_, bf16[4,256,1024]{2,1,0:T(8,128)(2,1)} %get-tuple-element.79), kind=kOutput, calls=%fused_computation | convolution fusion | flops 4297064448 | bytes 10485760 | tf_op jit(solution)/shard_map/krd,kru->du/dot_general | solution.py:843
  345.7 65.7 %shard_map.184 = (bf16[4,256,2048]{2,1,0:T(8,128)(2,1)}, f32[256,512]{1,0:T(8,128)}, f32[8,512]{1,0:T(8,128)}) custom-call(bf16[4,256,2048]{2,1,0:T(8,128)(2,1)} %get-tuple-element.74.refs_0_, f32[256,512]{1,0:T(8,128)} %constant_dynamic-slice_fusion.2.refs_2_.refs_1_, f32[256,512]{1,0:T(8,128)} %get-tuple-element.75.refs_2_, ...), custom_call_target="tpu_custom_call" | custom-call | flops 100000000 | bytes 100000000 | tf_op jit(solution)/shard_map/pallas_call | solution.py:366
  422.0 12.1 %shard_map.185 = (f32[4,256,384]{2,1,0:T(8,128)}, f32[8,256]{1,0:T(8,128)}, f32[8,128]{1,0:T(8,128)}) custom-call(bf16[4,256,2048]{2,1,0:T(8,128)(2,1)} %get-tuple-element.80.proj_ref, f32[4,256,384]{2,1,0:T(8,128)} %get-tuple-element.55.qkv_ref, f32[8,256]{1,0:T(8,128)} %shard_map.178.stats_ref, f32[2,128]{1,0:T(2,128)} %reshape.57.gain_ref, ...), custom_call_target="tpu_custom_call" | custom-call | flops 1000000000 | bytes 20000000 | tf_op jit(solution)/shard_map/pallas_call | solution.py:550
  434.1 12.8 %shard_map.186.inner_ref = f32[8,256]{1,0:T(8,128)} custom-call(f32[8,256]{1,0:T(8,128)} %get-tuple-element.82.stats_ref), custom_call_target="tpu_custom_call" | custom-call | tf_op jit(solution)/shard_map/pallas_call | solution.py:527
  446.9 3.5 fusion.1
  451.9 3.9 collective-permute-start.13
  455.8 8.3 %shard_map.187 = (bf16[4,256,384]{2,1,0:T(8,128)(2,1)}, bf16[4,256,2048]{2,1,0:T(8,128)(2,1)}) custom-call(f32[4,256,384]{2,1,0:T(8,128)} %get-tuple-element.81.scaled_ref, f32[4,256,384]{2,1,0:T(8,128)} %get-tuple-element.55.qkv_ref, f32[8,256]{1,0:T(8,128)} %shard_map.178.stats_ref, f32[8,256]{1,0:T(8,128)} %shard_map.186.inner_ref, ...), custom_call_target="tpu_custom_call" | custom-call | flops 1000000000 | bytes 20000000 | tf_op jit(solution)/shard_map/pallas_call | solution.py:550
  464.1 4.8 bitcast_convert_fusion.2
  469.9 42.3 %shard_map.188 = (bf16[1,256,2048]{2,1,0:T(8,128)(2,1)}, f32[8,640]{1,0:T(8,128)}) custom-call(bf16[4,256,2048]{2,1,0:T(8,128)(2,1)} %get-tuple-element.85.refs_0_, f32[256,512]{1,0:T(8,128)} %get-tuple-element.86.refs_1_, f32[8,512]{1,0:T(8,128)} %get-tuple-element.87.refs_2_, f32[8,512]{1,0:T(8,128)} %get-tuple-element.88.refs_3_, ...), custom_call_target="tpu_custom_call" | custom-call | flops 100000000 | bytes 100000000 | tf_op jit(solution)/shard_map/pallas_call | solution.py:366
  512.2 2.8 bitcast_convert_fusion.3
  523.5 2.8 collective-permute-start.14
  528.3 28.7 %collective-permute-done.14.refs_1_ = bf16[256,128]{1,0:T(8,128)(2,1)S(1)} collective-permute-done((bf16[256,128]{1,0:T(8,128)(2,1)S(1)}, bf16[256,128]{1,0:T(8,128)(2,1)S(1)}, u32[]{:S(2)}, u32[]{:S(2)}) %collective-permute-start.14) | collective-permute-done | bytes 65568 | tf_op jit(solution)/shard_map/ppermute | solution.py:43
  559.0 14.2 %collective-permute-done.15.refs_2_ = bf16[256,128]{1,0:T(8,128)(2,1)S(1)} collective-permute-done((bf16[256,128]{1,0:T(8,128)(2,1)S(1)}, bf16[256,128]{1,0:T(8,128)(2,1)S(1)}, u32[]{:S(2)}, u32[]{:S(2)}) %collective-permute-start.15) | collective-permute-done | bytes 65568 | tf_op jit(solution)/shard_map/ppermute | solution.py:43
  583.2 3.8 shard_map.191
  587.0 7.6 %copy.38 = f32[256,2,2048]{2,1,0:T(2,128)} copy(f32[256,2,2048]{2,0,1:T(8,128)} %bitcast.110) | data formatting | bytes 8388608
  (115 shorter events, 61.6 us)
Async XLA Ops:
  0.6 156.8 %copy-start = (f32[256,2048]{1,0:T(8,128)S(1)}, f32[256,2048]{1,0:T(8,128)}, u32[]{:S(2)}) copy-start(f32[256,2048]{1,0:T(8,128)} %param.19) | copy-start | bytes 6291460
  69.2 83.4 %collective-permute-start = (bf16[3,256,512]{2,1,0:T(8,128)(2,1)}, bf16[3,256,512]{2,1,0:T(8,128)(2,1)}, u32[]{:S(2)}, u32[]{:S(2)}) collective-permute-start(bf16[3,256,512]{2,1,0:T(8,128)(2,1)} %get-tuple-element.60), channel_id=1, source_target_pairs={{0,8},{8,0},{16,24},{24,16},{1,9},{9,1},{17,25},{25,17},{2,10},{10... | collective-permute-start | bytes 2359304 | tf_op jit(solution)/shard_map/ppermute | solution.py:43
  69.3 83.4 %collective-permute-start.1 = (bf16[3,256,512]{2,1,0:T(8,128)(2,1)}, bf16[3,256,512]{2,1,0:T(8,128)(2,1)}, u32[]{:S(2)}, u32[]{:S(2)}) collective-permute-start(bf16[3,256,512]{2,1,0:T(8,128)(2,1)} %get-tuple-element.61), channel_id=1, source_target_pairs={{0,16},{8,24},{16,0},{24,8},{1,17},{9,25},{17,1},{25,9},{2,18},{10... | collective-permute-start | bytes 2359304 | tf_op jit(solution)/shard_map/ppermute | solution.py:43
  72.2 80.4 %collective-permute-start.2 = (bf16[3,256,512]{2,1,0:T(8,128)(2,1)}, bf16[3,256,512]{2,1,0:T(8,128)(2,1)}, u32[]{:S(2)}, u32[]{:S(2)}) collective-permute-start(bf16[3,256,512]{2,1,0:T(8,128)(2,1)} %get-tuple-element.62), channel_id=1, source_target_pairs={{0,24},{8,16},{16,8},{24,0},{1,25},{9,17},{17,9},{25,1},{2,26},{10... | collective-permute-start | bytes 2359304 | tf_op jit(solution)/shard_map/ppermute | solution.py:43
  152.7 74.1 %collective-permute-start.3 = (bf16[3,256,512]{2,1,0:T(8,128)(2,1)S(1)}, bf16[3,256,512]{2,1,0:T(8,128)(2,1)}, u32[]{:S(2)}, u32[]{:S(2)}) collective-permute-start(bf16[3,256,512]{2,1,0:T(8,128)(2,1)S(1)} %copy-done.5), channel_id=1, source_target_pairs={{0,4},{4,0},{1,5},{5,1},{2,6},{6,2},{3,7},{7,3},{8,12},{12,8},{9,1... | collective-permute-start | bytes 2359304 | tf_op jit(solution)/shard_map/ppermute | solution.py:43
  154.4 72.3 %collective-permute-start.4 = (bf16[3,256,512]{2,1,0:T(8,128)(2,1)}, bf16[3,256,512]{2,1,0:T(8,128)(2,1)}, u32[]{:S(2)}, u32[]{:S(2)}) collective-permute-start(bf16[3,256,512]{2,1,0:T(8,128)(2,1)} %collective-permute-done.refs_2_), channel_id=1, source_target_pairs={{0,4},{4,0},{1,5},{5,1},{2,6},{6,2},{3,7},{7,3},{8,12},{12,8},{9,1... | collective-permute-start | bytes 2359304 | tf_op jit(solution)/shard_map/ppermute | solution.py:43
  154.8 72.0 %collective-permute-start.5 = (bf16[3,256,512]{2,1,0:T(8,128)(2,1)}, bf16[3,256,512]{2,1,0:T(8,128)(2,1)}, u32[]{:S(2)}, u32[]{:S(2)}) collective-permute-start(bf16[3,256,512]{2,1,0:T(8,128)(2,1)} %collective-permute-done.1.refs_4_), channel_id=1, source_target_pairs={{0,4},{4,0},{1,5},{5,1},{2,6},{6,2},{3,7},{7,3},{8,12},{12,8},{9,1... | collective-permute-start | bytes 2359304 | tf_op jit(solution)/shard_map/ppermute | solution.py:43
  156.5 70.3 %collective-permute-start.6 = (bf16[3,256,512]{2,1,0:T(8,128)(2,1)}, bf16[3,256,512]{2,1,0:T(8,128)(2,1)}, u32[]{:S(2)}, u32[]{:S(2)}) collective-permute-start(bf16[3,256,512]{2,1,0:T(8,128)(2,1)} %collective-permute-done.2.refs_6_), channel_id=1, source_target_pairs={{0,4},{4,0},{1,5},{5,1},{2,6},{6,2},{3,7},{7,3},{8,12},{12,8},{9,1... | collective-permute-start | bytes 2359304 | tf_op jit(solution)/shard_map/ppermute | solution.py:43
  339.3 75.6 %collective-permute-start.8 = (bf16[4,256,1024]{2,1,0:T(8,128)(2,1)}, bf16[4,256,1024]{2,1,0:T(8,128)(2,1)}, u32[]{:S(2)}, u32[]{:S(2)}) collective-permute-start(bf16[4,256,1024]{2,1,0:T(8,128)(2,1)} %dynamic-slice_bitcast_fusion), channel_id=1, source_target_pairs={{0,4},{4,0},{1,5},{5,1},{2,6},{6,2},{3,7},{7,3},{8,12},{12,8},{9,1... | collective-permute-start | bytes 6291464 | tf_op jit(solution)/shard_map/ppermute | solution.py:43
  344.4 68.6 %collective-permute-start.7 = (bf16[4,256,512]{2,1,0:T(8,128)(2,1)}, bf16[4,256,512]{2,1,0:T(8,128)(2,1)}, u32[]{:S(2)}, u32[]{:S(2)}) collective-permute-start(bf16[4,256,512]{2,1,0:T(8,128)(2,1)} %dynamic-slice_bitcast_fusion.1), channel_id=1, source_target_pairs={{0,4},{4,0},{1,5},{5,1},{2,6},{6,2},{3,7},{7,3},{8,12},{12,8},{9,1... | collective-permute-start | bytes 3145736 | tf_op jit(solution)/shard_map/ppermute | solution.py:43
  418.5 103.4 %collective-permute-start.20 = (bf16[256,512]{1,0:T(8,128)(2,1)}, bf16[256,512]{1,0:T(8,128)(2,1)S(1)}, u32[]{:S(2)}, u32[]{:S(2)}) collective-permute-start(bf16[256,512]{1,0:T(8,128)(2,1)} %get-tuple-element.122), channel_id=1, source_target_pairs={{0,8},{8,0},{16,24},{24,16},{1,9},{9,1},{17,25},{25,17},{2,10},{10... | collective-permute-start | bytes 786440 | tf_op jit(solution)/shard_map/ppermute | solution.py:43
  419.8 102.9 %collective-permute-start.21 = (bf16[256,512]{1,0:T(8,128)(2,1)}, bf16[256,512]{1,0:T(8,128)(2,1)}, u32[]{:S(2)}, u32[]{:S(2)}) collective-permute-start(bf16[256,512]{1,0:T(8,128)(2,1)} %get-tuple-element.121), channel_id=1, source_target_pairs={{0,16},{8,24},{16,0},{24,8},{1,17},{9,25},{17,1},{25,9},{2,18},{10... | collective-permute-start | bytes 786440 | tf_op jit(solution)/shard_map/ppermute | solution.py:43
  420.1 107.5 %collective-permute-start.22 = (bf16[256,512]{1,0:T(8,128)(2,1)}, bf16[256,512]{1,0:T(8,128)(2,1)}, u32[]{:S(2)}, u32[]{:S(2)}) collective-permute-start(bf16[256,512]{1,0:T(8,128)(2,1)} %get-tuple-element.120), channel_id=1, source_target_pairs={{0,24},{8,16},{16,8},{24,0},{1,25},{9,17},{17,9},{25,1},{2,26},{10... | collective-permute-start | bytes 786440 | tf_op jit(solution)/shard_map/ppermute | solution.py:43
  451.9 66.4 %collective-permute-start.13 = (bf16[4,256,128]{2,1,0:T(8,128)(2,1)}, bf16[4,256,128]{2,1,0:T(8,128)(2,1)}, u32[]{:S(2)}, u32[]{:S(2)}) collective-permute-start(bf16[4,256,128]{2,1,0:T(8,128)(2,1)} %dynamic-slice_bitcast_fusion.11), channel_id=1, source_target_pairs={{0,4},{4,0},{1,5},{5,1},{2,6},{6,2},{3,7},{7,3},{8,12},{12,8},{9,1... | collective-permute-start | bytes 786440 | tf_op jit(solution)/shard_map/ppermute | solution.py:43
  469.9 53.6 %collective-permute-start.9 = (bf16[4,256,384]{2,1,0:T(8,128)(2,1)}, bf16[4,256,384]{2,1,0:T(8,128)(2,1)}, u32[]{:S(2)}, u32[]{:S(2)}) collective-permute-start(bf16[4,256,384]{2,1,0:T(8,128)(2,1)} %dynamic-slice_bitcast_fusion.2), channel_id=1, source_target_pairs={{0,4},{4,0},{1,5},{5,1},{2,6},{6,2},{3,7},{7,3},{8,12},{12,8},{9,1... | collective-permute-start | bytes 2359304 | tf_op jit(solution)/shard_map/ppermute | solution.py:43
  518.3 58.3 %collective-permute-start.17 = (bf16[256,1024]{1,0:T(8,128)(2,1)S(1)}, bf16[256,1024]{1,0:T(8,128)(2,1)S(1)}, u32[]{:S(2)}, u32[]{:S(2)}) collective-permute-start(bf16[256,1024]{1,0:T(8,128)(2,1)S(1)} %get-tuple-element.118), channel_id=1, source_target_pairs={{0,8},{8,0},{16,24},{24,16},{1,9},{9,1},{17,25},{25,17},{2,10},{10... | collective-permute-start | bytes 1572872 | tf_op jit(solution)/shard_map/ppermute | solution.py:43
  521.9 60.5 %collective-permute-start.18 = (bf16[256,1024]{1,0:T(8,128)(2,1)}, bf16[256,1024]{1,0:T(8,128)(2,1)S(1)}, u32[]{:S(2)}, u32[]{:S(2)}) collective-permute-start(bf16[256,1024]{1,0:T(8,128)(2,1)} %get-tuple-element.117), channel_id=1, source_target_pairs={{0,16},{8,24},{16,0},{24,8},{1,17},{9,25},{17,1},{25,9},{2,18},{10... | collective-permute-start | bytes 1572872 | tf_op jit(solution)/shard_map/ppermute | solution.py:43
  522.7 59.8 %collective-permute-start.19 = (bf16[256,1024]{1,0:T(8,128)(2,1)}, bf16[256,1024]{1,0:T(8,128)(2,1)}, u32[]{:S(2)}, u32[]{:S(2)}) collective-permute-start(bf16[256,1024]{1,0:T(8,128)(2,1)} %get-tuple-element.116), channel_id=1, source_target_pairs={{0,24},{8,16},{16,8},{24,0},{1,25},{9,17},{17,9},{25,1},{2,26},{10... | collective-permute-start | bytes 1572872 | tf_op jit(solution)/shard_map/ppermute | solution.py:43
  523.5 33.5 %collective-permute-start.14 = (bf16[256,128]{1,0:T(8,128)(2,1)S(1)}, bf16[256,128]{1,0:T(8,128)(2,1)S(1)}, u32[]{:S(2)}, u32[]{:S(2)}) collective-permute-start(bf16[256,128]{1,0:T(8,128)(2,1)S(1)} %get-tuple-element.130), channel_id=1, source_target_pairs={{0,8},{8,0},{16,24},{24,16},{1,9},{9,1},{17,25},{25,17},{2,10},{10... | collective-permute-start | bytes 196616 | tf_op jit(solution)/shard_map/ppermute | solution.py:43
  527.6 45.6 %collective-permute-start.15 = (bf16[256,128]{1,0:T(8,128)(2,1)S(1)}, bf16[256,128]{1,0:T(8,128)(2,1)S(1)}, u32[]{:S(2)}, u32[]{:S(2)}) collective-permute-start(bf16[256,128]{1,0:T(8,128)(2,1)S(1)} %get-tuple-element.129), channel_id=1, source_target_pairs={{0,16},{8,24},{16,0},{24,8},{1,17},{9,25},{17,1},{25,9},{2,18},{10... | collective-permute-start | bytes 196616 | tf_op jit(solution)/shard_map/ppermute | solution.py:43
  557.0 18.9 %collective-permute-start.16 = (bf16[256,128]{1,0:T(8,128)(2,1)S(1)}, bf16[256,128]{1,0:T(8,128)(2,1)S(1)}, u32[]{:S(2)}, u32[]{:S(2)}) collective-permute-start(bf16[256,128]{1,0:T(8,128)(2,1)S(1)} %get-tuple-element.128), channel_id=1, source_target_pairs={{0,24},{8,16},{16,8},{24,0},{1,25},{9,17},{17,9},{25,1},{2,26},{10... | collective-permute-start | bytes 196616 | tf_op jit(solution)/shard_map/ppermute | solution.py:43
  573.2 21.5 %collective-permute-start.10 = (bf16[256,384]{1,0:T(8,128)(2,1)S(1)}, bf16[256,384]{1,0:T(8,128)(2,1)S(1)}, u32[]{:S(2)}, u32[]{:S(2)}) collective-permute-start(bf16[256,384]{1,0:T(8,128)(2,1)S(1)} %get-tuple-element.126), channel_id=1, source_target_pairs={{0,8},{8,0},{16,24},{24,16},{1,9},{9,1},{17,25},{25,17},{2,10},{10... | collective-permute-start | bytes 589832 | tf_op jit(solution)/shard_map/ppermute | solution.py:43
  575.9 18.7 %collective-permute-start.11 = (bf16[256,384]{1,0:T(8,128)(2,1)S(1)}, bf16[256,384]{1,0:T(8,128)(2,1)S(1)}, u32[]{:S(2)}, u32[]{:S(2)}) collective-permute-start(bf16[256,384]{1,0:T(8,128)(2,1)S(1)} %get-tuple-element.125), channel_id=1, source_target_pairs={{0,16},{8,24},{16,0},{24,8},{1,17},{9,25},{17,1},{25,9},{2,18},{10... | collective-permute-start | bytes 589832 | tf_op jit(solution)/shard_map/ppermute | solution.py:43
  576.6 18.0 %collective-permute-start.12 = (bf16[256,384]{1,0:T(8,128)(2,1)S(1)}, bf16[256,384]{1,0:T(8,128)(2,1)S(1)}, u32[]{:S(2)}, u32[]{:S(2)}) collective-permute-start(bf16[256,384]{1,0:T(8,128)(2,1)S(1)} %get-tuple-element.124), channel_id=1, source_target_pairs={{0,24},{8,16},{16,8},{24,0},{1,25},{9,17},{17,9},{25,1},{2,26},{10... | collective-permute-start | bytes 589832 | tf_op jit(solution)/shard_map/ppermute | solution.py:43
  (19 other events, 240.5 us)

commit v3 on v2

--- a/solution.py
+++ b/solution.py
@@ -108,12 +108,59 @@
     )
 
 
+def dot(left, right):
+    return jnp.dot(left, right, preferred_element_type=f32)
+
+
+def dot_t(left, right):
+    return lax.dot_general(left, right, (((1,), (1,)), ((), ())), preferred_element_type=f32)
+
+
+def t_dot(left, right):
+    return lax.dot_general(left, right, (((0,), (0,)), ((), ())), preferred_element_type=f32)
+
+
+def rotate(operand):
+    half = HD // 2
+    return jnp.concatenate([-operand[:, half:], operand[:, :half]], axis=1)
+
+
+def rotate_back(operand):
+    half = HD // 2
+    return jnp.concatenate([operand[:, half:], -operand[:, :half]], axis=1)
+
+
+def attention(k, qkv, stats, gain_ref, cos_ref, sin_ref):
+    stats = stats / HQ
+    q_inv = lax.rsqrt(to_column(stats, 2 * k) + epsilon)
+    k_inv = lax.rsqrt(to_column(stats, 2 * k + 1) + epsilon)
+    queries, key_rows = qkv[:, :HD], qkv[:, HD : 2 * HD]
+    values = qkv[:, 2 * HD :].astype(bf16)
+    cos_table, sine_table = cos_ref[...], sin_ref[...]
+    q_normed = queries * q_inv * gain_ref[0:1]
+    k_normed = key_rows * k_inv * gain_ref[1:2]
+    q_rot = (q_normed * cos_table + rotate(q_normed) * sine_table).astype(bf16)
+    k_rot = (k_normed * cos_table + rotate(k_normed) * sine_table).astype(bf16)
+    scores = dot_t(q_rot, k_rot) * HD ** (-0.5)
+    ahead = lax.broadcasted_iota(jnp.int32, scores.shape, 1) > lax.broadcasted_iota(
+        jnp.int32, scores.shape, 0
+    )
+    scores = jnp.where(ahead, -1e30, scores)
+    shifted = jnp.exp(scores - jnp.max(scores, axis=1, keepdims=True))
+    probs = shifted / jnp.sum(shifted, axis=1, keepdims=True)
+    return queries, key_rows, values, q_inv, k_inv, q_rot, k_rot, probs
+
+
 def reduce_kernel(na, nb, mode, *refs):
-    n_in = {"attn": 3, "mlp": 4, "back": 5, "tok": 5}[mode]
-    n_out = {"attn": 4, "mlp": 3, "back": 3, "tok": 2}[mode]
-    ins, outs, scratch = refs[:n_in], refs[n_in : n_in + n_out], refs[n_in + n_out :]
+    n_in = {"mlp": 4, "back": 5, "tok": 5}[mode]
+    n_out = {"mlp": 3, "back": 3, "tok": 2}[mode]
+    links = Links(*refs[-2:])
+    reduce(na, nb, mode, links, refs[:n_in], refs[n_in : n_in + n_out], refs[n_in + n_out : -2])
+    links.finish()
+
+
+def reduce(na, nb, mode, links, ins, outs, scratch, hooks=None):
     from_q, half_sum, from_p, to_a, from_a, total, parts, cols, stat, *scratch = scratch
-    send_sem, recv_sem = scratch[-2:]
     part_ref, out = ins[0], outs[0]
     a, b = lax.axis_index("a"), lax.axis_index("b")
     p, q = lax.axis_index("p"), lax.axis_index("q")
@@ -129,8 +176,9 @@
         own_sums[0:1, mine] = jnp.sum(ins[2][...], axis=0, keepdims=True)
         own_sums[1:2, mine] = jnp.sum(ins[3][...], axis=0, keepdims=True)
         peers += [{"b": across(b, j)} for j in range(1, nb)]
-    greet(peers)
-    links = Links(send_sem, recv_sem)
+    if hooks is None:
+        greet(peers)
+    hooks = hooks or {}
     halves = [slice(h * count, (h + 1) * count) for h in range(HALVES)]
     lead = list(range(2, na)) + [1, 0]
     give, keep = span(1 - q, half), span(q, half)
@@ -183,6 +231,7 @@
 
     for h in range(HALVES):
         send_a(h)
+    hooks.get("scattered", lambda: None)()
     if mode == "tok":
         sums_q.wait_recv()
         sums_a = [
@@ -307,6 +356,7 @@
         sums_b = [
             links.send(b_sums.at[0], b_sums.at[j], {"b": across(b, j)}) for j in range(1, nb)
         ]
+    hooks.get("spread", lambda: None)()
     for h, at_h in enumerate(halves):
         for k in blocks:
             if k:
@@ -334,7 +384,21 @@
         sums_ref[...] = held
     for copy in spread_q.values():
         copy.wait_recv()
-    links.finish()
+
+
+def reduce_scratch(na, rows, width):
+    quarter = width // 4
+    return [
+        pltpu.VMEM((na, rows, width // 2), bf16),
+        pltpu.VMEM((na, rows, width // 2), bf16),
+        pltpu.VMEM((na, rows, quarter), bf16),
+        pltpu.VMEM((na - 1, rows, quarter), bf16),
+        pltpu.VMEM((na - 1, rows, quarter), bf16),
+        pltpu.VMEM((rows, quarter), f32),
+        pltpu.VMEM((2, rows, 128), f32),
+        pltpu.VMEM((2, rows, 128), f32),
+        pltpu.VMEM((HALVES, 4, 8, rows // HALVES), f32),
+    ]
 
 
 def reduce_call(mode, nb, part, *operands):
@@ -346,7 +410,6 @@
     share = shape((rows, quarter), f32)
     sums = shape((8, quarter), f32)
     outs = {
-        "attn": (full, share, shape((rows, 128), f32), share),
         "mlp": (full, one, sums),
         "back": (full, share, sums),
         "tok": (one, shape((8, quarter + HD), f32)),
@@ -368,21 +431,11 @@
         out_shape=outs,
         in_specs=[vmem] * (1 + len(operands)),
         out_specs=(vmem,) * len(outs),
-        scratch_shapes=[
-            pltpu.VMEM((na, rows, width // 2), bf16),
-            pltpu.VMEM((na, rows, width // 2), bf16),
-            pltpu.VMEM((na, rows, quarter), bf16),
-            pltpu.VMEM((na - 1, rows, quarter), bf16),
-            pltpu.VMEM((na - 1, rows, quarter), bf16),
-            pltpu.VMEM((rows, quarter), f32),
-            pltpu.VMEM((2, rows, 128), f32),
-            pltpu.VMEM((2, rows, 128), f32),
-            pltpu.VMEM((HALVES, 4, 8, rows // HALVES), f32),
-        ]
+        scratch_shapes=reduce_scratch(na, rows, width)
         + extra
         + [pltpu.SemaphoreType.DMA((copies,)), pltpu.SemaphoreType.DMA((copies,))],
         compiler_params=pltpu.CompilerParams(
-            collective_id={"attn": 1, "mlp": 2, "back": 3, "tok": 4}[mode],
+            collective_id={"mlp": 2, "back": 3, "tok": 4}[mode],
             has_side_effects=True,
             vmem_limit_bytes=VMEM_LIMIT,
         ),
@@ -390,13 +443,17 @@
     )(part, *operands)
 
 
-def start_kernel(na, nb, *refs):
-    tok_ref, qkv_ref, wout_ref, gu_ref, down_ref = refs[:5]
-    gain_refs, (x_ref, w_ref, gains_ref) = refs[5:9], refs[9:12]
-    piece_refs, (own_gains, local_sem, send_sem, recv_sem) = refs[12 : 12 + na], refs[12 + na :]
+def enter_kernel(na, nb, *refs):
+    tok_ref, qkv_w_ref, wout_ref, gu_ref, down_ref, cos_ref, sin_ref = refs[:7]
+    gain_refs = refs[7:11]
+    x_ref, w_ref, mlp_w_ref, width_gain_ref, head_gain_ref, qkv_ref, stats_ref, att_ref = refs[11:19]
+    out, proj_ref, inv_ref, res_ref = refs[19:23]
+    own_gains, gains_ref, piece_ref, part_ref, held, stats_a = refs[23:29]
+    scratch, (local_sem, send_sem, recv_sem) = refs[29:-3], refs[-3:]
     a, b, p, q = (lax.axis_index(axis) for axis in ("a", "b", "p", "q"))
     rows = wout_ref.shape[0]
     quarter = tok_ref.shape[1]
+    units = down_ref.shape[1] // na
     own_gains[...] = jnp.zeros_like(own_gains)
     for i, ref in enumerate(gain_refs):
         own_gains[i : i + 1, : ref.shape[1]] = ref[...].astype(f32)
@@ -407,16 +464,17 @@
         + [{"b": across(b, j)} for j in range(1, nb)]
     )
     links = Links(send_sem, recv_sem)
+    mine, pair = span(2 * q + p, quarter), span(q, 2 * quarter)
+    place = span(a * nb + b, rows)
+
     gains_a = [
         links.send(own_gains, gains_ref.at[a, b], {"a": across(a, k)}) for k in range(1, na)
     ]
-    mine, pair = span(2 * q + p, quarter), span(q, 2 * quarter)
-    place = span(a * nb + b, rows)
     locals_ = [pltpu.make_async_copy(tok_ref, x_ref.at[0, :, mine], local_sem.at[0])]
     arrive, first = {}, {}
     for k in list(range(1, na)) + [0]:
         block = span(across(a, k), HD)
-        sources = [qkv_ref.at[c, :, block] for c in range(3)] + [wout_ref.at[:, block]]
+        sources = [qkv_w_ref.at[c, :, block] for c in range(3)] + [wout_ref.at[:, block]]
         for c, source in enumerate(sources):
             target = w_ref.at[place, c * HD : (c + 1) * HD]
             if k:
@@ -439,18 +497,37 @@
         second[k] = links.send(at, at, {"p": 1 - p})
 
     forward(0)
-    units = down_ref.shape[1] // na
+
     for k in range(na):
         block = span(across(a, k), units)
 
         def cut(i, carry, k=k, block=block):
             at = pl.ds(pl.multiple_of(i * TILE, TILE), TILE)
-            piece_refs[k][0, at] = gu_ref[at, 0, block]
-            piece_refs[k][1, at] = gu_ref[at, 1, block]
-            piece_refs[k][2, at] = down_ref[at, block]
+            cuts = (gu_ref[at, 0, block], gu_ref[at, 1, block], down_ref[at, block])
+            for c in range(3):
+                if k:
+                    piece_ref[k - 1, c, at] = cuts[c]
+                else:
+                    to = pl.ds(pl.multiple_of((a * nb + b) * rows + i * TILE, TILE), TILE)
+                    mlp_w_ref[to, c * units : (c + 1) * units] = cuts[c]
             return carry
 
         lax.fori_loop(0, rows // TILE, cut, 0)
+    mlp_copies, mlp_ends = {}, []
+
+    def queue(c):
+        for k in list(range(2, na)) + [1]:
+            target = mlp_w_ref.at[place, c * units : (c + 1) * units]
+            mlp_copies[k, c] = links.send(piece_ref.at[k - 1, c], target, {"a": across(a, k)})
+
+    def relay(c, k):
+        if k:
+            mlp_copies[k, c].wait_recv()
+        at = mlp_w_ref.at[span(across(a, k) * nb + b, rows), c * units : (c + 1) * units]
+        for j in range(1, nb):
+            mlp_ends.append(links.send(at, at, {"b": across(b, j)}))
+
+    queue(0)
     for copy in gains_a:
         copy.wait_recv()
     at = gains_ref.at[:, b]
@@ -461,34 +538,110 @@
             arrive[k, c].wait_recv()
         first[k].wait_recv()
         forward(k)
+    for c in range(3):
+        relay(c, 0)
     for k in range(na):
         second[k].wait_recv()
         at = x_ref.at[k, :, pair]
         ends.append(links.send(at, at, {"q": 1 - q}))
     for copy in ends:
         copy.wait_recv()
+
+    n_d, n_h = gain_refs[0].shape[1], gain_refs[2].shape[1]
+    width_gain_ref[...] = jnp.zeros_like(width_gain_ref)
+    head_gain_ref[...] = jnp.zeros_like(head_gain_ref)
+    for i in range(2):
+        width_gain_ref[i : i + 1] = jnp.concatenate(
+            [gains_ref[2 * q + p, j, i : i + 1, :n_d] for j in range(nb)], axis=1
+        )
+        head_gain_ref[i : i + 1] = jnp.concatenate(
+            [gains_ref[a, j, i + 2 : i + 3, :n_h] for j in range(nb)], axis=1
+        )
+
+    held[0] = jnp.zeros_like(held[0])
+
+    def project(k, carry):
+        proj = dot(x_ref[k], w_ref[:, : 3 * HD])
+        qkv_ref[k] = proj
+        queries, key_rows = proj[:, :HD], proj[:, HD : 2 * HD]
+        held[0] += to_row(queries * queries, 2 * k) + to_row(key_rows * key_rows, 2 * k + 1)
+        return carry
+
+    lax.fori_loop(0, na, project, 0)
+    add_over_heads(links, na, a, p, q, held, stats_a, stats_ref, lambda: queue(1))
+    for k in range(1, na):
+        relay(0, k)
+
+    def attend(k, carry):
+        values, probs = (
+            attention(k, qkv_ref[k], stats_ref[...], head_gain_ref, cos_ref, sin_ref)[i] for i in (2, 7)
+        )
+        attended = dot(probs.astype(bf16), values).astype(bf16)
+        att_ref[k] = attended
+        part_ref[k] = dot_t(attended, w_ref[:, 3 * HD :]).astype(bf16)
+        return carry
+
+    lax.fori_loop(0, na, attend, 0)
+
+    def scattered():
+        for k in range(1, na):
+            relay(1, k)
+
+    reduce(
+        na,
+        nb,
+        "attn",
+        links,
+        (part_ref, tok_ref, width_gain_ref),
+        (out, proj_ref, inv_ref, res_ref),
+        scratch,
+        {"scattered": scattered, "spread": lambda: queue(2)},
+    )
+    for k in range(1, na):
+        relay(2, k)
+    for copy in mlp_ends:
+        copy.wait_recv()
     links.finish()
 
 
-def start_call(na, nb, tok_mine, qkv, w_out, gu, down, gains):
+def enter_call(na, nb, tok_mine, qkv, w_out, gu, down, cos_table, sine_table, gains):
     rows, quarter = tok_mine.shape
     width = 4 * quarter
     w_rows, units = down.shape[0], down.shape[1] // na
     lanes = max(128, gains[0].shape[1])
-    copies = (na - 1) * 6 + na * (nb - 1) + (nb - 1) + 2 * na
     vmem = pl.BlockSpec(memory_space=pltpu.VMEM)
+    shape = jax.ShapeDtypeStruct
+    full = shape((na, rows, width), bf16)
     outs = [
-        jax.ShapeDtypeStruct((na, rows, width), bf16),
-        jax.ShapeDtypeStruct((width, 4 * HD), bf16),
-        jax.ShapeDtypeStruct((na, nb, 8, lanes), f32),
-    ] + [jax.ShapeDtypeStruct((3, w_rows, units), bf16)] * na
-    x_all, w_attn, gains_all, *pieces = pl.pallas_call(
-        functools.partial(start_kernel, na, nb),
+        full,
+        shape((width, 4 * HD), bf16),
+        shape((width, 3 * units), bf16),
+        shape((8, quarter), f32),
+        shape((8, HD), f32),
+        shape((na, rows, 3 * HD), f32),
+        shape((8, rows), f32),
+        shape((na, rows, HD), bf16),
+        full,
+        shape((rows, quarter), f32),
+        shape((rows, 128), f32),
+        shape((rows, quarter), f32),
+    ]
+    copies = 90 + 16 * nb
+    return pl.pallas_call(
+        functools.partial(enter_kernel, na, nb),
         out_shape=tuple(outs),
-        in_specs=[vmem] * 9,
+        in_specs=[vmem] * 11,
         out_specs=(vmem,) * len(outs),
         scratch_shapes=[
             pltpu.VMEM((8, lanes), f32),
+            pltpu.VMEM((na, nb, 8, lanes), f32),
+            pltpu.VMEM((na - 1, 3, w_rows, units), bf16),
+            pltpu.VMEM((na, rows, width), bf16),
+            pltpu.VMEM((5, 8, rows), f32),
+            pltpu.VMEM((na - 1, 8, rows), f32),
+        ]
+        + reduce_scratch(na, rows, width)
+        + [
             pltpu.SemaphoreType.DMA((5,)),
             pltpu.SemaphoreType.DMA((copies,)),
             pltpu.SemaphoreType.DMA((copies,)),
@@ -496,30 +649,36 @@
         compiler_params=pltpu.CompilerParams(
             collective_id=5, has_side_effects=True, vmem_limit_bytes=VMEM_LIMIT
         ),
-        name="start",
-    )(tok_mine, qkv, w_out, gu, down, *gains)
-    return x_all, w_attn, gains_all, pieces
-
-
-def stats_kernel(na, stats_ref, out_ref, held, from_a, send_sem, recv_sem):
-    a, p, q = lax.axis_index("a"), lax.axis_index("p"), lax.axis_index("q")
-    greet([{"q": 1 - q}, {"p": 1 - p}] + [{"a": across(a, k)} for k in range(1, na)])
-    links = Links(send_sem, recv_sem)
-    links.send(stats_ref, held.at[0], {"p": 1 - p}).wait_recv()
-    held[1] = stats_ref[...] + held[0]
-    links.send(held.at[1], held.at[2], {"q": 1 - q}).wait_recv()
-    held[3] = held[1] + held[2]
-    copies = [links.send(held.at[3], from_a.at[k - 1], {"a": across(a, k)}) for k in range(1, na)]
+        name="enter",
+    )(tok_mine, qkv, w_out, gu, down, cos_table, sine_table, *gains)
+
+
+def add_over_heads(links, na, a, p, q, held, from_a, out_ref, sent=None):
+    links.send(held.at[0], held.at[1], {"p": 1 - p}).wait_recv()
+    held[2] = held[0] + held[1]
+    links.send(held.at[2], held.at[3], {"q": 1 - q}).wait_recv()
+    held[4] = held[2] + held[3]
+    copies = [links.send(held.at[4], from_a.at[k - 1], {"a": across(a, k)}) for k in range(1, na)]
+    if sent is not None:
+        sent()
     for copy in copies:
         copy.wait_recv()
     for k in range(na):
         for i in range(2):
             at = 2 * k + i
-            total = held[3, at : at + 1]
+            total = held[4, at : at + 1]
             for j in range(1, na):
                 other = 2 * (k ^ j) + i
                 total = total + from_a[j - 1, other : other + 1]
             out_ref[at : at + 1] = total
+
+
+def stats_kernel(na, stats_ref, out_ref, held, from_a, send_sem, recv_sem):
+    a, p, q = lax.axis_index("a"), lax.axis_index("p"), lax.axis_index("q")
+    greet([{"q": 1 - q}, {"p": 1 - p}] + [{"a": across(a, k)} for k in range(1, na)])
+    links = Links(send_sem, recv_sem)
+    held[0] = stats_ref[...]
+    add_over_heads(links, na, a, p, q, held, from_a, out_ref)
     links.finish()
 
 
@@ -530,7 +689,7 @@
         in_specs=[pl.BlockSpec(memory_space=pltpu.VMEM)],
         out_specs=pl.BlockSpec(memory_space=pltpu.VMEM),
         scratch_shapes=[
-            pltpu.VMEM((4,) + stats.shape, f32),
+            pltpu.VMEM((5,) + stats.shape, f32),
             pltpu.VMEM((na - 1,) + stats.shape, f32),
             pltpu.SemaphoreType.DMA((na + 1,)),
             pltpu.SemaphoreType.DMA((na + 1,)),
@@ -561,18 +720,6 @@
     )(*[array for array, _ in operands])
 
 
-def dot(left, right):
-    return jnp.dot(left, right, preferred_element_type=f32)
-
-
-def dot_t(left, right):
-    return lax.dot_general(left, right, (((1,), (1,)), ((), ())), preferred_element_type=f32)
-
-
-def t_dot(left, right):
-    return lax.dot_general(left, right, (((0,), (0,)), ((), ())), preferred_element_type=f32)
-
-
 def add_stats(stats_ref, first, second):
     k = pl.program_id(0)
 
@@ -581,52 +728,6 @@
         stats_ref[...] = jnp.zeros_like(stats_ref)
 
     stats_ref[...] += to_row(first, 2 * k) + to_row(second, 2 * k + 1)
-
-
-def qkv_kernel(x_ref, w_ref, qkv_ref, stats_ref):
-    out = dot(x_ref[0], w_ref[:, : 3 * HD])
-    qkv_ref[0] = out
-    queries, key_rows = out[:, :HD], out[:, HD : 2 * HD]
-    add_stats(stats_ref, queries * queries, key_rows * key_rows)
-
-
-def rotate(operand):
-    half = HD // 2
-    return jnp.concatenate([-operand[:, half:], operand[:, :half]], axis=1)
-
-
-def rotate_back(operand):
-    half = HD // 2
-    return jnp.concatenate([operand[:, half:], -operand[:, :half]], axis=1)
-
-
-def attention(qkv_ref, stats_ref, gain_ref, cos_ref, sin_ref):
-    k = pl.program_id(0)
-    stats = stats_ref[...] / HQ
-    q_inv = lax.rsqrt(to_column(stats, 2 * k) + epsilon)
-    k_inv = lax.rsqrt(to_column(stats, 2 * k + 1) + epsilon)
-    queries, key_rows = qkv_ref[0, :, :HD], qkv_ref[0, :, HD : 2 * HD]
-    values = qkv_ref[0, :, 2 * HD :].astype(bf16)
-    cos_table, sine_table = cos_ref[...], sin_ref[...]
-    q_normed = queries * q_inv * gain_ref[0:1]
-    k_normed = key_rows * k_inv * gain_ref[1:2]
-    q_rot = (q_normed * cos_table + rotate(q_normed) * sine_table).astype(bf16)
-    k_rot = (k_normed * cos_table + rotate(k_normed) * sine_table).astype(bf16)
-    scores = dot_t(q_rot, k_rot) * HD ** (-0.5)
-    ahead = lax.broadcasted_iota(jnp.int32, scores.shape, 1) > lax.broadcasted_iota(
-        jnp.int32, scores.shape, 0
-    )
-    scores = jnp.where(ahead, -1e30, scores)
-    shifted = jnp.exp(scores - jnp.max(scores, axis=1, keepdims=True))
-    probs = shifted / jnp.sum(shifted, axis=1, keepdims=True)
-    return queries, key_rows, values, q_inv, k_inv, q_rot, k_rot, probs
-
-
-def attend_kernel(qkv_ref, stats_ref, gain_ref, cos_ref, sin_ref, w_ref, att_ref, part_ref):
-    values, probs = (attention(qkv_ref, stats_ref, gain_ref, cos_ref, sin_ref)[i] for i in (2, 7))
-    attended = dot(probs.astype(bf16), values).astype(bf16)
-    att_ref[0] = attended
-    part_ref[0] = dot_t(attended, w_ref[:, 3 * HD :]).astype(bf16)
 
 
 def attend_back_kernel(
@@ -634,7 +735,7 @@
 ):
     k = pl.program_id(0)
     queries, key_rows, values, q_inv, k_inv, q_rot, k_rot, probs = attention(
-        qkv_ref, stats_ref, gain_ref, cos_ref, sin_ref
+        k, qkv_ref[0], stats_ref[...], gain_ref, cos_ref, sin_ref
     )
     cos_table, sine_table = cos_ref[...], sin_ref[...]
     grad_att = dot(proj_ref[0], w_ref[:, 3 * HD :]).astype(bf16)
@@ -673,33 +774,7 @@
     part_ref[0] = dot_t(grad_ref[0], w_ref[:, : 3 * HD]).astype(bf16)
 
 
-def load_weights(na, nb, pieces, w_ref, sem):
-    a, b = lax.axis_index("a"), lax.axis_index("b")
-
-    @pl.when(pl.program_id(0) == 0)
-    def _():
-        rows, units = pieces[0].shape[1:]
-        copies = []
-        for k in range(na):
-            for j in range(nb):
-                place = span(across(a, k) * nb + across(b, j), rows)
-                for c in range(3):
-                    copies.append(
-                        pltpu.make_async_copy(
-                            pieces[k * nb + j].at[c],
-                            w_ref.at[place, c * units : (c + 1) * units],
-                            sem.at[len(copies)],
-                        )
-                    )
-        for copy in copies:
-            copy.start()
-        for copy in copies:
-            copy.wait()
-
-
-def mlp_kernel(na, nb, *refs):
-    pieces, (x_ref, gu_ref, hidden_ref, part_ref, w_ref, sem) = refs[: na * nb], refs[na * nb :]
-    load_weights(na, nb, pieces, w_ref, sem)
+def mlp_kernel(x_ref, w_ref, gu_ref, hidden_ref, part_ref):
     units = hidden_ref.shape[2]
     gate_up = dot(x_ref[0], w_ref[:, : 2 * units])
     gu_ref[0] = gate_up
@@ -709,9 +784,7 @@
     part_ref[0] = dot_t(hidden, w_ref[:, 2 * units :]).astype(bf16)
 
 
-def mlp_back_kernel(na, nb, *refs):
-    pieces, (grad_ref, gu_ref, out_ref, part_ref, w_ref, sem) = refs[: na * nb], refs[na * nb :]
-    load_weights(na, nb, pieces, w_ref, sem)
+def mlp_back_kernel(grad_ref, gu_ref, w_ref, out_ref, part_ref):
     units = gu_ref.shape[2] // 2
     grad_hidden = dot(grad_ref[0], w_ref[:, 2 * units :])
     gate, up = gu_ref[0, :, :units], gu_ref[0, :, units:]
@@ -780,7 +853,21 @@
         return lax.dynamic_slice_in_dim(operand, share * quarter, quarter, 1)
 
     tok_mine, grad_mine = quarter_of(tokens), quarter_of(out_grad)
-    x_all, w_attn, gains, cuts = start_call(
+    cos_table, sine_table = rope_tables(SEQ_LEN, HD)
+    (
+        x_all,
+        w_attn,
+        w_mlp,
+        width_gain,
+        head_gain,
+        qkv,
+        stats,
+        attended,
+        res_all,
+        proj_mine,
+        inv_mine,
+        res_mine,
+    ) = enter_call(
         na,
         nb,
         tok_mine,
@@ -788,55 +875,25 @@
         out_weight,
         gu_weight,
         down_weight,
+        cos_table,
+        sine_table,
         [gain[None] for gain in (attn_gain, ffn_gain, q_gain, k_gain)],
     )
     n_d, n_h = attn_gain.shape[0], q_gain.shape[0]
-    width_gain = pick(gains, share, 0)[:, :2, :n_d].transpose(1, 0, 2).reshape(2, quarter)
-    head_gain = pick(gains, a, 0)[:, 2:4, :n_h].transpose(1, 0, 2).reshape(2, HD)
-    cos_table, sine_table = rope_tables(SEQ_LEN, HD)
-
-    arrived = [cuts[k] if k == 0 else swap(cuts[k], "a", k) for k in range(na)]
-
-    qkv, stats = local_call(
-        qkv_kernel,
-        na,
-        [(x_all, "row"), (w_attn, "all")],
-        [((na, rows, 3 * HD), f32, "row"), ((8, rows), f32, "all")],
-    )
-    stats = stats_call(na, stats, 6)
     tables = [(stats, "all"), (head_gain, "all"), (cos_table, "all"), (sine_table, "all")]
     full = (na, rows, width)
-    attended, part = local_call(
-        attend_kernel,
+    gate_up, hidden, part = local_call(
+        mlp_kernel,
         na,
-        [(qkv, "row")] + tables + [(w_attn, "all")],
-        [((na, rows, HD), bf16, "row"), (full, bf16, "row")],
-    )
-    part, arrived = lax.optimization_barrier((part, arrived))
-    pieces = []
-    for piece in arrived:
-        pieces += [piece] + [swap(piece, "b", j) for j in range(1, nb)]
-    res_all, proj_mine, inv_mine, res_mine = reduce_call("attn", nb, part, tok_mine, width_gain)
-
-    mlp_scratch = [
-        pltpu.VMEM((width, 3 * units), bf16),
-        pltpu.SemaphoreType.DMA((3 * na * nb,)),
-    ]
-    far = [(piece, "far") for piece in pieces]
-    gate_up, hidden, part = local_call(
-        functools.partial(mlp_kernel, na, nb),
-        na,
-        far + [(res_all, "row")],
+        [(res_all, "row"), (w_mlp, "all")],
         [((na, rows, 2 * units), f32, "row"), ((na, rows, units), bf16, "row"), (full, bf16, "row")],
-        mlp_scratch,
     )
     grad_mlp, block_rows, ffn_sums = reduce_call("mlp", nb, part, res_mine, grad_mine, width_gain)
     grad_gu, part = local_call(
-        functools.partial(mlp_back_kernel, na, nb),
+        mlp_back_kernel,
         na,
-        far + [(grad_mlp, "row"), (gate_up, "row")],
+        [(grad_mlp, "row"), (gate_up, "row"), (w_mlp, "all")],
         [((na, rows, 2 * units), bf16, "row"), (full, bf16, "row")],
-        mlp_scratch,
     )
 
     def weight_grad(left, right):

time: 603 us -> 574 us (0.952)
  Pallas kernels: 464 us -> 445 us
  starting transfers between devices: 30.4 us -> 19.4 us
    pallas_call x1, Pallas kernels: 64.3 us -> 194 us  [enter_call(): pl.pallas_call(functools.partial(enter_kernel, na, nb), out_shape=tuple(o...]
    pallas_call x4 -> x3, Pallas kernels: 252 us -> 183 us  [reduce_call(): pl.pallas_call(functools.partial(reduce_kernel, na, nb, mode), out_shape=...]
    pallas_call x2 -> x1, Pallas kernels: 73.1 us -> 12.8 us  [stats_call(): pl.pallas_call(functools.partial(stats_kernel, na), out_shape=jax.ShapeDt...]
    pallas_call x6 -> x4, Pallas kernels: 64 us -> 44.7 us  [local_call(): pl.pallas_call(kernel, grid=(na,), out_shape=tuple((jax.ShapeDtypeStruct(...]
    ppermute x23 -> x16, starting transfers between devices: 30.4 us -> 19.4 us  [swap(): return lax.ppermute(operand, axis, [(i, i ^ k) for i in range(n)])]
    ppermute x23 -> x16, waiting for transfers between devices: 42.9 us -> 43.5 us  [swap(): return lax.ppermute(operand, axis, [(i, i ^ k) for i in range(n)])]
  transfers between devices with their start and end apart: 23 -> 16, of which waited for: 2 -> 2; matrix products, arithmetic and copies ran while one was open for 7% -> 6% of each run, Pallas kernels for 49% -> 27%
where the time goes in v3:
time: 574 us; the launch traced here: 569 us
  Pallas kernels  445 us (78%)
  waiting for transfers between devices  43.5 us (8%)
  local copies, waits for them, and re-layouts  27.2 us (5%)
  matrix products  20.3 us (4%)
  starting transfers between devices  19.4 us (3%)
  other arithmetic  12.6 us (2%)
    pallas_call x1, Pallas kernels, enter_call(): pl.pallas_call(functools.partial(enter_kernel, na, nb), out_shape=tuple(o...  194 us
    pallas_call x3, Pallas kernels, reduce_call(): pl.pallas_call(functools.partial(reduce_kernel, na, nb, mode), out_shape=...  183 us
    pallas_call x4, Pallas kernels, local_call(): pl.pallas_call(kernel, grid=(na,), out_shape=tuple((jax.ShapeDtypeStruct(...  44.7 us
    ppermute x16, waiting for transfers between devices, swap(): return lax.ppermute(operand, axis, [(i, i ^ k) for i in range(n)])  43.5 us
    dot_general x4, matrix products, weight_grad(): out = jnp.einsum('krd,kru->du', left, right, preferred_element_type=f32)  20.3 us
    ppermute x16, starting transfers between devices, swap(): return lax.ppermute(operand, axis, [(i, i ^ k) for i in range(n)])  19.4 us
    pallas_call x1, Pallas kernels, stats_call(): pl.pallas_call(functools.partial(stats_kernel, na), out_shape=jax.ShapeDt...  12.8 us
  transfers between devices with their start and end apart: 16, of which 2 were waited for; matrix products, arithmetic and copies ran while one was open for 6% of the time, Pallas kernels for 27%

profile of v3, /device:TPU:8, one launch (start us, length us, event | category | flops | bytes accessed | tf_op | source)
XLA Modules:
  0.0 569.1 jit_solution(6393643046183319536)
XLA Ops:
  7.1 193.7 %enter.1 = (bf16[4,256,2048]{2,1,0:T(8,128)(2,1)}, bf16[2048,512]{1,0:T(8,128)(2,1)}, bf16[2048,1536]{1,0:T(8,128)(2,1)}, f32[8,512]{1,0:T(8,128)}, f32[8,128]{1...) custom-call(bf16[256,512]{1,0:T(8,128)(2,1)} %constant_dynamic-slice, ...), custom_call_target="tpu_custom_call" | custom-call | tf_op jit(solution)/shard_map/enter/pallas_call | solution.py:630
  200.8 11.7 %shard_map.177 = (f32[4,256,1024]{2,1,0:T(8,128)}, bf16[4,256,512]{2,1,0:T(8,128)(2,1)}, bf16[4,256,2048]{2,1,0:T(8,128)(2,1)}) custom-call(bf16[4,256,2048]{2,1,0:T(8,128)(2,1)} %get-tuple-element.45.x_ref, bf16[2048,1536]{1,0:T(8,128)(2,1)} %get-tuple-element.46.w_ref), custom_call_target="tpu_custom_call" | custom-call | flops 1000000000 | bytes 20000000 | tf_op jit(solution)/shard_map/pallas_call | solution.py:709
  212.5 71.8 %shard_map.178 = (bf16[4,256,2048]{2,1,0:T(8,128)(2,1)}, bf16[1,256,2048]{2,1,0:T(8,128)(2,1)}, f32[8,512]{1,0:T(8,128)}) custom-call(bf16[4,256,2048]{2,1,0:T(8,128)(2,1)} %get-tuple-element.47.refs_0_, f32[256,512]{1,0:T(8,128)} %get-tuple-element.48.refs_1_, f32[256,512]{1,0:T(8,128)} %constant_dynamic-slice_fusion.2.refs_2_.refs_1_, ...), custom_call_target="tpu_custom_call" | custom-call | flops 100000000 | bytes 100000000 | tf_op jit(solution)/shard_map/pallas_call | solution.py:429
  284.3 12.6 %shard_map.179 = (bf16[4,256,1024]{2,1,0:T(8,128)(2,1)}, bf16[4,256,2048]{2,1,0:T(8,128)(2,1)}) custom-call(bf16[4,256,2048]{2,1,0:T(8,128)(2,1)} %get-tuple-element.51.grad_ref, f32[4,256,1024]{2,1,0:T(8,128)} %get-tuple-element.52.gu_ref, bf16[2048,1536]{1,0:T(8,128)(2,1)} %get-tuple-element.46.w_ref), custom_call_target="tpu_custom_call" | custom-call | flops 1000000000 | bytes 20000000 | tf_op jit(solution)/shard_map/pallas_call | solution.py:709
  296.9 9.5 %bitcast_convert_fusion = bf16[2048,1024]{1,0:T(8,128)(2,1)} fusion(bf16[4,256,2048]{2,1,0:T(8,128)(2,1)} %get-tuple-element.45.x_ref, bf16[4,256,1024]{2,1,0:T(8,128)(2,1)} %get-tuple-element.58), kind=kOutput, calls=%fused_computation | convolution fusion | flops 4297064448 | bytes 10485760 | tf_op jit(solution)/shard_map/krd,kru->du/dot_general | solution.py:900
  306.4 3.2 dynamic-slice_bitcast_fusion
  310.2 2.5 bitcast_convert_fusion.1
  315.2 69.4 %shard_map.180 = (bf16[4,256,2048]{2,1,0:T(8,128)(2,1)}, f32[256,512]{1,0:T(8,128)}, f32[8,512]{1,0:T(8,128)}) custom-call(bf16[4,256,2048]{2,1,0:T(8,128)(2,1)} %get-tuple-element.53.refs_0_, f32[256,512]{1,0:T(8,128)} %constant_dynamic-slice_fusion.2.refs_2_.refs_1_, f32[256,512]{1,0:T(8,128)} %get-tuple-element.54.refs_2_, ...), custom_call_target="tpu_custom_call" | custom-call | flops 100000000 | bytes 100000000 | tf_op jit(solution)/shard_map/pallas_call | solution.py:429
  388.2 2.6 fusion
  395.3 12.1 %shard_map.181 = (f32[4,256,384]{2,1,0:T(8,128)}, f32[8,256]{1,0:T(8,128)}, f32[8,128]{1,0:T(8,128)}) custom-call(bf16[4,256,2048]{2,1,0:T(8,128)(2,1)} %get-tuple-element.59.proj_ref, f32[4,256,384]{2,1,0:T(8,128)} %get-tuple-element.60.qkv_ref, f32[8,256]{1,0:T(8,128)} %get-tuple-element.61.stats_ref, f32[8,128]{1,0:T(8,128)} %get-tuple-element.62.gain_ref, ...), custom_call_target="tpu_custom_call" | custom-call | flops 1000000000 | bytes 20000000 | tf_op jit(solution)/shard_map/pallas_call | solution.py:709
  407.3 12.8 %shard_map.182.inner_ref = f32[8,256]{1,0:T(8,128)} custom-call(f32[8,256]{1,0:T(8,128)} %get-tuple-element.65.stats_ref), custom_call_target="tpu_custom_call" | custom-call | tf_op jit(solution)/shard_map/pallas_call | solution.py:686
  420.1 3.5 fusion.1
  425.7 8.3 %shard_map.183 = (bf16[4,256,384]{2,1,0:T(8,128)(2,1)}, bf16[4,256,2048]{2,1,0:T(8,128)(2,1)}) custom-call(f32[4,256,384]{2,1,0:T(8,128)} %get-tuple-element.64.scaled_ref, f32[4,256,384]{2,1,0:T(8,128)} %get-tuple-element.60.qkv_ref, f32[8,256]{1,0:T(8,128)} %get-tuple-element.61.stats_ref, f32[8,256]{1,0:T(8,128)} %shard_map.182.inner_ref, ...), custom_call_target="tpu_custom_call" | custom-call | flops 1000000000 | bytes 20000000 | tf_op jit(solution)/shard_map/pallas_call | solution.py:709
  434.0 4.8 bitcast_convert_fusion.2
  441.3 42.0 %shard_map.184 = (bf16[1,256,2048]{2,1,0:T(8,128)(2,1)}, f32[8,640]{1,0:T(8,128)}) custom-call(bf16[4,256,2048]{2,1,0:T(8,128)(2,1)} %get-tuple-element.68.refs_0_, f32[256,512]{1,0:T(8,128)} %get-tuple-element.69.refs_1_, f32[8,512]{1,0:T(8,128)} %get-tuple-element.70.refs_2_, f32[8,512]{1,0:T(8,128)} %get-tuple-element.71.refs_3_, ...), custom_call_target="tpu_custom_call" | custom-call | flops 100000000 | bytes 100000000 | tf_op jit(solution)/shard_map/pallas_call | solution.py:429
  483.3 2.8 bitcast_convert_fusion.3
  494.5 2.8 collective-permute-start.7
  498.8 29.3 %collective-permute-done.7.refs_1_ = bf16[256,128]{1,0:T(8,128)(2,1)S(1)} collective-permute-done((bf16[256,128]{1,0:T(8,128)(2,1)S(1)}, bf16[256,128]{1,0:T(8,128)(2,1)S(1)}, u32[]{:S(2)}, u32[]{:S(2)}) %collective-permute-start.7) | collective-permute-done | bytes 65568 | tf_op jit(solution)/shard_map/ppermute | solution.py:43
  529.6 14.1 %collective-permute-done.8.refs_2_ = bf16[256,128]{1,0:T(8,128)(2,1)S(1)} collective-permute-done((bf16[256,128]{1,0:T(8,128)(2,1)S(1)}, bf16[256,128]{1,0:T(8,128)(2,1)S(1)}, u32[]{:S(2)}, u32[]{:S(2)}) %collective-permute-start.8) | collective-permute-done | bytes 65568 | tf_op jit(solution)/shard_map/ppermute | solution.py:43
  543.7 3.2 collective-permute-start.3
  549.0 2.6 shard_map.188
  554.3 3.8 shard_map.187
  558.1 7.6 %copy.28 = f32[256,2,2048]{2,1,0:T(2,128)} copy(f32[256,2,2048]{2,0,1:T(8,128)} %bitcast.101) | data formatting | bytes 8388608
  566.5 2.6 shard_map.185
  (88 shorter events, 38.9 us)
Async XLA Ops:
  296.9 13.3 %copy-start.16 = (bf16[4,256,512]{2,1,0:T(8,128)(2,1)S(1)}, bf16[4,256,512]{2,1,0:T(8,128)(2,1)}, u32[]{:S(2)}) copy-start(bf16[4,256,512]{2,1,0:T(8,128)(2,1)} %get-tuple-element.57) | copy-start | bytes 3145732
  309.6 78.5 %collective-permute-start.1 = (bf16[4,256,1024]{2,1,0:T(8,128)(2,1)}, bf16[4,256,1024]{2,1,0:T(8,128)(2,1)}, u32[]{:S(2)}, u32[]{:S(2)}) collective-permute-start(bf16[4,256,1024]{2,1,0:T(8,128)(2,1)} %dynamic-slice_bitcast_fusion), channel_id=1, source_target_pairs={{0,4},{4,0},{1,5},{5,1},{2,6},{6,2},{3,7},{7,3},{8,12},{12,8},{9,1... | collective-permute-start | bytes 6291464 | tf_op jit(solution)/shard_map/ppermute | solution.py:43
  313.7 72.5 %collective-permute-start = (bf16[4,256,512]{2,1,0:T(8,128)(2,1)}, bf16[4,256,512]{2,1,0:T(8,128)(2,1)}, u32[]{:S(2)}, u32[]{:S(2)}) collective-permute-start(bf16[4,256,512]{2,1,0:T(8,128)(2,1)} %dynamic-slice_bitcast_fusion.1), channel_id=1, source_target_pairs={{0,4},{4,0},{1,5},{5,1},{2,6},{6,2},{3,7},{7,3},{8,12},{12,8},{9,1... | collective-permute-start | bytes 3145736 | tf_op jit(solution)/shard_map/ppermute | solution.py:43
  315.2 69.5 %copy-start.4 = (bf16[1,256,2048]{2,1,0:T(8,128)(2,1)S(1)}, bf16[1,256,2048]{2,1,0:T(8,128)(2,1)}, u32[]{:S(2)}) copy-start(bf16[1,256,2048]{2,1,0:T(8,128)(2,1)} %get-tuple-element.50) | copy-start | bytes 3145732
  391.8 101.1 %collective-permute-start.13 = (bf16[256,512]{1,0:T(8,128)(2,1)}, bf16[256,512]{1,0:T(8,128)(2,1)S(1)}, u32[]{:S(2)}, u32[]{:S(2)}) collective-permute-start(bf16[256,512]{1,0:T(8,128)(2,1)} %get-tuple-element.96), channel_id=1, source_target_pairs={{0,8},{8,0},{16,24},{24,16},{1,9},{9,1},{17,25},{25,17},{2,10},{10... | collective-permute-start | bytes 786440 | tf_op jit(solution)/shard_map/ppermute | solution.py:43
  391.8 101.5 %collective-permute-start.14 = (bf16[256,512]{1,0:T(8,128)(2,1)}, bf16[256,512]{1,0:T(8,128)(2,1)}, u32[]{:S(2)}, u32[]{:S(2)}) collective-permute-start(bf16[256,512]{1,0:T(8,128)(2,1)} %get-tuple-element.95), channel_id=1, source_target_pairs={{0,16},{8,24},{16,0},{24,8},{1,17},{9,25},{17,1},{25,9},{2,18},{10... | collective-permute-start | bytes 786440 | tf_op jit(solution)/shard_map/ppermute | solution.py:43
  393.8 104.9 %collective-permute-start.15 = (bf16[256,512]{1,0:T(8,128)(2,1)}, bf16[256,512]{1,0:T(8,128)(2,1)}, u32[]{:S(2)}, u32[]{:S(2)}) collective-permute-start(bf16[256,512]{1,0:T(8,128)(2,1)} %get-tuple-element.94), channel_id=1, source_target_pairs={{0,24},{8,16},{16,8},{24,0},{1,25},{9,17},{17,9},{25,1},{2,26},{10... | collective-permute-start | bytes 786440 | tf_op jit(solution)/shard_map/ppermute | solution.py:43
  395.3 24.9 %copy-start.17 = (bf16[4,256,128]{2,1,0:T(8,128)(2,1)S(1)}, bf16[4,256,128]{2,1,0:T(8,128)(2,1)}, u32[]{:S(2)}) copy-start(bf16[4,256,128]{2,1,0:T(8,128)(2,1)} %get-tuple-element.76) | copy-start | bytes 786436
  425.1 64.2 %collective-permute-start.6 = (bf16[4,256,128]{2,1,0:T(8,128)(2,1)}, bf16[4,256,128]{2,1,0:T(8,128)(2,1)}, u32[]{:S(2)}, u32[]{:S(2)}) collective-permute-start(bf16[4,256,128]{2,1,0:T(8,128)(2,1)} %dynamic-slice_bitcast_fusion.11), channel_id=1, source_target_pairs={{0,4},{4,0},{1,5},{5,1},{2,6},{6,2},{3,7},{7,3},{8,12},{12,8},{9,1... | collective-permute-start | bytes 786440 | tf_op jit(solution)/shard_map/ppermute | solution.py:43
  439.8 54.8 %collective-permute-start.2 = (bf16[4,256,384]{2,1,0:T(8,128)(2,1)}, bf16[4,256,384]{2,1,0:T(8,128)(2,1)}, u32[]{:S(2)}, u32[]{:S(2)}) collective-permute-start(bf16[4,256,384]{2,1,0:T(8,128)(2,1)} %dynamic-slice_bitcast_fusion.2), channel_id=1, source_target_pairs={{0,4},{4,0},{1,5},{5,1},{2,6},{6,2},{3,7},{7,3},{8,12},{12,8},{9,1... | collective-permute-start | bytes 2359304 | tf_op jit(solution)/shard_map/ppermute | solution.py:43
  489.4 57.8 %collective-permute-start.10 = (bf16[256,1024]{1,0:T(8,128)(2,1)S(1)}, bf16[256,1024]{1,0:T(8,128)(2,1)S(1)}, u32[]{:S(2)}, u32[]{:S(2)}) collective-permute-start(bf16[256,1024]{1,0:T(8,128)(2,1)S(1)} %get-tuple-element.92), channel_id=1, source_target_pairs={{0,8},{8,0},{16,24},{24,16},{1,9},{9,1},{17,25},{25,17},{2,10},{10... | collective-permute-start | bytes 1572872 | tf_op jit(solution)/shard_map/ppermute | solution.py:43
  492.9 56.1 %copy-start.9 = (bf16[256,512]{1,0:T(8,128)(2,1)}, bf16[256,512]{1,0:T(8,128)(2,1)S(1)}, u32[]{:S(2)}) copy-start(bf16[256,512]{1,0:T(8,128)(2,1)S(1)} %collective-permute-done.13.refs_1_) | copy-start | bytes 786436
  492.9 60.6 %collective-permute-start.11 = (bf16[256,1024]{1,0:T(8,128)(2,1)}, bf16[256,1024]{1,0:T(8,128)(2,1)S(1)}, u32[]{:S(2)}, u32[]{:S(2)}) collective-permute-start(bf16[256,1024]{1,0:T(8,128)(2,1)} %get-tuple-element.91), channel_id=1, source_target_pairs={{0,16},{8,24},{16,0},{24,8},{1,17},{9,25},{17,1},{25,9},{2,18},{10... | collective-permute-start | bytes 1572872 | tf_op jit(solution)/shard_map/ppermute | solution.py:43
  493.3 60.2 %collective-permute-start.12 = (bf16[256,1024]{1,0:T(8,128)(2,1)}, bf16[256,1024]{1,0:T(8,128)(2,1)}, u32[]{:S(2)}, u32[]{:S(2)}) collective-permute-start(bf16[256,1024]{1,0:T(8,128)(2,1)} %get-tuple-element.90), channel_id=1, source_target_pairs={{0,24},{8,16},{16,8},{24,0},{1,25},{9,17},{17,9},{25,1},{2,26},{10... | collective-permute-start | bytes 1572872 | tf_op jit(solution)/shard_map/ppermute | solution.py:43
  494.5 33.5 %collective-permute-start.7 = (bf16[256,128]{1,0:T(8,128)(2,1)S(1)}, bf16[256,128]{1,0:T(8,128)(2,1)S(1)}, u32[]{:S(2)}, u32[]{:S(2)}) collective-permute-start(bf16[256,128]{1,0:T(8,128)(2,1)S(1)} %get-tuple-element.104), channel_id=1, source_target_pairs={{0,8},{8,0},{16,24},{24,16},{1,9},{9,1},{17,25},{25,17},{2,10},{10... | collective-permute-start | bytes 196616 | tf_op jit(solution)/shard_map/ppermute | solution.py:43
  498.7 45.1 %collective-permute-start.8 = (bf16[256,128]{1,0:T(8,128)(2,1)S(1)}, bf16[256,128]{1,0:T(8,128)(2,1)S(1)}, u32[]{:S(2)}, u32[]{:S(2)}) collective-permute-start(bf16[256,128]{1,0:T(8,128)(2,1)S(1)} %get-tuple-element.103), channel_id=1, source_target_pairs={{0,16},{8,24},{16,0},{24,8},{1,17},{9,25},{17,1},{25,9},{2,18},{10... | collective-permute-start | bytes 196616 | tf_op jit(solution)/shard_map/ppermute | solution.py:43
  528.1 23.6 %copy-start.13 = (bf16[256,128]{1,0:T(8,128)(2,1)}, bf16[256,128]{1,0:T(8,128)(2,1)S(1)}, u32[]{:S(2)}) copy-start(bf16[256,128]{1,0:T(8,128)(2,1)S(1)} %collective-permute-done.7.refs_1_) | copy-start | bytes 196612
  528.1 18.9 %collective-permute-start.9 = (bf16[256,128]{1,0:T(8,128)(2,1)S(1)}, bf16[256,128]{1,0:T(8,128)(2,1)S(1)}, u32[]{:S(2)}, u32[]{:S(2)}) collective-permute-start(bf16[256,128]{1,0:T(8,128)(2,1)S(1)} %get-tuple-element.102), channel_id=1, source_target_pairs={{0,24},{8,16},{16,8},{24,0},{1,25},{9,17},{17,9},{25,1},{2,26},{10... | collective-permute-start | bytes 196616 | tf_op jit(solution)/shard_map/ppermute | solution.py:43
  543.7 7.9 %copy-start.14 = (bf16[256,128]{1,0:T(8,128)(2,1)}, bf16[256,128]{1,0:T(8,128)(2,1)S(1)}, u32[]{:S(2)}) copy-start(bf16[256,128]{1,0:T(8,128)(2,1)S(1)} %collective-permute-done.8.refs_2_) | copy-start | bytes 196612
  543.7 21.9 %collective-permute-start.3 = (bf16[256,384]{1,0:T(8,128)(2,1)S(1)}, bf16[256,384]{1,0:T(8,128)(2,1)S(1)}, u32[]{:S(2)}, u32[]{:S(2)}) collective-permute-start(bf16[256,384]{1,0:T(8,128)(2,1)S(1)} %get-tuple-element.100), channel_id=1, source_target_pairs={{0,8},{8,0},{16,24},{24,16},{1,9},{9,1},{17,25},{25,17},{2,10},{10... | collective-permute-start | bytes 589832 | tf_op jit(solution)/shard_map/ppermute | solution.py:43
  547.0 18.7 %collective-permute-start.4 = (bf16[256,384]{1,0:T(8,128)(2,1)S(1)}, bf16[256,384]{1,0:T(8,128)(2,1)S(1)}, u32[]{:S(2)}, u32[]{:S(2)}) collective-permute-start(bf16[256,384]{1,0:T(8,128)(2,1)S(1)} %get-tuple-element.99), channel_id=1, source_target_pairs={{0,16},{8,24},{16,0},{24,8},{1,17},{9,25},{17,1},{25,9},{2,18},{10... | collective-permute-start | bytes 589832 | tf_op jit(solution)/shard_map/ppermute | solution.py:43
  547.2 6.3 %copy-start.5 = (bf16[256,1024]{1,0:T(8,128)(2,1)}, bf16[256,1024]{1,0:T(8,128)(2,1)S(1)}, u32[]{:S(2)}) copy-start(bf16[256,1024]{1,0:T(8,128)(2,1)S(1)} %collective-permute-done.10.refs_1_) | copy-start | bytes 1572868
  547.2 18.5 %collective-permute-start.5 = (bf16[256,384]{1,0:T(8,128)(2,1)S(1)}, bf16[256,384]{1,0:T(8,128)(2,1)S(1)}, u32[]{:S(2)}, u32[]{:S(2)}) collective-permute-start(bf16[256,384]{1,0:T(8,128)(2,1)S(1)} %get-tuple-element.98), channel_id=1, source_target_pairs={{0,24},{8,16},{16,8},{24,0},{1,25},{9,17},{17,9},{25,1},{2,26},{10... | collective-permute-start | bytes 589832 | tf_op jit(solution)/shard_map/ppermute | solution.py:43
  558.1 11.0 %copy-start.1 = (f32[256,2048]{1,0:T(8,128)S(1)}, f32[256,2048]{1,0:T(8,128)}, u32[]{:S(2)}) copy-start(f32[256,2048]{1,0:T(8,128)} %param.19) | copy-start | bytes 6291460
  (10 other events, 23.7 us)

commit v4 on v3

--- a/solution.py
+++ b/solution.py
@@ -151,239 +151,446 @@
     return queries, key_rows, values, q_inv, k_inv, q_rot, k_rot, probs
 
 
-def reduce_kernel(na, nb, mode, *refs):
-    n_in = {"mlp": 4, "back": 5, "tok": 5}[mode]
-    n_out = {"mlp": 3, "back": 3, "tok": 2}[mode]
-    links = Links(*refs[-2:])
-    reduce(na, nb, mode, links, refs[:n_in], refs[n_in : n_in + n_out], refs[n_in + n_out : -2])
-    links.finish()
-
-
-def reduce(na, nb, mode, links, ins, outs, scratch, hooks=None):
-    from_q, half_sum, from_p, to_a, from_a, total, parts, cols, stat, *scratch = scratch
-    part_ref, out = ins[0], outs[0]
-    a, b = lax.axis_index("a"), lax.axis_index("b")
-    p, q = lax.axis_index("p"), lax.axis_index("q")
-    rows, width = part_ref.shape[1], part_ref.shape[2]
-    quarter, half = width // 4, width // 2
-    count = rows // HALVES
-    mine, pair = span(2 * q + p, quarter), span(q, half)
-    peers = [{"q": 1 - q}, {"p": 1 - p}] + [{"a": across(a, k)} for k in range(1, na)]
-    if mode == "tok":
-        own_sums, a_sums, b_sums = scratch[:3]
-        sums_ref = outs[1]
-        own_sums[...] = jnp.zeros_like(own_sums)
-        own_sums[0:1, mine] = jnp.sum(ins[2][...], axis=0, keepdims=True)
-        own_sums[1:2, mine] = jnp.sum(ins[3][...], axis=0, keepdims=True)
-        peers += [{"b": across(b, j)} for j in range(1, nb)]
-    if hooks is None:
-        greet(peers)
-    hooks = hooks or {}
-    halves = [slice(h * count, (h + 1) * count) for h in range(HALVES)]
-    lead = list(range(2, na)) + [1, 0]
-    give, keep = span(1 - q, half), span(q, half)
-
-    def each(h, body):
+class Reduce:
+    def __init__(self, na, links, part, out, scratch):
+        self.na, self.links, self.part, self.out = na, links, part, out
+        self.from_q, self.half_sum, self.from_p, self.to_a, self.from_a = scratch[:5]
+        self.total, self.parts, self.cols, self.stat = scratch[5:9]
+        self.a, self.p, self.q = (lax.axis_index(axis) for axis in ("a", "p", "q"))
+        self.rows, self.width = out.shape[1:]
+        self.quarter, self.half = self.width // 4, self.width // 2
+        self.count = self.rows // HALVES
+        self.mine, self.pair = span(2 * self.q + self.p, self.quarter), span(self.q, self.half)
+        self.lead = list(range(2, na)) + [1, 0]
+        self.step_q, self.step_p, self.step_a = {}, {}, {}
+        self.spread_a, self.spread_p, self.spread_q, self.stats = {}, {}, {}, {}
+
+    def at(self, h):
+        return slice(h * self.count, (h + 1) * self.count)
+
+    def each(self, h, body):
         def step(i, carry):
-            body(pl.ds(pl.multiple_of(h * count + i * TILE, TILE), TILE))
+            body(pl.ds(pl.multiple_of(h * self.count + i * TILE, TILE), TILE))
             return carry
 
-        lax.fori_loop(0, count // TILE, step, 0)
-
-    if mode == "tok":
-        sums_p = links.send(own_sums.at[:, mine], own_sums.at[:, mine], {"p": 1 - p})
-
-    step_q, step_p, step_a = {}, {}, {}
-    for h, at_h in enumerate(halves):
-        for k in lead:
-            step_q[h, k] = links.send(
-                part_ref.at[k, at_h, give], from_q.at[k, at_h], {"q": 1 - q}
-            )
-    for h, at_h in enumerate(halves):
-        for k in lead:
-            step_q[h, k].wait_recv()
-
-            def add_half(at, k=k):
-                own = part_ref[k, at, keep].astype(f32)
-                half_sum[k, at] = (own + from_q[k, at].astype(f32)).astype(bf16)
-
-            each(h, add_half)
-            step_p[h, k] = links.send(
-                half_sum.at[k, at_h, span(1 - p, quarter)], from_p.at[k, at_h], {"p": 1 - p}
-            )
-    if mode == "tok":
-        sums_p.wait_recv()
-        sums_q = links.send(own_sums.at[:, pair], own_sums.at[:, pair], {"q": 1 - q})
-
-    def send_a(h):
-        at_h = halves[h]
-        for k in lead[:-1]:
-            step_p[h, k].wait_recv()
-
-            def add_quarter(at, k=k):
-                own = half_sum[k, at, span(p, quarter)].astype(f32)
-                to_a[k - 1, at] = (own + from_p[k, at].astype(f32)).astype(bf16)
-
-            each(h, add_quarter)
-            step_a[h, k] = links.send(
-                to_a.at[k - 1, at_h], from_a.at[k - 1, at_h], {"a": across(a, k)}
-            )
-
-    for h in range(HALVES):
-        send_a(h)
-    hooks.get("scattered", lambda: None)()
-    if mode == "tok":
-        sums_q.wait_recv()
-        sums_a = [
-            links.send(own_sums.at[:, span(across(a, k), quarter)], a_sums.at[k - 1], {"a": across(a, k)})
-            for k in range(1, na)
-        ]
-
-    def add_all(at):
-        own = half_sum[0, at, span(p, quarter)].astype(f32) + from_p[0, at].astype(f32)
-        for k in range(1, na):
-            own = own + from_a[k - 1, at].astype(f32)
+        lax.fori_loop(0, self.count // TILE, step, 0)
+
+    def send_q(self, h, k):
+        at, q = self.at(h), self.q
+        source = self.part.at[k, at, span(1 - q, self.half)]
+        self.step_q[h, k] = self.links.send(source, self.from_q.at[k, at], {"q": 1 - q})
+
+    def send_p(self, h, k):
+        self.step_q[h, k].wait_recv()
+
+        def add(at):
+            own = self.part[k, at, span(self.q, self.half)].astype(f32)
+            self.half_sum[k, at] = (own + self.from_q[k, at].astype(f32)).astype(bf16)
+
+        self.each(h, add)
+        at, p = self.at(h), self.p
+        source = self.half_sum.at[k, at, span(1 - p, self.quarter)]
+        self.step_p[h, k] = self.links.send(source, self.from_p.at[k, at], {"p": 1 - p})
+
+    def send_a(self, h, k):
+        if not k:
+            return
+        self.step_p[h, k].wait_recv()
+
+        def add(at):
+            own = self.half_sum[k, at, span(self.p, self.quarter)].astype(f32)
+            self.to_a[k - 1, at] = (own + self.from_p[k, at].astype(f32)).astype(bf16)
+
+        self.each(h, add)
+        at = self.at(h)
+        self.step_a[h, k] = self.links.send(
+            self.to_a.at[k - 1, at], self.from_a.at[k - 1, at], {"a": across(self.a, k)}
+        )
+
+    def add_all(self, at):
+        own = self.half_sum[0, at, span(self.p, self.quarter)].astype(f32)
+        own = own + self.from_p[0, at].astype(f32)
+        for k in range(1, self.na):
+            own = own + self.from_a[k - 1, at].astype(f32)
         return own
 
-    def exchange(h, number):
-        at_h = halves[h]
-        stats = to_row(parts[0, at_h], 0)
-        if number == 2:
-            stats = stats + to_row(parts[1, at_h], 1)
-        stat[h, 0] = stats
-        links.send(stat.at[h, 0], stat.at[h, 1], {"p": 1 - p}).wait_recv()
+    def scattered(self, h, first, number):
+        self.step_p[h, 0].wait_recv()
+        for k in range(1, self.na):
+            self.step_a[h, k].wait_recv()
+        self.each(h, first)
+        if number:
+            at = self.at(h)
+            stats = to_row(self.parts[0, at], 0)
+            if number == 2:
+                stats = stats + to_row(self.parts[1, at], 1)
+            stat = self.stat
+            stat[h, 0] = stats
+            self.stats[h] = self.links.send(stat.at[h, 0], stat.at[h, 1], {"p": 1 - self.p})
+
+    def stats_q(self, h):
+        stat = self.stat
+        self.stats[h].wait_recv()
         stat[h, 2] = stat[h, 0] + stat[h, 1]
-        links.send(stat.at[h, 2], stat.at[h, 3], {"q": 1 - q}).wait_recv()
-        stats = (stat[h, 2] + stat[h, 3]) / width
+        self.stats[h] = self.links.send(stat.at[h, 2], stat.at[h, 3], {"q": 1 - self.q})
+
+    def stats_done(self, h, number):
+        stat = self.stat
+        self.stats[h].wait_recv()
+        stats = (stat[h, 2] + stat[h, 3]) / self.width
         for i in range(number):
-            cols[i, at_h] = to_column(stats, i)
-
-    if mode == "attn":
-        _, tok_ref, gain_ref = ins
-        _, proj_ref, inv_ref, res_ref = outs
-        number = 1
-
-        def first(at):
-            own = add_all(at)
-            proj_ref[at] = own
-            parts[0, at] = fold(own * own)
-
-        def second(at):
-            own = proj_ref[at]
-            inv = lax.rsqrt(cols[0, at] + epsilon)
-            inv_ref[at] = inv
-            residual = tok_ref[at].astype(f32) + own * wide(inv, quarter) * gain_ref[0:1]
-            res_ref[at] = residual
-            out[0, at, mine] = residual.astype(bf16)
-
-    elif mode == "mlp":
-        _, res_ref, grad_ref, gain_ref = ins
-        _, block_ref, sum_ref = outs
-        number = 2
-
-        def first(at):
-            own = add_all(at)
-            total[at] = own
-            parts[0, at] = fold(own * own)
-            parts[1, at] = fold(grad_ref[at] * gain_ref[1:2] * own)
-
-        sum_ref[...] = jnp.zeros_like(sum_ref)
-
-        def second(at):
-            own = total[at]
-            inv = wide(lax.rsqrt(cols[0, at] + epsilon), quarter)
-            upstream = grad_ref[at]
-            scaled = upstream * gain_ref[1:2]
-            normed = own * inv
-            block_ref[0, at, mine] = (res_ref[at] + normed * gain_ref[1:2]).astype(bf16)
-            gains = upstream * normed
-            sum_ref[...] += jnp.sum(gains.reshape(TILE // 8, 8, quarter), axis=0)
-            grad = inv * scaled - own * inv * inv * inv * wide(cols[1, at], quarter)
-            out[0, at, mine] = grad.astype(bf16)
-
-    elif mode == "back":
-        _, grad_ref, proj_ref, inv_ref, gain_ref = ins
-        _, res_ref, sum_ref = outs
-        number = 1
-
-        def first(at):
-            grad = grad_ref[at] + add_all(at)
-            res_ref[at] = grad
-            parts[0, at] = fold(grad * gain_ref[0:1] * proj_ref[at])
-
-        sum_ref[...] = jnp.zeros_like(sum_ref)
-
-        def second(at):
-            own = proj_ref[at]
-            inv = wide(inv_ref[at], quarter)
-            upstream = res_ref[at]
-            gains = upstream * own * inv
-            sum_ref[...] += jnp.sum(gains.reshape(TILE // 8, 8, quarter), axis=0)
-            grad = inv * (upstream * gain_ref[0:1])
-            grad = grad - own * inv * inv * inv * wide(cols[0, at], quarter)
-            out[0, at, mine] = grad.astype(bf16)
-
-    else:
-        grad_ref = ins[1]
-        number = 0
-
-        def first(at):
-            out[0, at, mine] = (grad_ref[at] + add_all(at)).astype(bf16)
-
-    blocks = range(1) if mode == "tok" else range(na)
-    spread_a, spread_p, spread_q = {}, {}, {}
-    for h, at_h in enumerate(halves):
-        step_p[h, 0].wait_recv()
-        for k in range(1, na):
-            step_a[h, k].wait_recv()
-        each(h, first)
-        if number:
-            exchange(h, number)
-            each(h, second)
-        here = out.at[0, at_h, mine]
+            self.cols[i, self.at(h)] = to_column(stats, i)
+
+    def spread(self, h, blocks):
+        here = self.out.at[0, self.at(h), self.mine]
         for k in blocks:
             if k:
-                spread_a[h, k] = links.send(here, out.at[k, at_h, mine], {"a": across(a, k)})
-        spread_p[h, 0] = links.send(here, here, {"p": 1 - p})
-    if mode == "tok":
-        for copy in sums_a:
-            copy.wait_recv()
-        held = own_sums[:, span(a, quarter)]
-        for k in range(1, na):
-            held = held + a_sums[k - 1]
-        b_sums[0, :, :quarter] = held
-        b_sums[0, :, quarter:] = ins[4][...]
-        sums_b = [
-            links.send(b_sums.at[0], b_sums.at[j], {"b": across(b, j)}) for j in range(1, nb)
+                target = self.out.at[k, self.at(h), self.mine]
+                self.spread_a[h, k] = self.links.send(here, target, {"a": across(self.a, k)})
+        self.spread_p[h, 0] = self.links.send(here, here, {"p": 1 - self.p})
+
+    def relay_p(self, h, k):
+        if not k:
+            return
+        self.spread_a[h, k].wait_recv()
+        here = self.out.at[k, self.at(h), self.mine]
+        self.spread_p[h, k] = self.links.send(here, here, {"p": 1 - self.p})
+
+    def relay_q(self, h, k):
+        self.spread_p[h, k].wait_recv()
+        here = self.out.at[k, self.at(h), self.pair]
+        self.spread_q[h, k] = self.links.send(here, here, {"q": 1 - self.q})
+
+    def arrived(self, h, k):
+        self.spread_q[h, k].wait_recv()
+
+
+def reduce_peers(na):
+    a, p, q = lax.axis_index("a"), lax.axis_index("p"), lax.axis_index("q")
+    return [{"q": 1 - q}, {"p": 1 - p}] + [{"a": across(a, k)} for k in range(1, na)]
+
+
+def attn_math(r, tok_ref, gain_ref, proj_ref, inv_ref, res_ref):
+    def first(at):
+        own = r.add_all(at)
+        proj_ref[at] = own
+        r.parts[0, at] = fold(own * own)
+
+    def second(at):
+        own = proj_ref[at]
+        inv = lax.rsqrt(r.cols[0, at] + epsilon)
+        inv_ref[at] = inv
+        residual = tok_ref[at].astype(f32) + own * wide(inv, r.quarter) * gain_ref[0:1]
+        res_ref[at] = residual
+        r.out[0, at, r.mine] = residual.astype(bf16)
+
+    return first, second
+
+
+def mlp_math(r, res_ref, grad_ref, gain_ref, block_ref, sum_ref):
+    def first(at):
+        own = r.add_all(at)
+        r.total[at] = own
+        r.parts[0, at] = fold(own * own)
+        r.parts[1, at] = fold(grad_ref[at] * gain_ref[1:2] * own)
+
+    def second(at):
+        own = r.total[at]
+        inv = wide(lax.rsqrt(r.cols[0, at] + epsilon), r.quarter)
+        upstream = grad_ref[at]
+        scaled = upstream * gain_ref[1:2]
+        normed = own * inv
+        block_ref[0, at, r.mine] = (res_ref[at] + normed * gain_ref[1:2]).astype(bf16)
+        gains = upstream * normed
+        sum_ref[...] += jnp.sum(gains.reshape(TILE // 8, 8, r.quarter), axis=0)
+        grad = inv * scaled - own * inv * inv * inv * wide(r.cols[1, at], r.quarter)
+        r.out[0, at, r.mine] = grad.astype(bf16)
+
+    return first, second
+
+
+def back_math(r, grad_ref, proj_ref, inv_ref, gain_ref, res_ref, sum_ref):
+    def first(at):
+        grad = grad_ref[at] + r.add_all(at)
+        res_ref[at] = grad
+        r.parts[0, at] = fold(grad * gain_ref[0:1] * proj_ref[at])
+
+    def second(at):
+        own = proj_ref[at]
+        inv = wide(inv_ref[at], r.quarter)
+        upstream = res_ref[at]
+        gains = upstream * own * inv
+        sum_ref[...] += jnp.sum(gains.reshape(TILE // 8, 8, r.quarter), axis=0)
+        grad = inv * (upstream * gain_ref[0:1])
+        grad = grad - own * inv * inv * inv * wide(r.cols[0, at], r.quarter)
+        r.out[0, at, r.mine] = grad.astype(bf16)
+
+    return first, second
+
+
+def middle_kernel(na, *refs):
+    x_ref, w_ref, res_ref, grad_ref, proj_ref, inv_ref, gain_ref = refs[:7]
+    out, block_ref, hidden_ref, grad_gu_ref, back_out = refs[7:12]
+    ffn_sum_ref, grad_res_ref, attn_sum_ref = refs[12:15]
+    gu_ref, part_ref, back_part_ref = refs[15:18]
+    scratch, (send_sem, recv_sem) = refs[18:-2], refs[-2:]
+    units = hidden_ref.shape[2]
+    width = x_ref.shape[2]
+    greet(reduce_peers(na))
+    links = Links(send_sem, recv_sem)
+    r = Reduce(na, links, part_ref, out, scratch[:9])
+    s = Reduce(na, links, back_part_ref, back_out, scratch[9:])
+    ffn_sum_ref[...] = jnp.zeros_like(ffn_sum_ref)
+    attn_sum_ref[...] = jnp.zeros_like(attn_sum_ref)
+    wide_tile = 512
+
+    def forward(k):
+        def gated(n, carry):
+            at, up_at = span(n, 256), pl.ds(pl.multiple_of(units + n * 256, 256), 256)
+            gate = dot(x_ref[k], w_ref[:, at])
+            up = dot(x_ref[k], w_ref[:, up_at])
+            gu_ref[k, :, at] = gate
+            gu_ref[k, :, up_at] = up
+            hidden_ref[k, :, at] = (gate * jax.nn.sigmoid(gate) * up).astype(bf16)
+            return carry
+
+        lax.fori_loop(0, units // 256, gated, 0)
+
+        def down(n, carry):
+            at = span(n, wide_tile)
+            part_ref[k, :, at] = dot_t(hidden_ref[k], w_ref[at, 2 * units :]).astype(bf16)
+            return carry
+
+        lax.fori_loop(0, width // wide_tile, down, 0)
+
+    def backward(h, k):
+        rows = r.at(h)
+
+        def gated(n, carry):
+            at, up_at = span(n, 256), pl.ds(pl.multiple_of(units + n * 256, 256), 256)
+            down_at = pl.ds(pl.multiple_of(2 * units + n * 256, 256), 256)
+            grad_hidden = dot(out[k, rows], w_ref[:, down_at])
+            gate, up = gu_ref[k, rows, at], gu_ref[k, rows, up_at]
+            sigmoid = jax.nn.sigmoid(gate)
+            active = gate * sigmoid
+            grad_gu_ref[k, rows, at] = (
+                grad_hidden * up * (sigmoid * (1.0 + gate * (1.0 - sigmoid)))
+            ).astype(bf16)
+            grad_gu_ref[k, rows, up_at] = (grad_hidden * active).astype(bf16)
+            return carry
+
+        lax.fori_loop(0, units // 256, gated, 0)
+
+        def back(n, carry):
+            at = span(n, wide_tile)
+            back_part_ref[k, rows, at] = dot_t(
+                grad_gu_ref[k, rows], w_ref[at, : 2 * units]
+            ).astype(bf16)
+            return carry
+
+        lax.fori_loop(0, width // wide_tile, back, 0)
+
+    lead = r.lead
+    for i, k in enumerate(lead):
+        forward(k)
+        for h in range(HALVES):
+            r.send_q(h, k)
+        if i:
+            r.send_p(0, lead[i - 1])
+    r.send_p(0, lead[-1])
+    for k in lead:
+        r.send_a(0, k)
+        r.send_p(1, k)
+    first, second = mlp_math(r, res_ref, grad_ref, gain_ref, block_ref, ffn_sum_ref)
+    for k in lead[:-2]:
+        r.send_a(1, k)
+    r.scattered(0, first, 2)
+    r.send_a(1, lead[-2])
+    r.stats_q(0)
+    r.stats_done(0, 2)
+    r.each(0, second)
+    r.spread(0, lead)
+    r.scattered(1, first, 2)
+    r.relay_q(0, 0)
+    r.stats_q(1)
+    r.arrived(0, 0)
+    r.stats_done(1, 2)
+    r.each(1, second)
+    r.spread(1, lead)
+    here = block_ref.at[0, :, r.mine]
+    block_p = links.send(here, here, {"p": 1 - r.p})
+    backward(0, 0)
+    s.send_q(0, 0)
+    r.relay_q(1, 0)
+    s.send_p(0, 0)
+    block_p.wait_recv()
+    here = block_ref.at[0, :, r.pair]
+    block_q = links.send(here, here, {"q": 1 - r.q})
+    r.arrived(1, 0)
+    backward(1, 0)
+    s.send_q(1, 0)
+    order = [(h, k) for h in range(HALVES) for k in lead[:-1]]
+    s.send_p(1, 0)
+    steps = len(order)
+    back_first, back_second = back_math(
+        s, grad_ref, proj_ref, inv_ref, gain_ref, grad_res_ref, attn_sum_ref
+    )
+    for i in range(steps + 4):
+        if 0 <= i - 4 < steps:
+            s.send_a(*order[i - 4])
+        if 0 <= i - 3 < steps:
+            s.send_p(*order[i - 3])
+        if 0 <= i - 2 < steps:
+            r.arrived(*order[i - 2])
+            backward(*order[i - 2])
+            s.send_q(*order[i - 2])
+        if 0 <= i - 1 < steps:
+            r.relay_q(*order[i - 1])
+        if i < steps:
+            r.relay_p(*order[i])
+    s.scattered(0, back_first, 1)
+    s.stats_q(0)
+    s.stats_done(0, 1)
+    s.each(0, back_second)
+    s.spread(0, lead)
+    s.scattered(1, back_first, 1)
+    s.relay_q(0, 0)
+    s.stats_q(1)
+    s.stats_done(1, 1)
+    s.each(1, back_second)
+    s.spread(1, lead)
+    for h, k in order:
+        s.relay_p(h, k)
+    s.relay_q(1, 0)
+    for h, k in order:
+        s.relay_q(h, k)
+    for h in range(HALVES):
+        for k in range(na):
+            s.arrived(h, k)
+    block_q.wait_recv()
+    links.finish()
+
+
+def middle_call(x_all, w_mlp, res_mine, grad_mine, proj_mine, inv_mine, width_gain):
+    na, rows, width = x_all.shape
+    quarter, units = width // 4, w_mlp.shape[1] // 3
+    vmem = pl.BlockSpec(memory_space=pltpu.VMEM)
+    shape = jax.ShapeDtypeStruct
+    full = shape((na, rows, width), bf16)
+    outs = (
+        full,
+        shape((1, rows, width), bf16),
+        shape((na, rows, units), bf16),
+        shape((na, rows, 2 * units), bf16),
+        full,
+        shape((8, quarter), f32),
+        shape((rows, quarter), f32),
+        shape((8, quarter), f32),
+    )
+    copies = 2 * HALVES * (6 * na + 1) + 2
+    return pl.pallas_call(
+        functools.partial(middle_kernel, na),
+        out_shape=outs,
+        in_specs=[vmem] * 7,
+        out_specs=(vmem,) * len(outs),
+        scratch_shapes=[
+            pltpu.VMEM((na, rows, 2 * units), f32),
+            pltpu.VMEM((na, rows, width), bf16),
+            pltpu.VMEM((na, rows, width), bf16),
         ]
-    hooks.get("spread", lambda: None)()
-    for h, at_h in enumerate(halves):
-        for k in blocks:
-            if k:
-                spread_a[h, k].wait_recv()
-                here = out.at[k, at_h, mine]
-                spread_p[h, k] = links.send(here, here, {"p": 1 - p})
-    if mode == "mlp":
-        here = block_ref.at[0, :, mine]
-        block_p = links.send(here, here, {"p": 1 - p})
-    for h, at_h in enumerate(halves):
-        for k in blocks:
-            spread_p[h, k].wait_recv()
-            here = out.at[k, at_h, pair]
-            spread_q[h, k] = links.send(here, here, {"q": 1 - q})
-    if mode == "mlp":
-        block_p.wait_recv()
-        here = block_ref.at[0, :, pair]
-        links.send(here, here, {"q": 1 - q}).wait_recv()
-    if mode == "tok":
-        for copy in sums_b:
-            copy.wait_recv()
-        held = b_sums[0]
-        for j in range(1, nb):
-            held = held + b_sums[j]
-        sums_ref[...] = held
-    for copy in spread_q.values():
+        + reduce_scratch(na, rows, width)
+        + reduce_scratch(na, rows, width)
+        + [pltpu.SemaphoreType.DMA((copies,)), pltpu.SemaphoreType.DMA((copies,))],
+        compiler_params=pltpu.CompilerParams(
+            collective_id=2, has_side_effects=True, vmem_limit_bytes=VMEM_LIMIT
+        ),
+        name="middle",
+    )(x_all, w_mlp, res_mine, grad_mine, proj_mine, inv_mine, width_gain)
+
+
+def last_kernel(na, nb, part_ref, grad_ref, attn_sum_ref, ffn_sum_ref, head_sum_ref, out, sums_ref, *refs):
+    own_sums, a_sums, b_sums = refs[:3]
+    scratch, (send_sem, recv_sem) = refs[3:-2], refs[-2:]
+    links = Links(send_sem, recv_sem)
+    r = Reduce(na, links, part_ref, out, scratch)
+    a, b, p, q, mine, pair, quarter = (
+        r.a, lax.axis_index("b"), r.p, r.q, r.mine, r.pair, r.quarter,
+    )
+    own_sums[...] = jnp.zeros_like(own_sums)
+    own_sums[0:1, mine] = jnp.sum(attn_sum_ref[...], axis=0, keepdims=True)
+    own_sums[1:2, mine] = jnp.sum(ffn_sum_ref[...], axis=0, keepdims=True)
+    greet(reduce_peers(na) + [{"b": across(b, j)} for j in range(1, nb)])
+    here = own_sums.at[:, mine]
+    sums_p = links.send(here, here, {"p": 1 - p})
+    for h in range(HALVES):
+        for k in r.lead:
+            r.send_q(h, k)
+    for h in range(HALVES):
+        for k in r.lead:
+            r.send_p(h, k)
+    sums_p.wait_recv()
+    here = own_sums.at[:, pair]
+    sums_q = links.send(here, here, {"q": 1 - q})
+    for h in range(HALVES):
+        for k in r.lead:
+            r.send_a(h, k)
+    sums_q.wait_recv()
+    sums_a = [
+        links.send(own_sums.at[:, span(across(a, k), quarter)], a_sums.at[k - 1], {"a": across(a, k)})
+        for k in range(1, na)
+    ]
+
+    def first(at):
+        out[0, at, mine] = (grad_ref[at] + r.add_all(at)).astype(bf16)
+
+    for h in range(HALVES):
+        r.scattered(h, first, 0)
+        r.spread(h, [0])
+    for copy in sums_a:
         copy.wait_recv()
+    held = own_sums[:, span(a, quarter)]
+    for k in range(1, na):
+        held = held + a_sums[k - 1]
+    b_sums[0, :, :quarter] = held
+    b_sums[0, :, quarter:] = head_sum_ref[...]
+    sums_b = [links.send(b_sums.at[0], b_sums.at[j], {"b": across(b, j)}) for j in range(1, nb)]
+    for h in range(HALVES):
+        r.relay_q(h, 0)
+    for copy in sums_b:
+        copy.wait_recv()
+    held = b_sums[0]
+    for j in range(1, nb):
+        held = held + b_sums[j]
+    sums_ref[...] = held
+    for h in range(HALVES):
+        r.arrived(h, 0)
+    links.finish()
+
+
+def last_call(nb, part, grad_res, attn_sums, ffn_sums, head_sums):
+    na, rows, width = part.shape
+    quarter = width // 4
+    vmem = pl.BlockSpec(memory_space=pltpu.VMEM)
+    shape = jax.ShapeDtypeStruct
+    copies = HALVES * (3 * na + 1) + 1 + na + nb
+    return pl.pallas_call(
+        functools.partial(last_kernel, na, nb),
+        out_shape=(shape((1, rows, width), bf16), shape((8, quarter + HD), f32)),
+        in_specs=[vmem] * 5,
+        out_specs=(vmem, vmem),
+        scratch_shapes=[
+            pltpu.VMEM((8, width), f32),
+            pltpu.VMEM((na - 1, 8, quarter), f32),
+            pltpu.VMEM((nb, 8, quarter + HD), f32),
+        ]
+        + reduce_scratch(na, rows, width)
+        + [pltpu.SemaphoreType.DMA((copies,)), pltpu.SemaphoreType.DMA((copies,))],
+        compiler_params=pltpu.CompilerParams(
+            collective_id=4, has_side_effects=True, vmem_limit_bytes=VMEM_LIMIT
+        ),
+        cost_estimate=pl.CostEstimate(flops=10**8, bytes_accessed=10**8, transcendentals=0),
+        name="last",
+    )(part, grad_res, attn_sums, ffn_sums, head_sums)
 
 
 def reduce_scratch(na, rows, width):
@@ -399,48 +606,6 @@
         pltpu.VMEM((2, rows, 128), f32),
         pltpu.VMEM((HALVES, 4, 8, rows // HALVES), f32),
     ]
-
-
-def reduce_call(mode, nb, part, *operands):
-    na, rows, width = part.shape
-    quarter = width // 4
-    shape = jax.ShapeDtypeStruct
-    full = shape((na, rows, width), bf16)
-    one = shape((1, rows, width), bf16)
-    share = shape((rows, quarter), f32)
-    sums = shape((8, quarter), f32)
-    outs = {
-        "mlp": (full, one, sums),
-        "back": (full, share, sums),
-        "tok": (one, shape((8, quarter + HD), f32)),
-    }[mode]
-    copies = HALVES * (3 * na - 1)
-    if mode == "tok":
-        copies += HALVES * 2 + 1 + na + nb
-        extra = [
-            pltpu.VMEM((8, width), f32),
-            pltpu.VMEM((na - 1, 8, quarter), f32),
-            pltpu.VMEM((nb, 8, quarter + HD), f32),
-        ]
-    else:
-        copies += HALVES * (2 + 3 * na - 1) + (2 if mode == "mlp" else 0)
-        extra = []
-    vmem = pl.BlockSpec(memory_space=pltpu.VMEM)
-    return pl.pallas_call(
-        functools.partial(reduce_kernel, na, nb, mode),
-        out_shape=outs,
-        in_specs=[vmem] * (1 + len(operands)),
-        out_specs=(vmem,) * len(outs),
-        scratch_shapes=reduce_scratch(na, rows, width)
-        + extra
-        + [pltpu.SemaphoreType.DMA((copies,)), pltpu.SemaphoreType.DMA((copies,))],
-        compiler_params=pltpu.CompilerParams(
-            collective_id={"mlp": 2, "back": 3, "tok": 4}[mode],
-            has_side_effects=True,
-            vmem_limit_bytes=VMEM_LIMIT,
-        ),
-        cost_estimate=pl.CostEstimate(flops=10**8, bytes_accessed=10**8, transcendentals=0),
-    )(part, *operands)
 
 
 def enter_kernel(na, nb, *refs):
@@ -583,20 +748,35 @@
 
     lax.fori_loop(0, na, attend, 0)
 
-    def scattered():
-        for k in range(1, na):
-            relay(1, k)
-
-    reduce(
-        na,
-        nb,
-        "attn",
-        links,
-        (part_ref, tok_ref, width_gain_ref),
-        (out, proj_ref, inv_ref, res_ref),
-        scratch,
-        {"scattered": scattered, "spread": lambda: queue(2)},
-    )
+    r = Reduce(na, links, part_ref, out, scratch)
+    for h in range(HALVES):
+        for k in r.lead:
+            r.send_q(h, k)
+    for h in range(HALVES):
+        for k in r.lead:
+            r.send_p(h, k)
+    for h in range(HALVES):
+        for k in r.lead:
+            r.send_a(h, k)
+    for k in range(1, na):
+        relay(1, k)
+    attn_first, attn_second = attn_math(r, tok_ref, width_gain_ref, proj_ref, inv_ref, res_ref)
+    for h in range(HALVES):
+        r.scattered(h, attn_first, 1)
+        r.stats_q(h)
+        r.stats_done(h, 1)
+        r.each(h, attn_second)
+        r.spread(h, range(na))
+    queue(2)
+    for h in range(HALVES):
+        for k in range(na):
+            r.relay_p(h, k)
+    for h in range(HALVES):
+        for k in range(na):
+            r.relay_q(h, k)
+    for h in range(HALVES):
+        for k in range(na):
+            r.arrived(h, k)
     for k in range(1, na):
         relay(2, k)
     for copy in mlp_ends:
@@ -774,29 +954,6 @@
     part_ref[0] = dot_t(grad_ref[0], w_ref[:, : 3 * HD]).astype(bf16)
 
 
-def mlp_kernel(x_ref, w_ref, gu_ref, hidden_ref, part_ref):
-    units = hidden_ref.shape[2]
-    gate_up = dot(x_ref[0], w_ref[:, : 2 * units])
-    gu_ref[0] = gate_up
-    gate, up = gate_up[:, :units], gate_up[:, units:]
-    hidden = (gate * jax.nn.sigmoid(gate) * up).astype(bf16)
-    hidden_ref[0] = hidden
-    part_ref[0] = dot_t(hidden, w_ref[:, 2 * units :]).astype(bf16)
-
-
-def mlp_back_kernel(grad_ref, gu_ref, w_ref, out_ref, part_ref):
-    units = gu_ref.shape[2] // 2
-    grad_hidden = dot(grad_ref[0], w_ref[:, 2 * units :])
-    gate, up = gu_ref[0, :, :units], gu_ref[0, :, units:]
-    sigmoid = jax.nn.sigmoid(gate)
-    active = gate * sigmoid
-    out_ref[0, :, :units] = (
-        grad_hidden * up * (sigmoid * (1.0 + gate * (1.0 - sigmoid)))
-    ).astype(bf16)
-    out_ref[0, :, units:] = (grad_hidden * active).astype(bf16)
-    part_ref[0] = dot_t(out_ref[0], w_ref[:, : 2 * units]).astype(bf16)
-
-
 def widen_kernel(na, count, *refs):
     pieces, out = refs[:na], refs[na]
     a = lax.axis_index("a")
@@ -847,7 +1004,6 @@
     rows, width = tokens.shape
     quarter = width // 4
     w_rows = out_weight.shape[0]
-    units = down_weight.shape[1] // na
 
     def quarter_of(operand):
         return lax.dynamic_slice_in_dim(operand, share * quarter, quarter, 1)
@@ -882,18 +1038,8 @@
     n_d, n_h = attn_gain.shape[0], q_gain.shape[0]
     tables = [(stats, "all"), (head_gain, "all"), (cos_table, "all"), (sine_table, "all")]
     full = (na, rows, width)
-    gate_up, hidden, part = local_call(
-        mlp_kernel,
-        na,
-        [(res_all, "row"), (w_mlp, "all")],
-        [((na, rows, 2 * units), f32, "row"), ((na, rows, units), bf16, "row"), (full, bf16, "row")],
-    )
-    grad_mlp, block_rows, ffn_sums = reduce_call("mlp", nb, part, res_mine, grad_mine, width_gain)
-    grad_gu, part = local_call(
-        mlp_back_kernel,
-        na,
-        [(grad_mlp, "row"), (gate_up, "row"), (w_mlp, "all")],
-        [((na, rows, 2 * units), bf16, "row"), (full, bf16, "row")],
+    grad_mlp, block_rows, hidden, grad_gu, grad_proj, ffn_sums, grad_res, attn_sums = middle_call(
+        res_all, w_mlp, res_mine, grad_mine, proj_mine, inv_mine, width_gain
     )
 
     def weight_grad(left, right):
@@ -912,11 +1058,6 @@
 
     down_sum = reduce_b(weight_grad(grad_mlp, hidden))
     gu_sum = reduce_b(weight_grad(res_all, grad_gu))
-    grad_proj, grad_res, attn_sums = reduce_call(
-        "back", nb, part, grad_mine, proj_mine, inv_mine, width_gain
-    )
-    grad_proj, down_sum, gu_sum = lax.optimization_barrier((grad_proj, down_sum, gu_sum))
-    down_sum = to_owner(down_sum)
     scaled, inner, head_sums = local_call(
         attend_back_kernel,
         na,
@@ -925,17 +1066,19 @@
     )
     out_sum = reduce_b(weight_grad(grad_proj, attended))
     inner = stats_call(na, inner, 7)
-    inner, gu_sum = lax.optimization_barrier((inner, gu_sum))
-    gu_sum = to_owner(gu_sum)
+    inner, down_sum = lax.optimization_barrier((inner, down_sum))
+    down_sum = to_owner(down_sum)
     grad_qkv, part = local_call(
         qkv_back_kernel,
         na,
         [(scaled, "row"), (qkv, "row"), (stats, "all"), (inner, "all"), (w_attn, "all")],
         [((na, rows, 3 * HD), bf16, "row"), (full, bf16, "row")],
     )
+    part, gu_sum = lax.optimization_barrier((part, gu_sum))
+    gu_sum = to_owner(gu_sum)
     qkv_sum = to_owner(reduce_b(weight_grad(x_all, grad_qkv)))
     out_sum = to_owner(out_sum)
-    grad_rows, sums = reduce_call("tok", nb, part, grad_res, attn_sums, ffn_sums, head_sums)
+    grad_rows, sums = last_call(nb, part, grad_res, attn_sums, ffn_sums, head_sums)
     width_sums = lax.dynamic_slice_in_dim(sums[:2, :quarter], b * n_d, n_d, 1)
     head_sums = lax.dynamic_slice_in_dim(sums[:2, quarter:], b * n_h, n_h, 1)
     return (

time: 574 us -> 628 us (1.094)
  waiting for transfers between devices: 43.5 us -> 108 us
  Pallas kernels: 445 us -> 433 us
    ppermute x16, waiting for transfers between devices: 43.5 us -> 108 us  [swap(): return lax.ppermute(operand, axis, [(i, i ^ k) for i in range(n)])]
    pallas_call x4 -> x2, Pallas kernels: 44.7 us -> 20.6 us  [local_call(): pl.pallas_call(kernel, grid=(na,), out_shape=tuple((jax.ShapeDtypeStruct(...]
    pallas_call x3 -> x2, Pallas kernels: 183 us -> 197 us  [the longest x1 156 us: middle_call(): pl.pallas_call(functools.partial(middle_kernel, na), out_shape=outs, in_s...]
    unnamed x37 -> x47, local copies, waits for them, and re-layouts: 10 us -> 14.1 us
  transfers between devices with their start and end apart: 16 -> 16, of which waited for: 2 -> 7; matrix products, arithmetic and copies ran while one was open for 6% -> 4% of each run, Pallas kernels for 27% -> 6%
where the time goes in v4:
time: 628 us; the launch traced here: 618 us
  Pallas kernels  433 us (69%)
  waiting for transfers between devices  108 us (17%)
  local copies, waits for them, and re-layouts  27.6 us (4%)
  matrix products  20.3 us (3%)
  starting transfers between devices  18.4 us (3%)
  other arithmetic  9.48 us (2%)
    pallas_call x1, Pallas kernels, enter_call(): pl.pallas_call(functools.partial(enter_kernel, na, nb), out_shape=tuple(o...  194 us
    pallas_call x1, Pallas kernels, middle_call(): pl.pallas_call(functools.partial(middle_kernel, na), out_shape=outs, in_s...  156 us
    ppermute x16, waiting for transfers between devices, swap(): return lax.ppermute(operand, axis, [(i, i ^ k) for i in range(n)])  108 us
    pallas_call x1, Pallas kernels, last_call(): pl.pallas_call(functools.partial(last_kernel, na, nb), out_shape=(shape((...  41.1 us
    pallas_call x2, Pallas kernels, local_call(): pl.pallas_call(kernel, grid=(na,), out_shape=tuple((jax.ShapeDtypeStruct(...  20.6 us
    dot_general x4, matrix products, weight_grad(): out = jnp.einsum('krd,kru->du', left, right, preferred_element_type=f32)  20.3 us
    ppermute x16, starting transfers between devices, swap(): return lax.ppermute(operand, axis, [(i, i ^ k) for i in range(n)])  18.4 us
    unnamed x47, local copies, waits for them, and re-layouts  14.1 us
  transfers between devices with their start and end apart: 16, of which 7 were waited for; matrix products, arithmetic and copies ran while one was open for 4% of the time, Pallas kernels for 6%

profile of v4, /device:TPU:8, one launch (start us, length us, event | category | flops | bytes accessed | tf_op | source)
XLA Modules:
  0.0 617.9 jit_solution(2310027679447723098)
XLA Ops:
  7.1 193.6 %enter.1 = (bf16[4,256,2048]{2,1,0:T(8,128)(2,1)}, bf16[2048,512]{1,0:T(8,128)(2,1)}, bf16[2048,1536]{1,0:T(8,128)(2,1)}, f32[8,512]{1,0:T(8,128)}, f32[8,128]{1...) custom-call(bf16[256,512]{1,0:T(8,128)(2,1)} %constant_dynamic-slice, ...), custom_call_target="tpu_custom_call" | custom-call | tf_op jit(solution)/shard_map/enter/pallas_call | solution.py:810
  200.6 156.3 %middle.1 = (bf16[4,256,2048]{2,1,0:T(8,128)(2,1)}, bf16[1,256,2048]{2,1,0:T(8,128)(2,1)}, bf16[4,256,512]{2,1,0:T(8,128)(2,1)}, bf16[4,256,1024]{2,1,0:T(8,128)...) custom-call(bf16[4,256,2048]{2,1,0:T(8,128)(2,1)} %get-tuple-element.41.refs_0_, ...), custom_call_target="tpu_custom_call" | custom-call | tf_op jit(solution)/shard_map/middle/pallas_call | solution.py:491
  356.9 4.9 bitcast_convert_fusion.1
  364.2 7.0 %bitcast_convert_fusion = bf16[2048,1024]{1,0:T(8,128)(2,1)S(1)} fusion(bf16[4,256,2048]{2,1,0:T(8,128)(2,1)} %get-tuple-element.41.refs_0_, bf16[4,256,1024]{2,1,0:T(8,128)(2,1)S(1)} %copy-done.21), kind=kOutput, calls=%fused_computation | convolution fusion | flops 4297064448 | bytes 10485760 | tf_op jit(solution)/shard_map/krd,kru->du/dot_general | solution.py:1046
  374.5 12.1 %shard_map.177 = (f32[4,256,384]{2,1,0:T(8,128)}, f32[8,256]{1,0:T(8,128)}, f32[8,128]{1,0:T(8,128)}) custom-call(bf16[4,256,2048]{2,1,0:T(8,128)(2,1)} %get-tuple-element.48.proj_ref, f32[4,256,384]{2,1,0:T(8,128)} %get-tuple-element.49.qkv_ref, f32[8,256]{1,0:T(8,128)} %get-tuple-element.50.stats_ref, f32[8,128]{1,0:T(8,128)} %get-tuple-element.51.gain_ref, ...), custom_call_target="tpu_custom_call" | custom-call | flops 1000000000 | bytes 20000000 | tf_op jit(solution)/shard_map/pallas_call | solution.py:889
  386.6 10.1 %shard_map.178.inner_ref = f32[8,256]{1,0:T(8,128)} custom-call(f32[8,256]{1,0:T(8,128)} %get-tuple-element.54.stats_ref), custom_call_target="tpu_custom_call" | custom-call | tf_op jit(solution)/shard_map/pallas_call | solution.py:866
  396.7 3.6 fusion.1
  401.9 8.5 %shard_map.179 = (bf16[4,256,384]{2,1,0:T(8,128)(2,1)}, bf16[4,256,2048]{2,1,0:T(8,128)(2,1)}) custom-call(f32[4,256,384]{2,1,0:T(8,128)} %get-tuple-element.53.scaled_ref, f32[4,256,384]{2,1,0:T(8,128)} %get-tuple-element.49.qkv_ref, f32[8,256]{1,0:T(8,128)} %get-tuple-element.50.stats_ref, f32[8,256]{1,0:T(8,128)} %shard_map.178.inner_ref, ...), custom_call_target="tpu_custom_call" | custom-call | flops 1000000000 | bytes 20000000 | tf_op jit(solution)/shard_map/pallas_call | solution.py:889
  410.5 4.8 bitcast_convert_fusion.2
  419.5 35.5 %collective-permute-done.6 = bf16[4,256,128]{2,1,0:T(8,128)(2,1)S(1)} collective-permute-done((bf16[4,256,128]{2,1,0:T(8,128)(2,1)S(1)}, bf16[4,256,128]{2,1,0:T(8,128)(2,1)S(1)}, u32[]{:S(2)}, u32[]{:S(2)}) %collective-permute-start.6) | collective-permute-done | bytes 262176 | tf_op jit(solution)/shard_map/ppermute | solution.py:43
  455.7 4.4 collective-permute-start.8
  461.7 3.0 collective-permute-start.9
  465.5 20.1 %collective-permute-done.9.refs_3_ = bf16[256,128]{1,0:T(8,128)(2,1)S(1)} collective-permute-done((bf16[256,128]{1,0:T(8,128)(2,1)S(1)}, bf16[256,128]{1,0:T(8,128)(2,1)S(1)}, u32[]{:S(2)}, u32[]{:S(2)}) %collective-permute-start.9) | collective-permute-done | bytes 65568 | tf_op jit(solution)/shard_map/ppermute | solution.py:43
  493.1 6.6 %collective-permute-done.15.refs_3_ = bf16[256,512]{1,0:T(8,128)(2,1)S(1)} collective-permute-done((bf16[256,512]{1,0:T(8,128)(2,1)S(1)}, bf16[256,512]{1,0:T(8,128)(2,1)S(1)}, u32[]{:S(2)}, u32[]{:S(2)}) %collective-permute-start.15) | collective-permute-done | bytes 262176 | tf_op jit(solution)/shard_map/ppermute | solution.py:43
  500.3 2.6 shard_map.183
  503.0 3.2 collective-permute-done.5.refs_3_
  506.9 2.6 shard_map.180
  509.5 3.2 fusion
  512.7 41.1 %last.1 = (bf16[1,256,2048]{2,1,0:T(8,128)(2,1)}, f32[8,640]{1,0:T(8,128)}) custom-call(bf16[4,256,2048]{2,1,0:T(8,128)(2,1)} %get-tuple-element.60.part_ref, f32[256,512]{1,0:T(8,128)} %get-tuple-element.61.grad_ref, f32[8,512]{1,0:T(8,128)} %get-tuple-element.62.attn_sum_ref, f32[8,512]{1,0:T(8,128)} %get-tuple-element.63.ffn_sum_ref, ...), custom_call_target="tpu_custom_call" | custom-call | flops 100000000 | bytes 100000000 | tf_op jit(solution)/shard_map/last/pallas_call | solution.py:576
  562.6 18.3 %collective-permute-done.10.refs_1_ = bf16[256,1024]{1,0:T(8,128)(2,1)S(1)} collective-permute-done((bf16[256,1024]{1,0:T(8,128)(2,1)S(1)}, bf16[256,1024]{1,0:T(8,128)(2,1)S(1)}, u32[]{:S(2)}, u32[]{:S(2)}) %collective-permute-start.10) | collective-permute-done | bytes 524320 | tf_op jit(solution)/shard_map/ppermute | solution.py:43
  580.9 13.7 %collective-permute-done.11.refs_2_ = bf16[256,1024]{1,0:T(8,128)(2,1)S(1)} collective-permute-done((bf16[256,1024]{1,0:T(8,128)(2,1)S(1)}, bf16[256,1024]{1,0:T(8,128)(2,1)S(1)}, u32[]{:S(2)}, u32[]{:S(2)}) %collective-permute-start.11) | collective-permute-done | bytes 524320 | tf_op jit(solution)/shard_map/ppermute | solution.py:43
  594.6 11.0 %collective-permute-done.12.refs_3_ = bf16[256,1024]{1,0:T(8,128)(2,1)S(1)} collective-permute-done((bf16[256,1024]{1,0:T(8,128)(2,1)S(1)}, bf16[256,1024]{1,0:T(8,128)(2,1)S(1)}, u32[]{:S(2)}, u32[]{:S(2)}) %collective-permute-start.12) | collective-permute-done | bytes 524320 | tf_op jit(solution)/shard_map/ppermute | solution.py:43
  606.4 3.8 shard_map.182
  610.2 7.6 %copy.28 = f32[256,2,2048]{2,1,0:T(2,128)} copy(f32[256,2,2048]{2,0,1:T(8,128)} %bitcast.101) | data formatting | bytes 8388608
  (95 shorter events, 39.2 us)
Async XLA Ops:
  361.9 38.5 %collective-permute-start = (bf16[4,256,512]{2,1,0:T(8,128)(2,1)S(1)}, bf16[4,256,512]{2,1,0:T(8,128)(2,1)}, u32[]{:S(2)}, u32[]{:S(2)}) collective-permute-start(bf16[4,256,512]{2,1,0:T(8,128)(2,1)S(1)} %dynamic-slice_bitcast_fusion.1), channel_id=1, source_target_pairs={{0,4},{4,0},{1,5},{5,1},{2,6},{6,2},{3,7},{7,3},{8,12},{12,8},{9,1... | collective-permute-start | bytes 3145736 | tf_op jit(solution)/shard_map/ppermute | solution.py:43
  373.9 135.6 %collective-permute-start.1 = (bf16[4,256,1024]{2,1,0:T(8,128)(2,1)}, bf16[4,256,1024]{2,1,0:T(8,128)(2,1)}, u32[]{:S(2)}, u32[]{:S(2)}) collective-permute-start(bf16[4,256,1024]{2,1,0:T(8,128)(2,1)} %dynamic-slice_bitcast_fusion), channel_id=1, source_target_pairs={{0,4},{4,0},{1,5},{5,1},{2,6},{6,2},{3,7},{7,3},{8,12},{12,8},{9,1... | collective-permute-start | bytes 6291464 | tf_op jit(solution)/shard_map/ppermute | solution.py:43
  374.5 22.2 %copy-start.22 = (bf16[4,256,128]{2,1,0:T(8,128)(2,1)S(1)}, bf16[4,256,128]{2,1,0:T(8,128)(2,1)}, u32[]{:S(2)}) copy-start(bf16[4,256,128]{2,1,0:T(8,128)(2,1)} %get-tuple-element.68) | copy-start | bytes 786436
  417.4 43.5 %collective-permute-start.2 = (bf16[4,256,384]{2,1,0:T(8,128)(2,1)}, bf16[4,256,384]{2,1,0:T(8,128)(2,1)S(1)}, u32[]{:S(2)}, u32[]{:S(2)}) collective-permute-start(bf16[4,256,384]{2,1,0:T(8,128)(2,1)} %dynamic-slice_bitcast_fusion.2), channel_id=1, source_target_pairs={{0,4},{4,0},{1,5},{5,1},{2,6},{6,2},{3,7},{7,3},{8,12},{12,8},{9,1... | collective-permute-start | bytes 2359304 | tf_op jit(solution)/shard_map/ppermute | solution.py:43
  419.1 35.9 %collective-permute-start.6 = (bf16[4,256,128]{2,1,0:T(8,128)(2,1)S(1)}, bf16[4,256,128]{2,1,0:T(8,128)(2,1)S(1)}, u32[]{:S(2)}, u32[]{:S(2)}) collective-permute-start(bf16[4,256,128]{2,1,0:T(8,128)(2,1)S(1)} %dynamic-slice_bitcast_fusion.11), channel_id=1, source_target_pairs={{0,4},{4,0},{1,5},{5,1},{2,6},{6,2},{3,7},{7,3},{8,12},{12,8},{9,1... | collective-permute-start | bytes 786440 | tf_op jit(solution)/shard_map/ppermute | solution.py:43
  419.5 42.0 %copy-start.6 = (bf16[2048,384]{1,0:T(8,128)(2,1)S(1)}, bf16[2048,384]{1,0:T(8,128)(2,1)}, u32[]{:S(2)}) copy-start(bf16[2048,384]{1,0:T(8,128)(2,1)} %copy-done.5) | copy-start | bytes 4718596
  455.7 6.0 collective-permute-start.7
  455.7 9.7 %collective-permute-start.8 = (bf16[256,128]{1,0:T(8,128)(2,1)S(1)}, bf16[256,128]{1,0:T(8,128)(2,1)S(1)}, u32[]{:S(2)}, u32[]{:S(2)}) collective-permute-start(bf16[256,128]{1,0:T(8,128)(2,1)S(1)} %get-tuple-element.95), channel_id=1, source_target_pairs={{0,16},{8,24},{16,0},{24,8},{1,17},{9,25},{17,1},{25,9},{2,18},{10... | collective-permute-start | bytes 196616 | tf_op jit(solution)/shard_map/ppermute | solution.py:43
  460.9 28.8 %copy-start.7 = (bf16[1,256,2048]{2,1,0:T(8,128)(2,1)S(1)}, bf16[1,256,2048]{2,1,0:T(8,128)(2,1)}, u32[]{:S(2)}) copy-start(bf16[1,256,2048]{2,1,0:T(8,128)(2,1)} %get-tuple-element.47) | copy-start | bytes 3145732
  460.9 25.3 %collective-permute-start.13 = (bf16[256,512]{1,0:T(8,128)(2,1)S(1)}, bf16[256,512]{1,0:T(8,128)(2,1)S(1)}, u32[]{:S(2)}, u32[]{:S(2)}) collective-permute-start(bf16[256,512]{1,0:T(8,128)(2,1)S(1)} %get-tuple-element.88), channel_id=1, source_target_pairs={{0,8},{8,0},{16,24},{24,16},{1,9},{9,1},{17,25},{25,17},{2,10},{10... | collective-permute-start | bytes 786440 | tf_op jit(solution)/shard_map/ppermute | solution.py:43
  460.9 26.3 %collective-permute-start.14 = (bf16[256,512]{1,0:T(8,128)(2,1)S(1)}, bf16[256,512]{1,0:T(8,128)(2,1)S(1)}, u32[]{:S(2)}, u32[]{:S(2)}) collective-permute-start(bf16[256,512]{1,0:T(8,128)(2,1)S(1)} %get-tuple-element.87), channel_id=1, source_target_pairs={{0,16},{8,24},{16,0},{24,8},{1,17},{9,25},{17,1},{25,9},{2,18},{10... | collective-permute-start | bytes 786440 | tf_op jit(solution)/shard_map/ppermute | solution.py:43
  461.7 29.6 %copy-start.18 = (bf16[256,128]{1,0:T(8,128)(2,1)}, bf16[256,128]{1,0:T(8,128)(2,1)S(1)}, u32[]{:S(2)}) copy-start(bf16[256,128]{1,0:T(8,128)(2,1)S(1)} %collective-permute-done.7.refs_1_) | copy-start | bytes 196612
  461.7 23.9 %collective-permute-start.9 = (bf16[256,128]{1,0:T(8,128)(2,1)S(1)}, bf16[256,128]{1,0:T(8,128)(2,1)S(1)}, u32[]{:S(2)}, u32[]{:S(2)}) collective-permute-start(bf16[256,128]{1,0:T(8,128)(2,1)S(1)} %get-tuple-element.94), channel_id=1, source_target_pairs={{0,24},{8,16},{16,8},{24,0},{1,25},{9,17},{17,9},{25,1},{2,26},{10... | collective-permute-start | bytes 196616 | tf_op jit(solution)/shard_map/ppermute | solution.py:43
  465.4 25.8 %copy-start.19 = (bf16[256,128]{1,0:T(8,128)(2,1)}, bf16[256,128]{1,0:T(8,128)(2,1)S(1)}, u32[]{:S(2)}) copy-start(bf16[256,128]{1,0:T(8,128)(2,1)S(1)} %collective-permute-done.8.refs_2_) | copy-start | bytes 196612
  465.4 34.2 %collective-permute-start.15 = (bf16[256,512]{1,0:T(8,128)(2,1)S(1)}, bf16[256,512]{1,0:T(8,128)(2,1)S(1)}, u32[]{:S(2)}, u32[]{:S(2)}) collective-permute-start(bf16[256,512]{1,0:T(8,128)(2,1)S(1)} %get-tuple-element.86), channel_id=1, source_target_pairs={{0,24},{8,16},{16,8},{24,0},{1,25},{9,17},{17,9},{25,1},{2,26},{10... | collective-permute-start | bytes 786440 | tf_op jit(solution)/shard_map/ppermute | solution.py:43
  486.2 16.8 %collective-permute-start.3 = (bf16[256,384]{1,0:T(8,128)(2,1)S(1)}, bf16[256,384]{1,0:T(8,128)(2,1)S(1)}, u32[]{:S(2)}, u32[]{:S(2)}) collective-permute-start(bf16[256,384]{1,0:T(8,128)(2,1)S(1)} %get-tuple-element.92), channel_id=1, source_target_pairs={{0,8},{8,0},{16,24},{24,16},{1,9},{9,1},{17,25},{25,17},{2,10},{10... | collective-permute-start | bytes 589832 | tf_op jit(solution)/shard_map/ppermute | solution.py:43
  486.2 13.4 %copy-start.12 = (bf16[256,512]{1,0:T(8,128)(2,1)}, bf16[256,512]{1,0:T(8,128)(2,1)S(1)}, u32[]{:S(2)}) copy-start(bf16[256,512]{1,0:T(8,128)(2,1)S(1)} %collective-permute-done.13.refs_1_) | copy-start | bytes 786436
  486.2 16.8 %collective-permute-start.4 = (bf16[256,384]{1,0:T(8,128)(2,1)S(1)}, bf16[256,384]{1,0:T(8,128)(2,1)S(1)}, u32[]{:S(2)}, u32[]{:S(2)}) collective-permute-start(bf16[256,384]{1,0:T(8,128)(2,1)S(1)} %get-tuple-element.91), channel_id=1, source_target_pairs={{0,16},{8,24},{16,0},{24,8},{1,17},{9,25},{17,1},{25,9},{2,18},{10... | collective-permute-start | bytes 589832 | tf_op jit(solution)/shard_map/ppermute | solution.py:43
  487.2 12.4 %copy-start.13 = (bf16[256,512]{1,0:T(8,128)(2,1)}, bf16[256,512]{1,0:T(8,128)(2,1)S(1)}, u32[]{:S(2)}) copy-start(bf16[256,512]{1,0:T(8,128)(2,1)S(1)} %collective-permute-done.14.refs_2_) | copy-start | bytes 786436
  487.2 19.0 %collective-permute-start.5 = (bf16[256,384]{1,0:T(8,128)(2,1)S(1)}, bf16[256,384]{1,0:T(8,128)(2,1)S(1)}, u32[]{:S(2)}, u32[]{:S(2)}) collective-permute-start(bf16[256,384]{1,0:T(8,128)(2,1)S(1)} %get-tuple-element.90), channel_id=1, source_target_pairs={{0,24},{8,16},{16,8},{24,0},{1,25},{9,17},{17,9},{25,1},{2,26},{10... | collective-permute-start | bytes 589832 | tf_op jit(solution)/shard_map/ppermute | solution.py:43
  556.3 24.6 %collective-permute-start.10 = (bf16[256,1024]{1,0:T(8,128)(2,1)S(1)}, bf16[256,1024]{1,0:T(8,128)(2,1)S(1)}, u32[]{:S(2)}, u32[]{:S(2)}) collective-permute-start(bf16[256,1024]{1,0:T(8,128)(2,1)S(1)} %get-tuple-element.84), channel_id=1, source_target_pairs={{0,8},{8,0},{16,24},{24,16},{1,9},{9,1},{17,25},{25,17},{2,10},{10... | collective-permute-start | bytes 1572872 | tf_op jit(solution)/shard_map/ppermute | solution.py:43
  558.1 36.4 %collective-permute-start.11 = (bf16[256,1024]{1,0:T(8,128)(2,1)S(1)}, bf16[256,1024]{1,0:T(8,128)(2,1)S(1)}, u32[]{:S(2)}, u32[]{:S(2)}) collective-permute-start(bf16[256,1024]{1,0:T(8,128)(2,1)S(1)} %get-tuple-element.83), channel_id=1, source_target_pairs={{0,16},{8,24},{16,0},{24,8},{1,17},{9,25},{17,1},{25,9},{2,18},{10... | collective-permute-start | bytes 1572872 | tf_op jit(solution)/shard_map/ppermute | solution.py:43
  559.8 45.8 %collective-permute-start.12 = (bf16[256,1024]{1,0:T(8,128)(2,1)S(1)}, bf16[256,1024]{1,0:T(8,128)(2,1)S(1)}, u32[]{:S(2)}, u32[]{:S(2)}) collective-permute-start(bf16[256,1024]{1,0:T(8,128)(2,1)S(1)} %get-tuple-element.82), channel_id=1, source_target_pairs={{0,24},{8,16},{16,8},{24,0},{1,25},{9,17},{17,9},{25,1},{2,26},{10... | collective-permute-start | bytes 1572872 | tf_op jit(solution)/shard_map/ppermute | solution.py:43
  580.9 24.7 %copy-start.9 = (bf16[256,1024]{1,0:T(8,128)(2,1)}, bf16[256,1024]{1,0:T(8,128)(2,1)S(1)}, u32[]{:S(2)}) copy-start(bf16[256,1024]{1,0:T(8,128)(2,1)S(1)} %collective-permute-done.10.refs_1_) | copy-start | bytes 1572868
  (15 other events, 57.6 us)

commit v5 on v4

--- a/solution.py
+++ b/solution.py
@@ -6,7 +6,6 @@
 from jax.experimental import pallas as pl
 from jax.experimental.pallas import tpu as pltpu
 from jax.sharding import Mesh, PartitionSpec as P
-
 
 HEADS = 16
 HD = 128
@@ -68,6 +67,13 @@
         self.count += 1
         self.copies.append(copy)
         return copy
+
+    def sent(self, copies):
+        done = [id(copy) for copy in copies]
+        for copy in self.copies:
+            if id(copy) in done:
+                copy.wait_send()
+        self.copies = [copy for copy in self.copies if id(copy) not in done]
 
     def finish(self):
         for copy in self.copies:
@@ -151,6 +157,42 @@
     return queries, key_rows, values, q_inv, k_inv, q_rot, k_rot, probs
 
 
+def weight_grad(left, right, out, block):
+    na, nb = left.shape[0], out.shape[1]
+    rows = out.shape[2]
+    total = None
+    for k in range(na):
+        term = t_dot(left[k, :, block * nb * rows : (block + 1) * nb * rows], right[k])
+        total = term if total is None else total + term
+    for j in range(nb):
+        out[block, j] = total[j * rows : (j + 1) * rows].astype(bf16)
+
+
+def exchange_b(links, grad, held, columns):
+    b = lax.axis_index("b")
+    return [
+        links.send(
+            grad.at[:, across(b, j), :, columns], held.at[j - 1, :, :, columns], {"b": across(b, j)}
+        )
+        for j in range(1, held.shape[0] + 1)
+    ]
+
+
+def sum_b(copies, grad, held, out, columns):
+    b = lax.axis_index("b")
+    for copy in copies:
+        copy.wait_recv()
+
+    def add(block, carry):
+        total = grad[block, b, :, columns].astype(f32)
+        for j in range(held.shape[0]):
+            total = total + held[j, block, :, columns].astype(f32)
+        out[block, :, columns] = total.astype(bf16)
+        return carry
+
+    lax.fori_loop(0, grad.shape[0], add, 0)
+
+
 class Reduce:
     def __init__(self, na, links, part, out, scratch):
         self.na, self.links, self.part, self.out = na, links, part, out
@@ -328,18 +370,18 @@
     return first, second
 
 
-def middle_kernel(na, *refs):
+def middle_kernel(na, nb, *refs):
     x_ref, w_ref, res_ref, grad_ref, proj_ref, inv_ref, gain_ref = refs[:7]
-    out, block_ref, hidden_ref, grad_gu_ref, back_out = refs[7:12]
-    ffn_sum_ref, grad_res_ref, attn_sum_ref = refs[12:15]
-    gu_ref, part_ref, back_part_ref = refs[15:18]
-    scratch, (send_sem, recv_sem) = refs[18:-2], refs[-2:]
+    block_ref, back_out, ffn_sum_ref, grad_res_ref, attn_sum_ref, down_sum_ref, gu_grad_ref = refs[7:14]
+    out, hidden_ref, grad_gu_ref, gu_ref, part_ref, down_grad, down_held = refs[14:21]
+    scratch, (send_sem, recv_sem) = refs[21:-2], refs[-2:]
     units = hidden_ref.shape[2]
     width = x_ref.shape[2]
-    greet(reduce_peers(na))
+    b = lax.axis_index("b")
+    greet(reduce_peers(na) + [{"b": across(b, j)} for j in range(1, nb)])
     links = Links(send_sem, recv_sem)
     r = Reduce(na, links, part_ref, out, scratch[:9])
-    s = Reduce(na, links, back_part_ref, back_out, scratch[9:])
+    s = Reduce(na, links, part_ref, back_out, scratch[9:])
     ffn_sum_ref[...] = jnp.zeros_like(ffn_sum_ref)
     attn_sum_ref[...] = jnp.zeros_like(attn_sum_ref)
     wide_tile = 512
@@ -383,7 +425,7 @@
 
         def back(n, carry):
             at = span(n, wide_tile)
-            back_part_ref[k, rows, at] = dot_t(
+            part_ref[k, rows, at] = dot_t(
                 grad_gu_ref[k, rows], w_ref[at, : 2 * units]
             ).astype(bf16)
             return carry
@@ -398,18 +440,22 @@
         if i:
             r.send_p(0, lead[i - 1])
     r.send_p(0, lead[-1])
-    for k in lead:
+    r.send_p(1, lead[0])
+    r.send_a(0, lead[0])
+    r.send_p(1, lead[1])
+    for k in lead[1:]:
         r.send_a(0, k)
+    first, second = mlp_math(r, res_ref, grad_ref, gain_ref, block_ref, ffn_sum_ref)
+    r.scattered(0, first, 2)
+    for k in lead[2:]:
         r.send_p(1, k)
-    first, second = mlp_math(r, res_ref, grad_ref, gain_ref, block_ref, ffn_sum_ref)
     for k in lead[:-2]:
         r.send_a(1, k)
-    r.scattered(0, first, 2)
-    r.send_a(1, lead[-2])
     r.stats_q(0)
     r.stats_done(0, 2)
     r.each(0, second)
     r.spread(0, lead)
+    r.send_a(1, lead[-2])
     r.scattered(1, first, 2)
     r.relay_q(0, 0)
     r.stats_q(1)
@@ -419,6 +465,7 @@
     r.spread(1, lead)
     here = block_ref.at[0, :, r.mine]
     block_p = links.send(here, here, {"p": 1 - r.p})
+    links.sent(r.step_q.values())
     backward(0, 0)
     s.send_q(0, 0)
     r.relay_q(1, 0)
@@ -435,35 +482,47 @@
     back_first, back_second = back_math(
         s, grad_ref, proj_ref, inv_ref, gain_ref, grad_res_ref, attn_sum_ref
     )
-    for i in range(steps + 4):
-        if 0 <= i - 4 < steps:
-            s.send_a(*order[i - 4])
+    for i in range(steps + 3):
         if 0 <= i - 3 < steps:
-            s.send_p(*order[i - 3])
+            s.send_a(*order[i - 3])
+        if i == steps + 1:
+            s.scattered(0, back_first, 1)
         if 0 <= i - 2 < steps:
-            r.arrived(*order[i - 2])
-            backward(*order[i - 2])
-            s.send_q(*order[i - 2])
+            s.send_p(*order[i - 2])
         if 0 <= i - 1 < steps:
             r.relay_q(*order[i - 1])
+            r.arrived(*order[i - 1])
+            backward(*order[i - 1])
+            s.send_q(*order[i - 1])
         if i < steps:
             r.relay_p(*order[i])
-    s.scattered(0, back_first, 1)
     s.stats_q(0)
+    for block in range(na):
+        weight_grad(out, hidden_ref, down_grad, block)
+    columns = slice(0, units)
+    down_copies = exchange_b(links, down_grad, down_held, columns)
     s.stats_done(0, 1)
     s.each(0, back_second)
     s.spread(0, lead)
     s.scattered(1, back_first, 1)
+    weight_grad(x_ref, grad_gu_ref, gu_grad_ref, 0)
     s.relay_q(0, 0)
     s.stats_q(1)
+    weight_grad(x_ref, grad_gu_ref, gu_grad_ref, 1)
     s.stats_done(1, 1)
     s.each(1, back_second)
     s.spread(1, lead)
-    for h, k in order:
+    weight_grad(x_ref, grad_gu_ref, gu_grad_ref, 2)
+    late = [(0, 0)] + order
+    for i, (h, k) in enumerate(order):
         s.relay_p(h, k)
+        if i == 1:
+            weight_grad(x_ref, grad_gu_ref, gu_grad_ref, 3)
+        if i:
+            s.relay_q(*late[i])
     s.relay_q(1, 0)
-    for h, k in order:
-        s.relay_q(h, k)
+    s.relay_q(*order[-1])
+    sum_b(down_copies, down_grad, down_held, down_sum_ref, columns)
     for h in range(HALVES):
         for k in range(na):
             s.arrived(h, k)
@@ -471,32 +530,35 @@
     links.finish()
 
 
-def middle_call(x_all, w_mlp, res_mine, grad_mine, proj_mine, inv_mine, width_gain):
+def middle_call(nb, x_all, w_mlp, res_mine, grad_mine, proj_mine, inv_mine, width_gain):
     na, rows, width = x_all.shape
     quarter, units = width // 4, w_mlp.shape[1] // 3
+    w_rows = width // (na * nb)
     vmem = pl.BlockSpec(memory_space=pltpu.VMEM)
     shape = jax.ShapeDtypeStruct
-    full = shape((na, rows, width), bf16)
     outs = (
-        full,
         shape((1, rows, width), bf16),
-        shape((na, rows, units), bf16),
-        shape((na, rows, 2 * units), bf16),
-        full,
+        shape((na, rows, width), bf16),
         shape((8, quarter), f32),
         shape((rows, quarter), f32),
         shape((8, quarter), f32),
-    )
-    copies = 2 * HALVES * (6 * na + 1) + 2
+        shape((na, w_rows, units), bf16),
+        shape((na, nb, w_rows, 2 * units), bf16),
+    )
+    copies = 2 * HALVES * (6 * na + 1) + 2 + nb
     return pl.pallas_call(
-        functools.partial(middle_kernel, na),
+        functools.partial(middle_kernel, na, nb),
         out_shape=outs,
         in_specs=[vmem] * 7,
         out_specs=(vmem,) * len(outs),
         scratch_shapes=[
+            pltpu.VMEM((na, rows, width), bf16),
+            pltpu.VMEM((na, rows, units), bf16),
+            pltpu.VMEM((na, rows, 2 * units), bf16),
             pltpu.VMEM((na, rows, 2 * units), f32),
             pltpu.VMEM((na, rows, width), bf16),
-            pltpu.VMEM((na, rows, width), bf16),
+            pltpu.VMEM((na, nb, w_rows, units), bf16),
+            pltpu.VMEM((nb - 1, na, w_rows, units), bf16),
         ]
         + reduce_scratch(na, rows, width)
         + reduce_scratch(na, rows, width)
@@ -508,29 +570,115 @@
     )(x_all, w_mlp, res_mine, grad_mine, proj_mine, inv_mine, width_gain)
 
 
-def last_kernel(na, nb, part_ref, grad_ref, attn_sum_ref, ffn_sum_ref, head_sum_ref, out, sums_ref, *refs):
-    own_sums, a_sums, b_sums = refs[:3]
-    scratch, (send_sem, recv_sem) = refs[3:-2], refs[-2:]
+def last_kernel(na, nb, *refs):
+    proj_ref, x_ref, qkv_ref, stats_ref, gain_ref, cos_ref, sin_ref, w_ref, att_ref = refs[:9]
+    grad_ref, attn_sum_ref, ffn_sum_ref, down_sum_ref, gu_grad_ref = refs[9:14]
+    out, sums_ref, down_out, gu_out, qkv_out, wout_out = refs[14:20]
+    scaled_ref, grad_qkv_ref, part_ref, head_sums, held, stats_a, inner_ref = refs[20:27]
+    own_sums, a_sums, b_sums, gu_held, gu_sum, attn_grad, attn_held, attn_sum = refs[27:35]
+    down_in, gu_in, attn_in = refs[35:38]
+    scratch, (send_sem, recv_sem) = refs[38:-2], refs[-2:]
     links = Links(send_sem, recv_sem)
     r = Reduce(na, links, part_ref, out, scratch)
     a, b, p, q, mine, pair, quarter = (
         r.a, lax.axis_index("b"), r.p, r.q, r.mine, r.pair, r.quarter,
     )
+    units = down_sum_ref.shape[2]
     own_sums[...] = jnp.zeros_like(own_sums)
     own_sums[0:1, mine] = jnp.sum(attn_sum_ref[...], axis=0, keepdims=True)
     own_sums[1:2, mine] = jnp.sum(ffn_sum_ref[...], axis=0, keepdims=True)
     greet(reduce_peers(na) + [{"b": across(b, j)} for j in range(1, nb)])
+    far = list(range(2, na)) + [1]
+
+    def to_owners(source, target, columns):
+        return [
+            (k, links.send(
+                source.at[across(a, k), :, columns], target.at[k - 1, :, columns], {"a": across(a, k)}
+            ))
+            for k in far
+        ]
+
+    whole = slice(0, units)
+    halves = [slice(0, units), slice(units, 2 * units)]
+    down_copies = to_owners(down_sum_ref, down_in, whole)
+    gu_b = [exchange_b(links, gu_grad_ref, gu_held, columns) for columns in halves]
     here = own_sums.at[:, mine]
     sums_p = links.send(here, here, {"p": 1 - p})
-    for h in range(HALVES):
-        for k in r.lead:
-            r.send_q(h, k)
-    for h in range(HALVES):
-        for k in r.lead:
-            r.send_p(h, k)
+
+    held[0] = jnp.zeros_like(held[0])
+    head_sums[...] = jnp.zeros_like(head_sums)
+
+    def attend_back(k, carry):
+        queries, key_rows, values, q_inv, k_inv, q_rot, k_rot, probs = attention(
+            k, qkv_ref[k], stats_ref[...], gain_ref, cos_ref, sin_ref
+        )
+        cos_table, sine_table = cos_ref[...], sin_ref[...]
+        grad_att = dot(proj_ref[k], w_ref[:, 3 * HD :]).astype(bf16)
+        grad_v = t_dot(probs.astype(bf16), grad_att)
+        grad_p = dot_t(grad_att, values)
+        delta = jnp.sum(probs * grad_p, axis=1, keepdims=True)
+        grad_scores = (probs * (grad_p - delta) * HD ** (-0.5)).astype(bf16)
+        grad_q = dot(grad_scores, k_rot)
+        grad_k = t_dot(grad_scores, q_rot)
+        grad_q = grad_q * cos_table + rotate_back(grad_q * sine_table)
+        grad_k = grad_k * cos_table + rotate_back(grad_k * sine_table)
+        head_sums[0:1] += jnp.sum(grad_q * queries * q_inv, axis=0, keepdims=True)
+        head_sums[1:2] += jnp.sum(grad_k * key_rows * k_inv, axis=0, keepdims=True)
+        scaled_q = grad_q * gain_ref[0:1]
+        scaled_k = grad_k * gain_ref[1:2]
+        scaled_ref[k, :, :HD] = scaled_q
+        scaled_ref[k, :, HD:] = scaled_k
+        grad_qkv_ref[k, :, 2 * HD :] = grad_v.astype(bf16)
+        held[0] += to_row(scaled_q * queries, 2 * k) + to_row(scaled_k * key_rows, 2 * k + 1)
+        return carry
+
+    lax.fori_loop(0, na, attend_back, 0)
     sums_p.wait_recv()
     here = own_sums.at[:, pair]
     sums_q = links.send(here, here, {"q": 1 - q})
+    gu_copies = []
+
+    def sent():
+        for block in range(na):
+            total = None
+            for k in range(na):
+                term = t_dot(proj_ref[k, :, block * quarter : (block + 1) * quarter], att_ref[k])
+                total = term if total is None else total + term
+            rows = attn_grad.shape[2]
+            for j in range(nb):
+                attn_grad[block, j, :, 3 * HD :] = total[j * rows : (j + 1) * rows].astype(bf16)
+        sum_b(gu_b[0], gu_grad_ref, gu_held, gu_sum, halves[0])
+        gu_copies.append(to_owners(gu_sum, gu_in, halves[0]))
+
+    add_over_heads(links, na, a, p, q, held, stats_a, inner_ref, sent)
+
+    def qkv_back(k, carry):
+        for i in range(2):
+            at = slice(i * HD, (i + 1) * HD)
+            inv = lax.rsqrt(to_column(stats_ref[...] / HQ, 2 * k + i) + epsilon)
+            mean = to_column(inner_ref[...] / HQ, 2 * k + i)
+            grad = inv * scaled_ref[k, :, at] - qkv_ref[k, :, at] * inv * inv * inv * mean
+            grad_qkv_ref[k, :, at] = grad.astype(bf16)
+        part_ref[k] = dot_t(grad_qkv_ref[k], w_ref[:, : 3 * HD]).astype(bf16)
+        return carry
+
+    for k in r.lead:
+        qkv_back(k, 0)
+        for h in range(HALVES):
+            r.send_q(h, k)
+    for h in range(HALVES):
+        for k in r.lead:
+            r.send_p(h, k)
+    for block in range(na):
+        total = None
+        for k in range(na):
+            term = t_dot(x_ref[k, :, block * quarter : (block + 1) * quarter], grad_qkv_ref[k])
+            total = term if total is None else total + term
+        rows = attn_grad.shape[2]
+        for j in range(nb):
+            attn_grad[block, j, :, : 3 * HD] = total[j * rows : (j + 1) * rows].astype(bf16)
+    attn_columns = slice(0, 4 * HD)
+    attn_b = exchange_b(links, attn_grad, attn_held, attn_columns)
     for h in range(HALVES):
         for k in r.lead:
             r.send_a(h, k)
@@ -539,6 +687,8 @@
         links.send(own_sums.at[:, span(across(a, k), quarter)], a_sums.at[k - 1], {"a": across(a, k)})
         for k in range(1, na)
     ]
+    sum_b(gu_b[1], gu_grad_ref, gu_held, gu_sum, halves[1])
+    gu_copies.append(to_owners(gu_sum, gu_in, halves[1]))
 
     def first(at):
         out[0, at, mine] = (grad_ref[at] + r.add_all(at)).astype(bf16)
@@ -548,49 +698,96 @@
         r.spread(h, [0])
     for copy in sums_a:
         copy.wait_recv()
-    held = own_sums[:, span(a, quarter)]
+    total = own_sums[:, span(a, quarter)]
     for k in range(1, na):
-        held = held + a_sums[k - 1]
-    b_sums[0, :, :quarter] = held
-    b_sums[0, :, quarter:] = head_sum_ref[...]
+        total = total + a_sums[k - 1]
+    b_sums[0, :, :quarter] = total
+    b_sums[0, :, quarter:] = head_sums[...]
     sums_b = [links.send(b_sums.at[0], b_sums.at[j], {"b": across(b, j)}) for j in range(1, nb)]
     for h in range(HALVES):
         r.relay_q(h, 0)
+    sum_b(attn_b, attn_grad, attn_held, attn_sum, attn_columns)
+    attn_copies = to_owners(attn_sum, attn_in, attn_columns)
+
+    def store(target, index, size, value):
+        target[:, span(index, size)] = value.astype(f32)
+
+    store(down_out, a, units, down_sum_ref[a])
+    for c in range(2):
+        store(gu_out.at[c], a, units, gu_sum[a, :, halves[c]])
+    for c in range(3):
+        store(qkv_out.at[c], a, HD, attn_sum[a, :, c * HD : (c + 1) * HD])
+    store(wout_out, a, HD, attn_sum[a, :, 3 * HD :])
+    for k, copy in down_copies:
+        copy.wait_recv()
+        store(down_out, across(a, k), units, down_in[k - 1])
     for copy in sums_b:
         copy.wait_recv()
-    held = b_sums[0]
+    total = b_sums[0]
     for j in range(1, nb):
-        held = held + b_sums[j]
-    sums_ref[...] = held
+        total = total + b_sums[j]
+    sums_ref[...] = total
+    for c in range(2):
+        for k, copy in gu_copies[c]:
+            copy.wait_recv()
+            store(gu_out.at[c], across(a, k), units, gu_in[k - 1, :, halves[c]])
+    for k, copy in attn_copies:
+        copy.wait_recv()
+        for c in range(3):
+            store(qkv_out.at[c], across(a, k), HD, attn_in[k - 1, :, c * HD : (c + 1) * HD])
+        store(wout_out, across(a, k), HD, attn_in[k - 1, :, 3 * HD :])
     for h in range(HALVES):
         r.arrived(h, 0)
     links.finish()
 
 
-def last_call(nb, part, grad_res, attn_sums, ffn_sums, head_sums):
-    na, rows, width = part.shape
+def last_call(nb, *operands):
+    na, rows, width = operands[0].shape
+    w_rows, units = operands[12].shape[1:]
     quarter = width // 4
     vmem = pl.BlockSpec(memory_space=pltpu.VMEM)
     shape = jax.ShapeDtypeStruct
-    copies = HALVES * (3 * na + 1) + 1 + na + nb
+    outs = (
+        shape((1, rows, width), bf16),
+        shape((8, quarter + HD), f32),
+        shape((w_rows, na * units), f32),
+        shape((2, w_rows, na * units), f32),
+        shape((3, w_rows, na * HD), f32),
+        shape((w_rows, na * HD), f32),
+    )
+    copies = HALVES * (3 * na + 1) + 2 + 6 * na + 4 * nb
     return pl.pallas_call(
         functools.partial(last_kernel, na, nb),
-        out_shape=(shape((1, rows, width), bf16), shape((8, quarter + HD), f32)),
-        in_specs=[vmem] * 5,
-        out_specs=(vmem, vmem),
+        out_shape=outs,
+        in_specs=[vmem] * 14,
+        out_specs=(vmem,) * len(outs),
         scratch_shapes=[
+            pltpu.VMEM((na, rows, 2 * HD), f32),
+            pltpu.VMEM((na, rows, 3 * HD), bf16),
+            pltpu.VMEM((na, rows, width), bf16),
+            pltpu.VMEM((8, HD), f32),
+            pltpu.VMEM((5, 8, rows), f32),
+            pltpu.VMEM((na - 1, 8, rows), f32),
+            pltpu.VMEM((8, rows), f32),
             pltpu.VMEM((8, width), f32),
             pltpu.VMEM((na - 1, 8, quarter), f32),
             pltpu.VMEM((nb, 8, quarter + HD), f32),
+            pltpu.VMEM((nb - 1, na, w_rows, 2 * units), bf16),
+            pltpu.VMEM((na, w_rows, 2 * units), bf16),
+            pltpu.VMEM((na, nb, w_rows, 4 * HD), bf16),
+            pltpu.VMEM((nb - 1, na, w_rows, 4 * HD), bf16),
+            pltpu.VMEM((na, w_rows, 4 * HD), bf16),
+            pltpu.VMEM((na - 1, w_rows, units), bf16),
+            pltpu.VMEM((na - 1, w_rows, 2 * units), bf16),
+            pltpu.VMEM((na - 1, w_rows, 4 * HD), bf16),
         ]
         + reduce_scratch(na, rows, width)
         + [pltpu.SemaphoreType.DMA((copies,)), pltpu.SemaphoreType.DMA((copies,))],
         compiler_params=pltpu.CompilerParams(
             collective_id=4, has_side_effects=True, vmem_limit_bytes=VMEM_LIMIT
         ),
-        cost_estimate=pl.CostEstimate(flops=10**8, bytes_accessed=10**8, transcendentals=0),
         name="last",
-    )(part, grad_res, attn_sums, ffn_sums, head_sums)
+    )(*operands)
 
 
 def reduce_scratch(na, rows, width):
@@ -853,130 +1050,6 @@
             out_ref[at : at + 1] = total
 
 
-def stats_kernel(na, stats_ref, out_ref, held, from_a, send_sem, recv_sem):
-    a, p, q = lax.axis_index("a"), lax.axis_index("p"), lax.axis_index("q")
-    greet([{"q": 1 - q}, {"p": 1 - p}] + [{"a": across(a, k)} for k in range(1, na)])
-    links = Links(send_sem, recv_sem)
-    held[0] = stats_ref[...]
-    add_over_heads(links, na, a, p, q, held, from_a, out_ref)
-    links.finish()
-
-
-def stats_call(na, stats, ident):
-    return pl.pallas_call(
-        functools.partial(stats_kernel, na),
-        out_shape=jax.ShapeDtypeStruct(stats.shape, f32),
-        in_specs=[pl.BlockSpec(memory_space=pltpu.VMEM)],
-        out_specs=pl.BlockSpec(memory_space=pltpu.VMEM),
-        scratch_shapes=[
-            pltpu.VMEM((5,) + stats.shape, f32),
-            pltpu.VMEM((na - 1,) + stats.shape, f32),
-            pltpu.SemaphoreType.DMA((na + 1,)),
-            pltpu.SemaphoreType.DMA((na + 1,)),
-        ],
-        compiler_params=pltpu.CompilerParams(collective_id=ident, has_side_effects=True),
-    )(stats)
-
-
-def local_call(kernel, na, operands, outs, scratch=(), flops=10**9):
-    def spec(shape, kind):
-        if kind == "row":
-            return pl.BlockSpec((1,) + tuple(shape[1:]), lambda k: (k,) + (0,) * (len(shape) - 1))
-        if kind == "all":
-            return pl.BlockSpec(tuple(shape), lambda k: (0,) * len(shape))
-        return pl.BlockSpec(memory_space=pl.ANY)
-
-    return pl.pallas_call(
-        kernel,
-        grid=(na,),
-        out_shape=tuple(jax.ShapeDtypeStruct(shape, dtype) for shape, dtype, _ in outs),
-        in_specs=[spec(array.shape, kind) for array, kind in operands],
-        out_specs=tuple(spec(shape, kind) for shape, _, kind in outs),
-        scratch_shapes=list(scratch),
-        compiler_params=pltpu.CompilerParams(
-            dimension_semantics=("arbitrary",), vmem_limit_bytes=VMEM_LIMIT
-        ),
-        cost_estimate=pl.CostEstimate(flops=flops, bytes_accessed=2 * 10**7, transcendentals=0),
-    )(*[array for array, _ in operands])
-
-
-def add_stats(stats_ref, first, second):
-    k = pl.program_id(0)
-
-    @pl.when(k == 0)
-    def _():
-        stats_ref[...] = jnp.zeros_like(stats_ref)
-
-    stats_ref[...] += to_row(first, 2 * k) + to_row(second, 2 * k + 1)
-
-
-def attend_back_kernel(
-    proj_ref, qkv_ref, stats_ref, gain_ref, cos_ref, sin_ref, w_ref, grad_ref, inner_ref, sums_ref
-):
-    k = pl.program_id(0)
-    queries, key_rows, values, q_inv, k_inv, q_rot, k_rot, probs = attention(
-        k, qkv_ref[0], stats_ref[...], gain_ref, cos_ref, sin_ref
-    )
-    cos_table, sine_table = cos_ref[...], sin_ref[...]
-    grad_att = dot(proj_ref[0], w_ref[:, 3 * HD :]).astype(bf16)
-    grad_v = t_dot(probs.astype(bf16), grad_att)
-    grad_p = dot_t(grad_att, values)
-    delta = jnp.sum(probs * grad_p, axis=1, keepdims=True)
-    grad_scores = (probs * (grad_p - delta) * HD ** (-0.5)).astype(bf16)
-    grad_q = dot(grad_scores, k_rot)
-    grad_k = t_dot(grad_scores, q_rot)
-    grad_q = grad_q * cos_table + rotate_back(grad_q * sine_table)
-    grad_k = grad_k * cos_table + rotate_back(grad_k * sine_table)
-
-    @pl.when(k == 0)
-    def _():
-        sums_ref[...] = jnp.zeros_like(sums_ref)
-
-    sums_ref[0:1] += jnp.sum(grad_q * queries * q_inv, axis=0, keepdims=True)
-    sums_ref[1:2] += jnp.sum(grad_k * key_rows * k_inv, axis=0, keepdims=True)
-    scaled_q = grad_q * gain_ref[0:1]
-    scaled_k = grad_k * gain_ref[1:2]
-    grad_ref[0, :, :HD] = scaled_q
-    grad_ref[0, :, HD : 2 * HD] = scaled_k
-    grad_ref[0, :, 2 * HD :] = grad_v
-    add_stats(inner_ref, scaled_q * queries, scaled_k * key_rows)
-
-
-def qkv_back_kernel(scaled_ref, qkv_ref, stats_ref, inner_ref, w_ref, grad_ref, part_ref):
-    k = pl.program_id(0)
-    for i in range(2):
-        at = slice(i * HD, (i + 1) * HD)
-        inv = lax.rsqrt(to_column(stats_ref[...] / HQ, 2 * k + i) + epsilon)
-        mean = to_column(inner_ref[...] / HQ, 2 * k + i)
-        grad = inv * scaled_ref[0, :, at] - qkv_ref[0, :, at] * inv * inv * inv * mean
-        grad_ref[0, :, at] = grad.astype(bf16)
-    grad_ref[0, :, 2 * HD :] = scaled_ref[0, :, 2 * HD :].astype(bf16)
-    part_ref[0] = dot_t(grad_ref[0], w_ref[:, : 3 * HD]).astype(bf16)
-
-
-def widen_kernel(na, count, *refs):
-    pieces, out = refs[:na], refs[na]
-    a = lax.axis_index("a")
-    columns = out.shape[2] // na
-    for k in range(na):
-        for c in range(count):
-            out[c, :, span(across(a, k), columns)] = pieces[k][
-                :, c * columns : (c + 1) * columns
-            ].astype(f32)
-
-
-def widen(pieces, count):
-    na = len(pieces)
-    rows, width = pieces[0].shape
-    return pl.pallas_call(
-        functools.partial(widen_kernel, na, count),
-        out_shape=jax.ShapeDtypeStruct((count, rows, na * width // count), f32),
-        in_specs=[pl.BlockSpec(memory_space=pltpu.VMEM)] * na,
-        out_specs=pl.BlockSpec(memory_space=pltpu.VMEM),
-        compiler_params=pltpu.CompilerParams(vmem_limit_bytes=VMEM_LIMIT),
-    )(*pieces)
-
-
 def rope_tables(length, width):
     half_width = width // 2
     inv_freq = rope_base ** (-(jnp.arange(half_width, dtype=f32) * 2.0) / width)
@@ -986,7 +1059,7 @@
     return cos_table, sine_table
 
 
-def block(
+def on_device(
     tokens,
     qkv_weight,
     out_weight,
@@ -1004,6 +1077,7 @@
     rows, width = tokens.shape
     quarter = width // 4
     w_rows = out_weight.shape[0]
+    units = down_weight.shape[1] // na
 
     def quarter_of(operand):
         return lax.dynamic_slice_in_dim(operand, share * quarter, quarter, 1)
@@ -1036,58 +1110,35 @@
         [gain[None] for gain in (attn_gain, ffn_gain, q_gain, k_gain)],
     )
     n_d, n_h = attn_gain.shape[0], q_gain.shape[0]
-    tables = [(stats, "all"), (head_gain, "all"), (cos_table, "all"), (sine_table, "all")]
-    full = (na, rows, width)
-    grad_mlp, block_rows, hidden, grad_gu, grad_proj, ffn_sums, grad_res, attn_sums = middle_call(
-        res_all, w_mlp, res_mine, grad_mine, proj_mine, inv_mine, width_gain
-    )
-
-    def weight_grad(left, right):
-        out = jnp.einsum("krd,kru->du", left, right, preferred_element_type=f32)
-        return out.astype(bf16).reshape(na, nb, w_rows, right.shape[2])
-
-    def reduce_b(grad):
-        total = pick(grad, b, 1).astype(f32)
-        for j in range(1, nb):
-            total = total + swap(pick(grad, b ^ j, 1), "b", j).astype(f32)
-        return total.astype(bf16)
-
-    def to_owner(grad):
-        parts = [pick(grad, a ^ k, 0) for k in range(na)]
-        return parts[:1] + [swap(parts[k], "a", k) for k in range(1, na)]
-
-    down_sum = reduce_b(weight_grad(grad_mlp, hidden))
-    gu_sum = reduce_b(weight_grad(res_all, grad_gu))
-    scaled, inner, head_sums = local_call(
-        attend_back_kernel,
-        na,
-        [(grad_proj, "row"), (qkv, "row")] + tables + [(w_attn, "all")],
-        [((na, rows, 3 * HD), f32, "row"), ((8, rows), f32, "all"), ((8, HD), f32, "all")],
-    )
-    out_sum = reduce_b(weight_grad(grad_proj, attended))
-    inner = stats_call(na, inner, 7)
-    inner, down_sum = lax.optimization_barrier((inner, down_sum))
-    down_sum = to_owner(down_sum)
-    grad_qkv, part = local_call(
-        qkv_back_kernel,
-        na,
-        [(scaled, "row"), (qkv, "row"), (stats, "all"), (inner, "all"), (w_attn, "all")],
-        [((na, rows, 3 * HD), bf16, "row"), (full, bf16, "row")],
-    )
-    part, gu_sum = lax.optimization_barrier((part, gu_sum))
-    gu_sum = to_owner(gu_sum)
-    qkv_sum = to_owner(reduce_b(weight_grad(x_all, grad_qkv)))
-    out_sum = to_owner(out_sum)
-    grad_rows, sums = last_call(nb, part, grad_res, attn_sums, ffn_sums, head_sums)
+    block_rows, grad_proj, ffn_sums, grad_res, attn_sums, down_sum, gu_grad = middle_call(
+        nb, res_all, w_mlp, res_mine, grad_mine, proj_mine, inv_mine, width_gain
+    )
+    grad_rows, sums, down_grad, gu_grad, qkv_grad, out_grad_w = last_call(
+        nb,
+        grad_proj,
+        x_all,
+        qkv,
+        stats,
+        head_gain,
+        cos_table,
+        sine_table,
+        w_attn,
+        attended,
+        grad_res,
+        attn_sums,
+        ffn_sums,
+        down_sum,
+        gu_grad,
+    )
     width_sums = lax.dynamic_slice_in_dim(sums[:2, :quarter], b * n_d, n_d, 1)
     head_sums = lax.dynamic_slice_in_dim(sums[:2, quarter:], b * n_h, n_h, 1)
     return (
         block_rows[0].astype(f32),
         grad_rows[0].astype(f32),
-        widen(qkv_sum, 3).transpose(1, 0, 2),
-        widen(out_sum, 1)[0],
-        widen(gu_sum, 2).transpose(1, 0, 2),
-        widen(down_sum, 1)[0],
+        qkv_grad.transpose(1, 0, 2),
+        out_grad_w,
+        gu_grad.transpose(1, 0, 2),
+        down_grad,
         width_sums[0],
         width_sums[1],
         head_sums[0],
@@ -1102,7 +1153,7 @@
     dp_axes, tp_axes = ("a", "b"), ("p", "q")
     both = tp_axes + dp_axes
     return jax.shard_map(
-        block,
+        on_device,
         mesh=fine,
         in_specs=(
             P(dp_axes, None),

time: 628 us -> 520 us (0.83); the launches traced: 618 us -> 519 us
  waiting for transfers between devices: 108 us -> 0 us
  Pallas kernels: 433 us -> 495 us
  matrix products: 20.3 us -> 0 us
  starting transfers between devices: 18.4 us -> 0 us
  local copies, waits for them, and re-layouts: 27.6 us -> 18.9 us
    ppermute x16 -> x0, waiting for transfers between devices: 108 us -> none  [swap(): return lax.ppermute(operand, axis, [(i, i ^ k) for i in range(n)])]
    pallas_call x9 -> x2, Pallas kernels: 239 us -> 302 us  [the longest x1 171 us: middle_call(): pl.pallas_call(functools.partial(middle_kernel, na, nb), out_shape=outs,...]
    dot_general x4 -> x0, matrix products: 20.3 us -> none  [weight_grad(): out = jnp.einsum('krd,kru->du', left, right, preferred_element_type=f32)]
    ppermute x16 -> x0, starting transfers between devices: 18.4 us -> none  [swap(): return lax.ppermute(operand, axis, [(i, i ^ k) for i in range(n)])]
    unnamed x47 -> x16, local copies, waits for them, and re-layouts: 14.1 us -> 11.2 us
  transfers between devices with their start and end apart: 16 -> 0, of which waited for: 7 -> 0; matrix products, arithmetic and copies ran while one was open for 4% -> 0% of each run, Pallas kernels for 6% -> 0%
where the time goes in v5:
time: 520 us; the launch traced here: 519 us
  Pallas kernels  495 us (95%)
  local copies, waits for them, and re-layouts  18.9 us (4%)
    pallas_call x1, Pallas kernels, enter_call(): pl.pallas_call(functools.partial(enter_kernel, na, nb), out_shape=tuple(o...  194 us
    pallas_call x1, Pallas kernels, middle_call(): pl.pallas_call(functools.partial(middle_kernel, na, nb), out_shape=outs,...  171 us
    pallas_call x1, Pallas kernels, last_call(): pl.pallas_call(functools.partial(last_kernel, na, nb), out_shape=outs, in...  131 us
    unnamed x16, local copies, waits for them, and re-layouts  11.2 us

profile of v5, /device:TPU:8, one launch (start us, length us, event | category | flops | bytes accessed | tf_op | source)
XLA Modules:
  0.0 519.4 jit_solution(15561853636275251338)
XLA Ops:
  0.6 0.0 copy-start
  0.7 1.8 constant_dynamic-slice_fusion.3.refs_0_
  2.5 0.5 fusion
  3.0 0.8 pad_maximum_fusion
  3.8 1.2 broadcast_in_dim.14.refs_7_
  5.1 1.2 broadcast_in_dim.15.refs_8_
  6.3 193.7 %enter.1 = (bf16[4,256,2048]{2,1,0:T(8,128)(2,1)}, bf16[2048,512]{1,0:T(8,128)(2,1)}, bf16[2048,1536]{1,0:T(8,128)(2,1)}, f32[8,512]{1,0:T(8,128)}, f32[8,128]{1...) custom-call(bf16[256,512]{1,0:T(8,128)(2,1)} %constant_dynamic-slice, ...), custom_call_target="tpu_custom_call" | custom-call | tf_op jit(solution)/shard_map/enter/pallas_call | solution.py:1007
  200.0 0.0 copy-done
  200.0 0.8 constant_dynamic-slice_fusion.2.refs_3_
  200.9 171.1 %middle.1 = (bf16[1,256,2048]{2,1,0:T(8,128)(2,1)}, bf16[4,256,2048]{2,1,0:T(8,128)(2,1)}, f32[8,512]{1,0:T(8,128)}, f32[256,512]{1,0:T(8,128)}, f32[8,512]{1,0:...) custom-call(bf16[4,256,2048]{2,1,0:T(8,128)(2,1)} %get-tuple-element.35.refs_0_, ...), custom_call_target="tpu_custom_call" | custom-call | tf_op jit(solution)/shard_map/middle/pallas_call | solution.py:549
  372.0 130.5 %last.1 = (bf16[1,256,2048]{2,1,0:T(8,128)(2,1)}, f32[8,640]{1,0:T(8,128)}, f32[256,2048]{1,0:T(8,128)}, f32[2,256,2048]{2,1,0:T(8,128)}, f32[3,256,512]{2,1,0:T(8,128)}, /*index=5*/f32[256,512]{1,0:T(8,128)}) custom-call(bf16[4,256,2048]{2,1,0:T(8,128)(2,1)} %get-tuple-element.42.refs_0_, bf16[4,256,2048]{2,1,0:T(8,128)(2,1)} %get-tuple-element.43.refs_1_, ...), custom_call_target="tpu_custom_call" | custom-call | tf_op jit(solution)/shard_map/last/pallas_call | solution.py:759
  502.5 7.5 %copy.20 = f32[256,2,2048]{2,1,0:T(2,128)} copy(f32[256,2,2048]{2,0,1:T(8,128)} %bitcast.17) | data formatting | bytes 8388608
  510.0 1.6 bitcast_convert_fusion
  511.6 0.7 slice.18
  512.3 0.6 fusion.2
  512.9 0.7 slice.21
  513.6 0.1 constant_dynamic-slice_fusion.1
  513.7 0.5 slice_bitcast_fusion
  514.2 1.6 bitcast_convert_fusion.1
  515.8 1.1 copy.24
  516.9 0.2 copy-done.5
  517.2 0.8 copy.25
  517.9 0.2 copy-done.1
  518.1 1.3 copy.26
  (9 shorter events, 0.0 us)
Async XLA Ops:
  0.6 199.4 %copy-start = (f32[256,2048]{1,0:T(8,128)S(1)}, f32[256,2048]{1,0:T(8,128)}, u32[]{:S(2)}) copy-start(f32[256,2048]{1,0:T(8,128)} %param.19) | copy-start | bytes 6291460
  502.5 7.5 %copy-start.4 = (bf16[1,256,2048]{2,1,0:T(8,128)(2,1)S(1)}, bf16[1,256,2048]{2,1,0:T(8,128)(2,1)}, u32[]{:S(2)}) copy-start(bf16[1,256,2048]{2,1,0:T(8,128)(2,1)} %get-tuple-element.54) | copy-start | bytes 3145732
  510.0 4.2 copy-start.3
  513.6 2.2 copy-start.2
  515.8 1.4 copy-start.5
  515.8 2.3 copy-start.1

commit v6 on v5

--- a/solution.py
+++ b/solution.py
@@ -306,6 +306,32 @@
     def arrived(self, h, k):
         self.spread_q[h, k].wait_recv()
 
+    def steps(self, first, second, number):
+        def normed(h):
+            self.stats_done(h, number)
+            self.each(h, second)
+
+        def spread_own(h):
+            here = self.out.at[0, self.at(h), self.mine]
+            self.spread_p[h, 0] = self.links.send(here, here, {"p": 1 - self.p})
+
+        def spread_far(h, k):
+            here = self.out.at[0, self.at(h), self.mine]
+            target = self.out.at[k, self.at(h), self.mine]
+            self.spread_a[h, k] = self.links.send(here, target, {"a": across(self.a, k)})
+
+        return {
+            "P": self.send_p,
+            "A": self.send_a,
+            "SC": lambda h: self.scattered(h, first, number),
+            "SQ": self.stats_q,
+            "SD": normed,
+            "X": spread_own,
+            "Z": spread_far,
+            "RP": self.relay_p,
+            "RQ": self.relay_q,
+        }
+
 
 def reduce_peers(na):
     a, p, q = lax.axis_index("a"), lax.axis_index("p"), lax.axis_index("q")
@@ -368,6 +394,25 @@
         r.out[0, at, r.mine] = grad.astype(bf16)
 
     return first, second
+
+
+MIDDLE = (
+    ("F", 1), ("F", 2), ("rP", 0, 1), ("F", 3), ("rP", 0, 2), ("rA", 0, 1), ("rP", 0, 3), ("rP", 1, 1),
+    ("rP", 1, 3), ("rA", 0, 2), ("F", 0), ("rA", 0, 3), ("rA", 1, 1), ("rA", 1, 3), ("rP", 0, 0),
+    ("rP", 1, 2), ("rSC", 0), ("rP", 1, 0), ("rSQ", 0), ("rA", 1, 2), ("rSD", 0), ("rZ", 0, 1),
+    ("rZ", 0, 2), ("rX", 0), ("rRP", 0, 1), ("rSC", 1), ("rRP", 0, 2), ("rRQ", 0, 1), ("rSQ", 1),
+    ("rZ", 0, 3), ("rRQ", 0, 0), ("rRQ", 0, 2), ("rSD", 1), ("rZ", 1, 2), ("B", 0, 2), ("rRP", 0, 3),
+    ("sP", 0, 2), ("B", 0, 1), ("sP", 0, 1), ("rZ", 1, 3), ("rRQ", 0, 3), ("rZ", 1, 1), ("B", 0, 0),
+    ("rRP", 1, 2), ("B", 0, 3), ("rRP", 1, 3), ("sA", 0, 2), ("rRQ", 1, 2), ("sP", 0, 3), ("B", 1, 2),
+    ("rRP", 1, 1), ("rRQ", 1, 3), ("rX", 1), ("sA", 0, 3), ("sP", 1, 2), ("B", 1, 3), ("rRQ", 1, 1),
+    ("sA", 0, 1), ("sP", 0, 0), ("rRQ", 1, 0), ("B", 1, 1), ("sA", 1, 2), ("sP", 1, 3), ("B", 1, 0),
+    ("sP", 1, 1), ("sSC", 0), ("sA", 1, 3), ("sP", 1, 0), ("sA", 1, 1), ("BP",), ("sSQ", 0), ("sSD", 0),
+    ("sZ", 0, 2), ("sX", 0), ("D",), ("sSC", 1), ("sZ", 0, 1), ("sRP", 0, 2), ("sZ", 0, 3), ("G", 3),
+    ("sSQ", 1), ("sSD", 1), ("sZ", 1, 2), ("sX", 1), ("sZ", 1, 1), ("G", 1), ("sRP", 0, 3), ("sZ", 1, 3),
+    ("G", 0), ("sRP", 0, 1), ("sRP", 1, 2), ("sRQ", 1, 0), ("BQ",), ("sRP", 1, 1), ("sRP", 1, 3),
+    ("sRQ", 0, 1), ("sRQ", 1, 2), ("sRQ", 0, 2), ("G", 2), ("sRQ", 0, 3), ("DS",), ("sRQ", 1, 1),
+    ("sRQ", 0, 0), ("sRQ", 1, 3),
+)
 
 
 def middle_kernel(na, nb, *refs):
@@ -432,101 +477,57 @@
 
         lax.fori_loop(0, width // wide_tile, back, 0)
 
-    lead = r.lead
-    for i, k in enumerate(lead):
+    first, second = mlp_math(r, res_ref, grad_ref, gain_ref, block_ref, ffn_sum_ref)
+    back_first, back_second = back_math(
+        s, grad_ref, proj_ref, inv_ref, gain_ref, grad_res_ref, attn_sum_ref
+    )
+    copies, reused = {}, []
+    columns = slice(0, units)
+
+    def forward_step(k):
         forward(k)
         for h in range(HALVES):
             r.send_q(h, k)
-        if i:
-            r.send_p(0, lead[i - 1])
-    r.send_p(0, lead[-1])
-    r.send_p(1, lead[0])
-    r.send_a(0, lead[0])
-    r.send_p(1, lead[1])
-    for k in lead[1:]:
-        r.send_a(0, k)
-    first, second = mlp_math(r, res_ref, grad_ref, gain_ref, block_ref, ffn_sum_ref)
-    r.scattered(0, first, 2)
-    for k in lead[2:]:
-        r.send_p(1, k)
-    for k in lead[:-2]:
-        r.send_a(1, k)
-    r.stats_q(0)
-    r.stats_done(0, 2)
-    r.each(0, second)
-    r.spread(0, lead)
-    r.send_a(1, lead[-2])
-    r.scattered(1, first, 2)
-    r.relay_q(0, 0)
-    r.stats_q(1)
-    r.arrived(0, 0)
-    r.stats_done(1, 2)
-    r.each(1, second)
-    r.spread(1, lead)
-    here = block_ref.at[0, :, r.mine]
-    block_p = links.send(here, here, {"p": 1 - r.p})
-    links.sent(r.step_q.values())
-    backward(0, 0)
-    s.send_q(0, 0)
-    r.relay_q(1, 0)
-    s.send_p(0, 0)
-    block_p.wait_recv()
-    here = block_ref.at[0, :, r.pair]
-    block_q = links.send(here, here, {"q": 1 - r.q})
-    r.arrived(1, 0)
-    backward(1, 0)
-    s.send_q(1, 0)
-    order = [(h, k) for h in range(HALVES) for k in lead[:-1]]
-    s.send_p(1, 0)
-    steps = len(order)
-    back_first, back_second = back_math(
-        s, grad_ref, proj_ref, inv_ref, gain_ref, grad_res_ref, attn_sum_ref
-    )
-    for i in range(steps + 3):
-        if 0 <= i - 3 < steps:
-            s.send_a(*order[i - 3])
-        if i == steps + 1:
-            s.scattered(0, back_first, 1)
-        if 0 <= i - 2 < steps:
-            s.send_p(*order[i - 2])
-        if 0 <= i - 1 < steps:
-            r.relay_q(*order[i - 1])
-            r.arrived(*order[i - 1])
-            backward(*order[i - 1])
-            s.send_q(*order[i - 1])
-        if i < steps:
-            r.relay_p(*order[i])
-    s.stats_q(0)
-    for block in range(na):
-        weight_grad(out, hidden_ref, down_grad, block)
-    columns = slice(0, units)
-    down_copies = exchange_b(links, down_grad, down_held, columns)
-    s.stats_done(0, 1)
-    s.each(0, back_second)
-    s.spread(0, lead)
-    s.scattered(1, back_first, 1)
-    weight_grad(x_ref, grad_gu_ref, gu_grad_ref, 0)
-    s.relay_q(0, 0)
-    s.stats_q(1)
-    weight_grad(x_ref, grad_gu_ref, gu_grad_ref, 1)
-    s.stats_done(1, 1)
-    s.each(1, back_second)
-    s.spread(1, lead)
-    weight_grad(x_ref, grad_gu_ref, gu_grad_ref, 2)
-    late = [(0, 0)] + order
-    for i, (h, k) in enumerate(order):
-        s.relay_p(h, k)
-        if i == 1:
-            weight_grad(x_ref, grad_gu_ref, gu_grad_ref, 3)
-        if i:
-            s.relay_q(*late[i])
-    s.relay_q(1, 0)
-    s.relay_q(*order[-1])
-    sum_b(down_copies, down_grad, down_held, down_sum_ref, columns)
+
+    def backward_step(h, k):
+        if not reused:
+            links.sent(r.step_q.values())
+            reused.append(True)
+        r.arrived(h, k)
+        backward(h, k)
+        s.send_q(h, k)
+
+    def block_p():
+        here = block_ref.at[0, :, r.mine]
+        copies["p"] = links.send(here, here, {"p": 1 - r.p})
+
+    def block_q():
+        copies["p"].wait_recv()
+        here = block_ref.at[0, :, r.pair]
+        copies["q"] = links.send(here, here, {"q": 1 - r.q})
+
+    def down_grads():
+        for block in range(na):
+            weight_grad(out, hidden_ref, down_grad, block)
+        copies["b"] = exchange_b(links, down_grad, down_held, columns)
+
+    table = {
+        "F": forward_step,
+        "B": backward_step,
+        "BP": block_p,
+        "BQ": block_q,
+        "D": down_grads,
+        "DS": lambda: sum_b(copies["b"], down_grad, down_held, down_sum_ref, columns),
+        "G": lambda block: weight_grad(x_ref, grad_gu_ref, gu_grad_ref, block),
+    }
+    table.update({"r" + key: step for key, step in r.steps(first, second, 2).items()})
+    table.update({"s" + key: step for key, step in s.steps(back_first, back_second, 1).items()})
+    for key, *where in MIDDLE:
+        table[key](*where)
     for h in range(HALVES):
         for k in range(na):
             s.arrived(h, k)
-    block_q.wait_recv()
+    copies["q"].wait_recv()
     links.finish()
 
 

time: 520 us -> 481 us (0.925)
  Pallas kernels: 495 us -> 457 us
    pallas_call x1, Pallas kernels: 171 us -> 131 us  [middle_call(): pl.pallas_call(functools.partial(middle_kernel, na, nb), out_shape=outs,...]
where the time goes in v6:
time: 481 us
  Pallas kernels  457 us (95%)
  local copies, waits for them, and re-layouts  18.9 us (4%)
    pallas_call x1, Pallas kernels, enter_call(): pl.pallas_call(functools.partial(enter_kernel, na, nb), out_shape=tuple(o...  194 us
    pallas_call x1, Pallas kernels, last_call(): pl.pallas_call(functools.partial(last_kernel, na, nb), out_shape=outs, in...  132 us
    pallas_call x1, Pallas kernels, middle_call(): pl.pallas_call(functools.partial(middle_kernel, na, nb), out_shape=outs,...  131 us
    unnamed x16, local copies, waits for them, and re-layouts  11.2 us

profile of v6, /device:TPU:8, one launch (start us, length us, event | category | flops | bytes accessed | tf_op | source)
XLA Modules:
  0.0 481.1 jit_solution(1911513122578793002)
XLA Ops:
  0.6 0.0 copy-start
  0.7 1.8 constant_dynamic-slice_fusion.3.refs_0_
  2.5 0.5 fusion
  3.0 0.8 pad_maximum_fusion
  3.8 1.2 broadcast_in_dim.14.refs_7_
  5.1 1.2 broadcast_in_dim.15.refs_8_
  6.3 193.7 %enter.1 = (bf16[4,256,2048]{2,1,0:T(8,128)(2,1)}, bf16[2048,512]{1,0:T(8,128)(2,1)}, bf16[2048,1536]{1,0:T(8,128)(2,1)}, f32[8,512]{1,0:T(8,128)}, f32[8,128]{1...) custom-call(bf16[256,512]{1,0:T(8,128)(2,1)} %constant_dynamic-slice, ...), custom_call_target="tpu_custom_call" | custom-call | tf_op jit(solution)/shard_map/enter/pallas_call | solution.py:1008
  200.0 0.8 constant_dynamic-slice_fusion.2.refs_3_
  200.9 131.3 %middle.1 = (bf16[1,256,2048]{2,1,0:T(8,128)(2,1)}, bf16[4,256,2048]{2,1,0:T(8,128)(2,1)}, f32[8,512]{1,0:T(8,128)}, f32[256,512]{1,0:T(8,128)}, f32[8,512]{1,0:...) custom-call(bf16[4,256,2048]{2,1,0:T(8,128)(2,1)} %get-tuple-element.35.refs_0_, ...), custom_call_target="tpu_custom_call" | custom-call | tf_op jit(solution)/shard_map/middle/pallas_call | solution.py:550
  332.2 131.9 %last.1 = (bf16[1,256,2048]{2,1,0:T(8,128)(2,1)}, f32[8,640]{1,0:T(8,128)}, f32[256,2048]{1,0:T(8,128)}, f32[2,256,2048]{2,1,0:T(8,128)}, f32[3,256,512]{2,1,0:T(8,128)}, /*index=5*/f32[256,512]{1,0:T(8,128)}) custom-call(bf16[4,256,2048]{2,1,0:T(8,128)(2,1)} %get-tuple-element.42.refs_0_, bf16[4,256,2048]{2,1,0:T(8,128)(2,1)} %get-tuple-element.43.refs_1_, ...), custom_call_target="tpu_custom_call" | custom-call | tf_op jit(solution)/shard_map/last/pallas_call | solution.py:760
  464.2 0.0 copy-start.4
  464.2 7.5 %copy.20 = f32[256,2,2048]{2,1,0:T(2,128)} copy(f32[256,2,2048]{2,0,1:T(8,128)} %bitcast.17) | data formatting | bytes 8388608
  471.7 1.6 bitcast_convert_fusion
  473.3 0.7 slice.18
  474.0 0.6 fusion.2
  474.6 0.7 slice.21
  475.3 0.1 constant_dynamic-slice_fusion.1
  475.4 0.5 slice_bitcast_fusion
  475.9 1.6 bitcast_convert_fusion.1
  477.5 1.1 copy.24
  478.6 0.2 copy-done.5
  478.8 0.8 copy.25
  479.6 0.2 copy-done.1
  479.8 1.3 copy.26
  (9 shorter events, 0.0 us)
Async XLA Ops:
  0.6 199.4 %copy-start = (f32[256,2048]{1,0:T(8,128)S(1)}, f32[256,2048]{1,0:T(8,128)}, u32[]{:S(2)}) copy-start(f32[256,2048]{1,0:T(8,128)} %param.19) | copy-start | bytes 6291460
  464.2 7.5 %copy-start.4 = (bf16[1,256,2048]{2,1,0:T(8,128)(2,1)S(1)}, bf16[1,256,2048]{2,1,0:T(8,128)(2,1)}, u32[]{:S(2)}) copy-start(bf16[1,256,2048]{2,1,0:T(8,128)(2,1)} %get-tuple-element.54) | copy-start | bytes 3145732
  471.7 4.2 copy-start.3
  475.3 2.2 copy-start.2
  477.4 1.4 copy-start.5
  477.5 2.3 copy-start.1
